TPU v7x, 32 devices: a whole 2x2x4 slice. The times are simulated.
32 devices in a mesh: rep: 8 (over y, x, core), ep: 4 (over z).
Axes of the slice: x: 2, y: 2, z: 4, core: 2. Of those that a mesh axis runs over, the one named last changes fastest.
Arguments:
- tokens: bfloat16 [2, 512, 4096], P(None, 'ep', 'rep'), may hold values from -6 to 6
- expert_ids: int32 [2, 512, 2], P(None, 'ep'), may hold values from 0 to 3, all different within a row; in each aligned block of 128 rows (0 to 127, 128 to 255, ..., all dimensions but the last counted through in order) at most 96 rows name the same one
- router_weight: bfloat16 [4096, 4], P('rep'), may hold values from -0.09375 to 0.09375
- w_gate: bfloat16 [4, 4096, 8192], P('ep', None, 'rep'), may hold values from -0.09375 to 0.09375
- w_up: bfloat16 [4, 4096, 8192], P('ep', None, 'rep'), may hold values from -0.09375 to 0.09375
- w_down: bfloat16 [4, 8192, 4096], P('ep', 'rep'), may hold values from -0.0625 to 0.0625
- cotangent: bfloat16 [2, 512, 4096], P(None, 'ep', 'rep'), may hold values from -6 to 6
Outputs:
- mixed: bfloat16 [2, 512, 4096], P(None, 'ep', 'rep')
- token_grad: bfloat16 [2, 512, 4096], P(None, 'ep', 'rep')
- gate_grad: bfloat16 [4, 4096, 8192], P('ep', None, 'rep')
- up_grad: bfloat16 [4, 4096, 8192], P('ep', None, 'rep')
- down_grad: bfloat16 [4, 8192, 4096], P('ep', 'rep')
- router_grad: float32 [4096, 4], P('rep')
Inputs may be any that keep to these rules, and one draw needn't show every extreme that they name: `expert_ids`: each row names 2 different experts. Among the 128 rows of one index of ep in one microbatch no expert is named by more than 96 rows, and in every draw some expert is named by exactly 96 of them.
All inputs are finite; a program needn't handle non-finite values.
Results may differ from a plain program's by a relative error of at most 0.025.
Values may be sent and summed in bfloat16 or wider, within the bound.
No kernel may reach another device: no remote copies, remote signals or barrier semaphores. Data moves between devices by JAX's collectives and lax.ppermute only.
A program may use at most 192 MiB of HBM per device.

v0:
```python
import jax
import jax.numpy as jnp
from jax import lax
from jax.sharding import PartitionSpec as P

TOP = 2


def contract_first(left, right):
    return lax.dot_general(
        left, right, (((0,), (0,)), ((), ())), preferred_element_type=jnp.float32
    )


def contract_last(left, right):
    return lax.dot_general(
        left, right, (((1,), (1,)), ((), ())), preferred_element_type=jnp.float32
    )


def route(route_ids, experts, capacity, slot_count):
    hits = route_ids[:, :, None] == jnp.arange(experts, dtype=jnp.int32)[None, None, :]
    per_token = jnp.sum(hits.astype(jnp.int32), axis=1)
    before = jnp.cumsum(per_token, axis=0) - per_token
    places = jnp.sum(jnp.where(hits, before[:, None, :], 0), axis=2)
    slots = route_ids * capacity + places
    match = jnp.arange(slot_count, dtype=jnp.int32)[:, None, None] == slots[None, :, :]
    token_count = route_ids.shape[0]
    source_row = jnp.sum(
        jnp.where(match, jnp.arange(token_count, dtype=jnp.int32)[None, :, None], 0), axis=(1, 2)
    )
    filled = jnp.any(match, axis=(1, 2))
    return (hits, slots, match, source_row, filled)


def pack(rows, source_row, filled, scale):
    picked = jnp.take(rows, source_row, axis=0)
    if scale is None:
        return jnp.where(filled[:, None], picked, jnp.zeros_like(picked))
    return (picked.astype(jnp.float32) * scale[:, None]).astype(jnp.bfloat16)


def deliver(rows, source_row, filled, scale):
    moved = lax.all_to_all(
        pack(rows, source_row, filled, scale), "ep", split_axis=0, concat_axis=0, tiled=True
    )
    result = lax.all_gather(moved, "rep", axis=1, tiled=True)
    return result


def collect(columns):
    return lax.all_to_all(columns, "ep", split_axis=1, concat_axis=1, tiled=True)


def shards(tokens, expert_ids, router_weight, w_gate, w_up, w_down, cotangent):
    micro_count = tokens.shape[0]
    tok_rows = tokens.shape[1]
    experts = router_weight.shape[1]
    capacity = min(tok_rows, 3 * tok_rows * TOP // (2 * experts))
    slot_count = lax.axis_size("ep") * capacity
    gate_w = w_gate[0]
    up_w = w_up[0]
    down_w = w_down[0]
    gate_acc = jnp.zeros(gate_w.shape, jnp.float32)
    up_acc = jnp.zeros(up_w.shape, jnp.float32)
    down_acc = jnp.zeros(down_w.shape, jnp.float32)
    router_acc = jnp.zeros(router_weight.shape, jnp.float32)
    router_wide = router_weight.astype(jnp.float32)
    mixed = []
    token_grad = []
    for step in range(micro_count):
        route_ids = expert_ids[step]
        hits, slots, match, source_row, filled = route(route_ids, experts, capacity, slot_count)
        logits = lax.psum(
            jnp.dot(tokens[step], router_weight, preferred_element_type=jnp.float32), "rep"
        )
        chosen = jnp.sum(jnp.where(hits, logits[:, None, :], 0.0), axis=2)
        spread = chosen[:, 0] - chosen[:, 1]
        first = jax.nn.sigmoid(spread)
        second = jax.nn.sigmoid(-spread)
        gates = jnp.stack([first, second], axis=1)
        slot_gate = jnp.sum(jnp.where(match, gates[None, :, :], 0.0), axis=(1, 2))
        expert_rows = deliver(tokens[step], source_row, filled, None)
        pre_gate = jnp.dot(expert_rows, gate_w, preferred_element_type=jnp.float32)
        pre_up = jnp.dot(expert_rows, up_w, preferred_element_type=jnp.float32)
        gate_sig = jax.nn.sigmoid(pre_gate)
        gate_act = pre_gate * gate_sig
        hidden = (gate_act * pre_up).astype(jnp.bfloat16)
        outputs = lax.psum_scatter(
            lax.dot_general(
                down_w, hidden, (((0,), (1,)), ((), ())), preferred_element_type=jnp.float32
            ).astype(jnp.bfloat16),
            "rep",
            scatter_dimension=0,
            tiled=True,
        )
        returned = collect(outputs)
        first_out = jnp.take(returned, slots[:, 0], axis=1).astype(jnp.float32)
        second_out = jnp.take(returned, slots[:, 1], axis=1).astype(jnp.float32)
        mixed.append(
            (first[None, :] * first_out + second[None, :] * second_out).T.astype(jnp.bfloat16)
        )
        cot_cols = cotangent[step].T.astype(jnp.float32)
        partial_dots = jnp.stack(
            [jnp.sum(cot_cols * first_out, axis=0), jnp.sum(cot_cols * second_out, axis=0)]
        )
        gate_dots = lax.psum(partial_dots, "rep")
        delta = (gate_dots[0] - gate_dots[1]) * first * second
        logit_grad = delta[:, None] * (
            hits[:, 0].astype(jnp.float32) - hits[:, 1].astype(jnp.float32)
        )
        router_acc = router_acc + jnp.dot(
            tokens[step].astype(jnp.float32).T, logit_grad, precision=lax.Precision.HIGHEST
        )
        router_in = jnp.dot(logit_grad, router_wide.T, precision=lax.Precision.HIGHEST)
        expert_cots = deliver(cotangent[step], source_row, filled, slot_gate)
        hidden_grad = contract_last(expert_cots, down_w)
        gate_pre_grad = (
            hidden_grad * pre_up * (gate_sig * (1.0 + pre_gate * (1.0 - gate_sig)))
        ).astype(jnp.bfloat16)
        up_pre_grad = (hidden_grad * gate_act).astype(jnp.bfloat16)
        down_acc = down_acc + contract_first(hidden, expert_cots)
        gate_acc = gate_acc + contract_first(expert_rows, gate_pre_grad)
        up_acc = up_acc + contract_first(expert_rows, up_pre_grad)
        input_cols = lax.psum_scatter(
            (contract_last(gate_w, gate_pre_grad) + contract_last(up_w, up_pre_grad)).astype(
                jnp.bfloat16
            ),
            "rep",
            scatter_dimension=0,
            tiled=True,
        )
        returned_grad = collect(input_cols)
        grad_cols = jnp.take(returned_grad, slots[:, 0], axis=1).astype(jnp.float32)
        grad_cols = grad_cols + jnp.take(returned_grad, slots[:, 1], axis=1).astype(jnp.float32)
        token_grad.append((grad_cols + router_in.T).T.astype(jnp.bfloat16))
    router_total = lax.psum(router_acc, "ep")
    return (
        jnp.stack(mixed),
        jnp.stack(token_grad),
        gate_acc.astype(jnp.bfloat16)[None],
        up_acc.astype(jnp.bfloat16)[None],
        down_acc.astype(jnp.bfloat16)[None],
        router_total,
    )


def solution(mesh):
    in_specs = (
        P(None, "ep", "rep"),
        P(None, "ep", None),
        P("rep", None),
        P("ep", None, "rep"),
        P("ep", None, "rep"),
        P("ep", "rep", None),
        P(None, "ep", "rep"),
    )
    out_specs = (
        P(None, "ep", "rep"),
        P(None, "ep", "rep"),
        P("ep", None, "rep"),
        P("ep", None, "rep"),
        P("ep", "rep", None),
        P("rep", None),
    )
    return jax.shard_map(shards, mesh=mesh, in_specs=in_specs, out_specs=out_specs, check_vma=False)
```

profile of v0, /device:TPU:0, one launch (start us, length us, event | category | flops | bytes accessed | tf_op | source)
XLA Modules:
  0.0 448.8 jit_solution(6220161404998173433)
XLA Ops:
  9.8 1.0 slice_bitcast_fusion.2
  10.8 2.1 gather_fusion.3
  13.0 17.9 %all_to_all.96 = bf16[4,96,512]{2,1,0:T(8,128)(2,1)} all-to-all(bf16[4,96,512]{2,1,0:T(8,128)(2,1)S(1)} %bitcast.265), channel_id=1, replica_groups=mesh['rep'=8,'ep'=4] {'ep'}, dimensions={0} | all-to-all | bytes 786432 | tf_op jit(solution)/shard_map/all_to_all | solution.py:44
  31.2 2.1 gather_fusion
  33.7 14.0 %all_to_all.97 = bf16[4,96,512]{2,1,0:T(8,128)(2,1)} all-to-all(bf16[4,96,512]{2,1,0:T(8,128)(2,1)S(1)} %bitcast.266), channel_id=1, replica_groups=mesh['rep'=8,'ep'=4] {'ep'}, dimensions={0} | all-to-all | bytes 786432 | tf_op jit(solution)/shard_map/all_to_all | solution.py:44
  47.7 15.3 %all-gather.7.cloned.1.call-done = bf16[384,4096]{1,0:T(8,128)(2,1)} async-done(((bf16[384,512]{1,0:T(8,128)(2,1)}), bf16[384,4096]{1,0:T(8,128)(2,1)}) %all-gather.7.cloned.1.call-update) | async-done | bytes 3145744 | tf_op jit(solution)/shard_map/all_gather | solution.py:47
  63.0 7.7 %fusion.23 = f32[384,1024]{1,0:T(8,128)S(1)} fusion(bf16[384,4096]{1,0:T(8,128)(2,1)} %all-gather.7.cloned.1.call-done, bf16[1,4096,1024]{2,1,0:T(8,128)(2,1)} %param.14), kind=kOutput, calls=%fused_computation.38 | convolution fusion | flops 3221225472 | bytes 13107200 | tf_op jit(solution)/shard_map/dot_general | solution.py:84
  70.8 8.9 %multiply_convert_fusion.4 = (bf16[384,1024]{1,0:T(8,128)(2,1)S(1)}, f32[384,1024]{1,0:T(8,128)}) fusion(f32[384,1024]{1,0:T(8,128)S(1)} %fusion.23, bf16[384,4096]{1,0:T(8,128)(2,1)S(1)} %copy-done.1, bf16[1,4096,1024]{2,1,0:T(8,128)(2,1)} %param.15), kind=kOutput, calls=%fused_computation.54 | convolution fusion | flops 3223584768 | bytes 15466496 | tf_op jit(solution)/shard_map/dot_general | solution.py:85
  79.7 0.9 copy-done.4
  80.6 8.1 %fusion.37 = bf16[4096,384]{0,1:T(8,128)(2,1)} fusion(bf16[384,1024]{1,0:T(8,128)(2,1)S(1)} %get-tuple-element.50, bf16[1,1024,4096]{2,1,0:T(8,128)(2,1)} %param.16), kind=kOutput, calls=%fused_computation.46 | convolution fusion | flops 3222798336 | bytes 12320768 | tf_op jit(solution)/shard_map/dot_general | solution.py:90
  89.3 8.3 %all-gather.5.cloned.1.call-done = bf16[384,4096]{1,0:T(8,128)(2,1)} async-done(((bf16[384,512]{1,0:T(8,128)(2,1)}), bf16[384,4096]{1,0:T(8,128)(2,1)}) %all-gather.5.cloned.1.call-update) | async-done | bytes 3145744 | tf_op jit(solution)/shard_map/all_gather | solution.py:47
  97.6 7.8 %fusion.25 = f32[384,1024]{1,0:T(8,128)S(1)} fusion(bf16[384,4096]{1,0:T(8,128)(2,1)} %all-gather.5.cloned.1.call-done, bf16[1,4096,1024]{2,1,0:T(8,128)(2,1)} %param.14), kind=kOutput, calls=%fused_computation.40 | convolution fusion | flops 3221225472 | bytes 13107200 | tf_op jit(solution)/shard_map/dot_general | solution.py:84
  105.4 9.1 %multiply_convert_fusion.5 = (bf16[384,1024]{1,0:T(8,128)(2,1)S(1)}, f32[384,1024]{1,0:T(8,128)}) fusion(f32[384,1024]{1,0:T(8,128)S(1)} %fusion.25, bf16[384,4096]{1,0:T(8,128)(2,1)S(1)} %copy-done.2, bf16[1,4096,1024]{2,1,0:T(8,128)(2,1)} %param.15), kind=kOutput, calls=%fused_computation.57 | convolution fusion | flops 3223584768 | bytes 15466496 | tf_op jit(solution)/shard_map/dot_general | solution.py:85
  114.5 0.9 copy-done.7
  115.4 8.1 %fusion.40 = bf16[4096,384]{0,1:T(8,128)(2,1)} fusion(bf16[384,1024]{1,0:T(8,128)(2,1)S(1)} %get-tuple-element.48, bf16[1,1024,4096]{2,1,0:T(8,128)(2,1)} %param.16), kind=kOutput, calls=%fused_computation.47 | convolution fusion | flops 3222798336 | bytes 12320768 | tf_op jit(solution)/shard_map/dot_general | solution.py:90
  124.8 22.8 %reduce-scatter.7.cloned.1.call-done = bf16[512,384]{0,1:T(8,128)(2,1)} async-done(((bf16[4096,384]{0,1:T(8,128)(2,1)}), bf16[512,384]{0,1:T(8,128)(2,1)}) %reduce-scatter.7.cloned.1.call-update) | async-done | bytes 393232 | tf_op jit(solution)/shard_map/reduce_scatter | solution.py:89
  147.6 4.6 %all-to-all-start.3 = ((bf16[512,4,96]{0,2,1:T(8,128)(2,1)}), bf16[512,4,96]{0,2,1:T(8,128)(2,1)}, u32[]{:S(2)}, u32[]{:S(2)}) async-start(bf16[512,4,96]{0,2,1:T(8,128)(2,1)} %bitcast.271), calls=%async_computation.5 | async-start | bytes 786432 | tf_op jit(solution)/shard_map/all_to_all | solution.py:52
  153.4 1.0 slice_bitcast_fusion.1
  154.4 43.2 %reduce-scatter.5.cloned.1.call-done = bf16[512,384]{0,1:T(8,128)(2,1)} async-done(((bf16[4096,384]{0,1:T(8,128)(2,1)}), bf16[512,384]{0,1:T(8,128)(2,1)}) %reduce-scatter.5.cloned.1.call-update) | async-done | bytes 393232 | tf_op jit(solution)/shard_map/reduce_scatter | solution.py:89
  197.5 4.6 %all-to-all-start.1 = ((bf16[512,4,96]{0,2,1:T(8,128)(2,1)}), bf16[512,4,96]{0,2,1:T(8,128)(2,1)}, u32[]{:S(2)}, u32[]{:S(2)}) async-start(bf16[512,4,96]{0,2,1:T(8,128)(2,1)} %bitcast.270), calls=%async_computation.2 | async-start | bytes 786432 | tf_op jit(solution)/shard_map/all_to_all | solution.py:52
  202.7 2.6 gather_fusion.9
  205.9 1.6 fusion.94
  207.5 1.6 fusion.93
  209.2 1.9 gather_fusion.4
  211.1 2.0 gather_fusion.5
  213.8 2.7 gather_fusion.1
  216.5 2.7 gather_fusion.2
  219.2 1.5 fusion.62
  221.8 12.9 %all-reduce = (f32[128,4]{0,1:T(4,128)}, f32[128,4]{0,1:T(4,128)}, f32[2,128]{1,0:T(2,128)}, f32[2,128]{1,0:T(2,128)}) all-reduce(f32[128,4]{0,1:T(4,128)} %fusion.94, f32[128,4]{0,1:T(4,128)} %fusion.93, f32[2,128]{1,0:T(2,128)} %pad_maximum_fusion.5, f32[2,128]{1,0:T(2,128)} %pad_maximum_fusion.3), channel_id=1, replica_groups=mesh['rep'=8,'ep'=4] {'rep'}, use_global_device_ids=true, to_apply=%region_8.11 | all-reduce | flops 1536 | bytes 12288 | tf_op jit(solution)/shard_map/psum | solution.py:74
  235.4 1.4 fusion.90
  237.4 0.8 select_reduce_fusion
  238.2 1.2 multiply_convert_fusion.6
  239.4 15.9 %all_to_all.98 = bf16[4,96,512]{2,1,0:T(8,128)(2,1)} all-to-all(bf16[4,96,512]{2,1,0:T(8,128)(2,1)S(1)} %bitcast.267), channel_id=1, replica_groups=mesh['rep'=8,'ep'=4] {'ep'}, dimensions={0} | all-to-all | bytes 786432 | tf_op jit(solution)/shard_map/all_to_all | solution.py:44
  255.3 2.6 gather_fusion.6
  258.6 1.3 fusion.92
  260.4 0.8 select_reduce_fusion.1
  261.2 1.2 multiply_convert_fusion.7
  262.4 13.9 %all_to_all.99 = bf16[4,96,512]{2,1,0:T(8,128)(2,1)} all-to-all(bf16[4,96,512]{2,1,0:T(8,128)(2,1)S(1)} %bitcast.268), channel_id=1, replica_groups=mesh['rep'=8,'ep'=4] {'ep'}, dimensions={0} | all-to-all | bytes 786432 | tf_op jit(solution)/shard_map/all_to_all | solution.py:44
  276.6 9.7 %all-gather.11.cloned.1.call-done = bf16[384,4096]{1,0:T(8,128)(2,1)} async-done(((bf16[384,512]{1,0:T(8,128)(2,1)}), bf16[384,4096]{1,0:T(8,128)(2,1)}) %all-gather.11.cloned.1.call-update) | async-done | bytes 3145744 | tf_op jit(solution)/shard_map/all_gather | solution.py:47
  286.3 9.1 %multiply_convert_fusion.1 = (bf16[384,1024]{1,0:T(8,128)(2,1)S(1)}, bf16[384,1024]{1,0:T(8,128)(2,1)S(1)}) fusion(f32[384,1024]{1,0:T(8,128)} %copy-done.36, f32[384,1024]{1,0:T(8,128)} %get-tuple-element.51, bf16[384,4096]{1,0:T(8,128)(2,1)} %all-gather.11.cloned.1.call-done, bf16[1,1024,4096]{2,1,0:T(8,128)(2,1)} %param.16), kind=kOutput, calls=%fused_computation.51 | convolution fusion | flops 3226337280 | bytes 16252928 | tf_op jit(solution)/shard_map/dot_general | solution.py:16
  295.5 11.5 %fusion.11 = f32[384,4096]{1,0:T(8,128)} fusion(bf16[384,1024]{1,0:T(8,128)(2,1)S(1)} %get-tuple-element.33, bf16[1,4096,1024]{2,1,0:T(8,128)(2,1)} %param.15), kind=kOutput, calls=%fused_computation.26 | convolution fusion | flops 3221225472 | bytes 15466496 | tf_op jit(solution)/shard_map/dot_general | solution.py:16
  307.0 7.2 %fusion.46 = bf16[4096,384]{0,1:T(8,128)(2,1)} fusion(f32[384,4096]{1,0:T(8,128)} %fusion.11, bf16[384,1024]{1,0:T(8,128)(2,1)S(1)} %get-tuple-element.32, bf16[1,4096,1024]{2,1,0:T(8,128)(2,1)S(1)} %bitcast.282), kind=kOutput, calls=%fused_computation.49 | convolution fusion | flops 3224371200 | bytes 18612224 | tf_op jit(solution)/shard_map/dot_general | solution.py:16
  314.4 1.1 fusion.71
  315.4 1.1 fusion.57
  316.5 12.6 %psum.39 = f32[512,4]{0,1:T(4,128)} all-reduce(f32[512,4]{0,1:T(4,128)S(1)} %fusion.57), channel_id=1, replica_groups=mesh['rep'=8,'ep'=4] {'ep'}, use_global_device_ids=true, to_apply=%region_26.29 | all-reduce | flops 2048 | bytes 16384 | tf_op jit(solution)/shard_map/psum | solution.py:137
  329.1 0.8 fusion.68
  330.0 1.1 fusion.69
  331.1 0.7 pad_maximum_fusion
  331.8 10.0 %multiply_convert_fusion.3 = (bf16[384,1024]{1,0:T(8,128)(2,1)S(1)}, bf16[384,1024]{1,0:T(8,128)(2,1)S(1)}) fusion(f32[384,1024]{1,0:T(8,128)} %copy-done.35, f32[384,1024]{1,0:T(8,128)} %get-tuple-element.49, bf16[384,4096]{1,0:T(8,128)(2,1)} %all-gather.9.cloned.1.call-done, bf16[1,1024,4096]{2,1,0:T(8,128)(2,1)} %param.16), kind=kOutput, calls=%fused_computation.53 | convolution fusion | flops 3226337280 | bytes 16252928 | tf_op jit(solution)/shard_map/dot_general | solution.py:16
  341.9 11.5 %fusion.13 = f32[384,4096]{1,0:T(8,128)} fusion(bf16[384,1024]{1,0:T(8,128)(2,1)S(1)} %get-tuple-element.31, bf16[1,4096,1024]{2,1,0:T(8,128)(2,1)} %param.15), kind=kOutput, calls=%fused_computation.28 | convolution fusion | flops 3221225472 | bytes 15466496 | tf_op jit(solution)/shard_map/dot_general | solution.py:16
  353.4 6.9 %fusion.43 = bf16[4096,384]{0,1:T(8,128)(2,1)} fusion(f32[384,4096]{1,0:T(8,128)} %fusion.13, bf16[384,1024]{1,0:T(8,128)(2,1)S(1)} %get-tuple-element.30, bf16[1,4096,1024]{2,1,0:T(8,128)(2,1)S(1)} %bitcast.284), kind=kOutput, calls=%fused_computation.48 | convolution fusion | flops 3224371200 | bytes 18612224 | tf_op jit(solution)/shard_map/dot_general | solution.py:16
  360.3 12.5 %fusion.95 = f32[4096,1024]{1,0:T(8,128)} fusion(bf16[384,4096]{1,0:T(8,128)(2,1)} %all-gather.5.cloned.1.call-done, bf16[384,1024]{1,0:T(8,128)(2,1)} %copy-done.10), kind=kOutput, calls=%fused_computation.183 | convolution fusion | flops 3221225472 | bytes 20709376 | tf_op jit(solution)/shard_map/dot_general | solution.py:10
  372.9 8.7 %fusion.96 = f32[4096,1024]{1,0:T(8,128)} fusion(bf16[384,4096]{1,0:T(8,128)(2,1)S(1)} %copy-done.3, bf16[384,1024]{1,0:T(8,128)(2,1)S(1)} %copy-done.9), kind=kOutput, calls=%fused_computation.184 | convolution fusion | flops 3221225472 | bytes 20709376 | tf_op jit(solution)/shard_map/dot_general | solution.py:10
  381.5 11.2 %fusion = bf16[1,4096,1024]{2,1,0:T(8,128)(2,1)} fusion(f32[4096,1024]{1,0:T(8,128)} %fusion.95, bf16[384,4096]{1,0:T(8,128)(2,1)S(1)} %copy-done.1, bf16[384,1024]{1,0:T(8,128)(2,1)S(1)} %copy-done.14), kind=kOutput, calls=%fused_computation.15 | convolution fusion | flops 3229614080 | bytes 29097984 | tf_op jit(solution)/shard_map/dot_general | solution.py:10
  392.8 10.8 %fusion.1 = bf16[1,4096,1024]{2,1,0:T(8,128)(2,1)} fusion(f32[4096,1024]{1,0:T(8,128)} %fusion.96, bf16[384,4096]{1,0:T(8,128)(2,1)S(1)} %copy-done.1, bf16[384,1024]{1,0:T(8,128)(2,1)S(1)} %copy-done.12), kind=kOutput, calls=%fused_computation.16 | convolution fusion | flops 3229614080 | bytes 29097984 | tf_op jit(solution)/shard_map/dot_general | solution.py:10
  403.6 3.5 all-to-all-start.7
  407.0 12.5 %fusion.97 = f32[1024,4096]{1,0:T(8,128)} fusion(bf16[384,1024]{1,0:T(8,128)(2,1)} %copy-done.7, bf16[384,4096]{1,0:T(8,128)(2,1)} %all-gather.9.cloned.1.call-done), kind=kOutput, calls=%fused_computation.185 | convolution fusion | flops 3221225472 | bytes 20709376 | tf_op jit(solution)/shard_map/dot_general | solution.py:10
  419.7 5.2 %all-to-all-start.5 = ((bf16[512,4,96]{0,2,1:T(8,128)(2,1)}), bf16[512,4,96]{0,2,1:T(8,128)(2,1)S(1)}, u32[]{:S(2)}, u32[]{:S(2)}) async-start(bf16[512,4,96]{0,2,1:T(8,128)(2,1)} %bitcast.272), calls=%async_computation.8 | async-start | bytes 786432 | tf_op jit(solution)/shard_map/all_to_all | solution.py:52
  424.9 11.1 %fusion.2 = bf16[1,1024,4096]{2,1,0:T(8,128)(2,1)} fusion(f32[1024,4096]{1,0:T(8,128)} %fusion.97, bf16[384,1024]{1,0:T(8,128)(2,1)S(1)} %copy-done.5, bf16[384,4096]{1,0:T(8,128)(2,1)} %all-gather.11.cloned.1.call-done), kind=kOutput, calls=%fused_computation.17 | convolution fusion | flops 3229614080 | bytes 29097984 | tf_op jit(solution)/shard_map/dot_general | solution.py:10
  436.0 1.0 gather_fusion.11
  437.0 1.0 gather_fusion.10
  438.0 1.0 gather_fusion.8
  439.0 1.0 gather_fusion.7
  440.7 0.7 pad_maximum_fusion.1
  (146 shorter events, 13.1 us)
Async XLA Ops:
  7.2 198.7 %copy-start = (bf16[512,4]{0,1:T(4,128)(2,1)S(1)}, bf16[512,4]{0,1:T(4,128)(2,1)}, u32[]{:S(2)}) copy-start(bf16[512,4]{0,1:T(4,128)(2,1)} %param.13) | copy-start | bytes 12292
  7.2 55.8 %all-gather.7.cloned.1.call-start = ((), (), s32[]{:S(2)}) async-start(), calls=%async_computation.14 | async-start | bytes 3538944 | tf_op jit(solution)/shard_map/all_gather | solution.py:47
  9.4 23.8 %copy-start.16 = (s32[128,2]{0,1:T(2,128)}, s32[128,2]{0,1:T(2,128)S(1)}, u32[]{:S(2)}) copy-start(s32[128,2]{0,1:T(2,128)S(1)} %get-tuple-element.41) | copy-start | bytes 3076
  9.4 23.9 %copy-start.17 = (s32[128,2]{0,1:T(2,128)}, s32[128,2]{0,1:T(2,128)S(1)}, u32[]{:S(2)}) copy-start(s32[128,2]{0,1:T(2,128)S(1)} %get-tuple-element.40) | copy-start | bytes 3076
  9.6 23.7 %copy-start.27 = (pred[384]{0:T(512)(128)(4,1)}, pred[384]{0:T(512)(128)(4,1)S(1)}, u32[]{:S(2)}) copy-start(pred[384]{0:T(512)(128)(4,1)S(1)} %compare_and_fusion.2) | copy-start | bytes 1156
  31.0 66.6 %all-gather.5.cloned.1.call-start = ((), (), s32[]{:S(2)}) async-start(), calls=%async_computation.12 | async-start | bytes 3538944 | tf_op jit(solution)/shard_map/all_gather | solution.py:47
  33.5 37.3 %copy-start.28 = (pred[384]{0:T(512)(128)(4,1)}, pred[384]{0:T(512)(128)(4,1)S(1)}, u32[]{:S(2)}) copy-start(pred[384]{0:T(512)(128)(4,1)S(1)} %compare_and_fusion.5) | copy-start | bytes 1156
  47.7 100.0 %reduce-scatter.7.cloned.1.call-start = ((), (), s32[]{:S(2)}) async-start(), calls=%async_computation.15 | async-start | bytes 3538944 | tf_op jit(solution)/shard_map/reduce_scatter | solution.py:89
  63.0 7.8 %copy-start.1 = (bf16[384,4096]{1,0:T(8,128)(2,1)S(1)}, bf16[384,4096]{1,0:T(8,128)(2,1)}, u32[]{:S(2)}) copy-start(bf16[384,4096]{1,0:T(8,128)(2,1)} %all-gather.7.cloned.1.call-done) | copy-start | bytes 9437188
  70.8 8.9 %copy-start.36 = (f32[384,1024]{1,0:T(8,128)}, f32[384,1024]{1,0:T(8,128)S(1)}, u32[]{:S(2)}) copy-start(f32[384,1024]{1,0:T(8,128)S(1)} %fusion.23) | copy-start | bytes 4718596
  79.7 0.9 copy-start.4
  88.8 108.8 %reduce-scatter.5.cloned.1.call-start = ((), (), s32[]{:S(2)}) async-start(), calls=%async_computation.13 | async-start | bytes 3538944 | tf_op jit(solution)/shard_map/reduce_scatter | solution.py:89
  97.6 7.8 %copy-start.2 = (bf16[384,4096]{1,0:T(8,128)(2,1)S(1)}, bf16[384,4096]{1,0:T(8,128)(2,1)}, u32[]{:S(2)}) copy-start(bf16[384,4096]{1,0:T(8,128)(2,1)} %all-gather.5.cloned.1.call-done) | copy-start | bytes 9437188
  105.4 9.1 %copy-start.35 = (f32[384,1024]{1,0:T(8,128)}, f32[384,1024]{1,0:T(8,128)S(1)}, u32[]{:S(2)}) copy-start(f32[384,1024]{1,0:T(8,128)S(1)} %fusion.25) | copy-start | bytes 4718596
  114.5 0.9 copy-start.7
  123.6 0.7 copy-start.15
  147.6 49.9 %all-to-all-start.3 = ((bf16[512,4,96]{0,2,1:T(8,128)(2,1)}), bf16[512,4,96]{0,2,1:T(8,128)(2,1)}, u32[]{:S(2)}, u32[]{:S(2)}) async-start(bf16[512,4,96]{0,2,1:T(8,128)(2,1)} %bitcast.271), calls=%async_computation.5 | async-start | bytes 786432 | tf_op jit(solution)/shard_map/all_to_all | solution.py:52
  153.4 55.8 %copy-start.18 = (s32[1024]{0:T(1024)}, s32[1024]{0:T(1024)S(1)}, u32[]{:S(2)}) copy-start(s32[1024]{0:T(1024)S(1)} %pad_clamp_fusion.1) | copy-start | bytes 12292
  197.5 16.2 %all-to-all-start.1 = ((bf16[512,4,96]{0,2,1:T(8,128)(2,1)}), bf16[512,4,96]{0,2,1:T(8,128)(2,1)}, u32[]{:S(2)}, u32[]{:S(2)}) async-start(bf16[512,4,96]{0,2,1:T(8,128)(2,1)} %bitcast.270), calls=%async_computation.2 | async-start | bytes 786432 | tf_op jit(solution)/shard_map/all_to_all | solution.py:52
  202.1 84.2 %all-gather.11.cloned.1.call-start = ((), (), s32[]{:S(2)}) async-start(), calls=%async_computation.18 | async-start | bytes 3538944 | tf_op jit(solution)/shard_map/all_gather | solution.py:47
  236.8 0.6 copy-start.23
  236.8 0.6 copy-start.24
  255.3 76.5 %all-gather.9.cloned.1.call-start = ((), (), s32[]{:S(2)}) async-start(), calls=%async_computation.16 | async-start | bytes 3538944 | tf_op jit(solution)/shard_map/all_gather | solution.py:47
  259.9 0.5 copy-start.25
  259.9 0.5 copy-start.26
  276.3 127.2 %reduce-scatter.11.cloned.1.call-start = ((), (), s32[]{:S(2)}) async-start(), calls=%async_computation.19 | async-start | bytes 3538944 | tf_op jit(solution)/shard_map/reduce_scatter | solution.py:125
  286.3 20.7 %slice-start = ((s8[8388608]{0:T(1024)(128)(4,1)}), s8[4194304]{0:T(1024)(128)(4,1)S(1)}, s32[]{:S(2)}) async-start(s8[8388608]{0:T(1024)(128)(4,1)} %bitcast.281), calls=%async_computation.20 | async-start | bytes 8388608
  295.5 11.5 %copy-start.11 = (bf16[384,1024]{1,0:T(8,128)(2,1)}, bf16[384,1024]{1,0:T(8,128)(2,1)S(1)}, u32[]{:S(2)}) copy-start(bf16[384,1024]{1,0:T(8,128)(2,1)S(1)} %get-tuple-element.33) | copy-start | bytes 2359300
  295.5 11.5 %copy-start.13 = (bf16[384,1024]{1,0:T(8,128)(2,1)}, bf16[384,1024]{1,0:T(8,128)(2,1)S(1)}, u32[]{:S(2)}) copy-start(bf16[384,1024]{1,0:T(8,128)(2,1)S(1)} %get-tuple-element.32) | copy-start | bytes 2359300
  295.5 11.5 %slice-start.1 = ((s8[8388608]{0:T(1024)(128)(4,1)}), s8[4194304]{0:T(1024)(128)(4,1)S(1)}, s32[]{:S(2)}) async-start(s8[8388608]{0:T(1024)(128)(4,1)} %bitcast.281), calls=%async_computation.21 | async-start | bytes 8388608
  314.2 15.7 %copy-start.6 = (bf16[128,512]{1,0:T(8,128)(2,1)S(1)}, bf16[128,512]{1,0:T(8,128)(2,1)}, u32[]{:S(2)}) copy-start(bf16[128,512]{1,0:T(8,128)(2,1)} %gather_fusion.1) | copy-start | bytes 393220
  314.3 15.7 %copy-start.19 = (pred[128]{0:T(512)(128)(4,1)S(1)}, pred[128]{0:T(512)(128)(4,1)}, u32[]{:S(2)}) copy-start(pred[128]{0:T(512)(128)(4,1)} %get-tuple-element.22) | copy-start | bytes 388
  314.3 105.4 %reduce-scatter.9.cloned.1.call-start = ((), (), s32[]{:S(2)}) async-start(), calls=%async_computation.17 | async-start | bytes 3538944 | tf_op jit(solution)/shard_map/reduce_scatter | solution.py:125
  314.3 1.1 copy-start.29
  314.4 1.1 copy-start.31
  331.8 21.6 %slice-start.2 = ((s8[8388608]{0:T(1024)(128)(4,1)}), s8[4194304]{0:T(1024)(128)(4,1)S(1)}, s32[]{:S(2)}) async-start(s8[8388608]{0:T(1024)(128)(4,1)} %bitcast.283), calls=%async_computation.22 | async-start | bytes 8388608
  341.8 11.6 %copy-start.8 = (bf16[384,1024]{1,0:T(8,128)(2,1)}, bf16[384,1024]{1,0:T(8,128)(2,1)S(1)}, u32[]{:S(2)}) copy-start(bf16[384,1024]{1,0:T(8,128)(2,1)S(1)} %get-tuple-element.31) | copy-start | bytes 2359300
  341.9 11.6 %copy-start.10 = (bf16[384,1024]{1,0:T(8,128)(2,1)}, bf16[384,1024]{1,0:T(8,128)(2,1)S(1)}, u32[]{:S(2)}) copy-start(bf16[384,1024]{1,0:T(8,128)(2,1)S(1)} %get-tuple-element.30) | copy-start | bytes 2359300
  341.9 11.5 %slice-start.3 = ((s8[8388608]{0:T(1024)(128)(4,1)}), s8[4194304]{0:T(1024)(128)(4,1)S(1)}, s32[]{:S(2)}) async-start(s8[8388608]{0:T(1024)(128)(4,1)} %bitcast.283), calls=%async_computation.23 | async-start | bytes 8388608
  360.3 12.6 %copy-start.3 = (bf16[384,4096]{1,0:T(8,128)(2,1)S(1)}, bf16[384,4096]{1,0:T(8,128)(2,1)}, u32[]{:S(2)}) copy-start(bf16[384,4096]{1,0:T(8,128)(2,1)} %all-gather.5.cloned.1.call-done) | copy-start | bytes 9437188
  360.3 12.5 %copy-start.9 = (bf16[384,1024]{1,0:T(8,128)(2,1)S(1)}, bf16[384,1024]{1,0:T(8,128)(2,1)}, u32[]{:S(2)}) copy-start(bf16[384,1024]{1,0:T(8,128)(2,1)} %copy-done.8) | copy-start | bytes 2359300
  372.9 8.7 %copy-start.14 = (bf16[384,1024]{1,0:T(8,128)(2,1)S(1)}, bf16[384,1024]{1,0:T(8,128)(2,1)}, u32[]{:S(2)}) copy-start(bf16[384,1024]{1,0:T(8,128)(2,1)} %copy-done.13) | copy-start | bytes 2359300
  381.5 11.2 %copy-start.12 = (bf16[384,1024]{1,0:T(8,128)(2,1)S(1)}, bf16[384,1024]{1,0:T(8,128)(2,1)}, u32[]{:S(2)}) copy-start(bf16[384,1024]{1,0:T(8,128)(2,1)} %copy-done.11) | copy-start | bytes 2359300
  403.6 16.1 %all-to-all-start.7 = ((bf16[512,4,96]{0,2,1:T(8,128)(2,1)}), bf16[512,4,96]{0,2,1:T(8,128)(2,1)S(1)}, u32[]{:S(2)}, u32[]{:S(2)}) async-start(bf16[512,4,96]{0,2,1:T(8,128)(2,1)} %bitcast.269), calls=%async_computation.11 | async-start | bytes 786432 | tf_op jit(solution)/shard_map/all_to_all | solution.py:52
  407.0 17.9 %copy-start.5 = (bf16[384,1024]{1,0:T(8,128)(2,1)S(1)}, bf16[384,1024]{1,0:T(8,128)(2,1)}, u32[]{:S(2)}) copy-start(bf16[384,1024]{1,0:T(8,128)(2,1)} %copy-done.4) | copy-start | bytes 2359300
  419.7 18.3 %all-to-all-start.5 = ((bf16[512,4,96]{0,2,1:T(8,128)(2,1)}), bf16[512,4,96]{0,2,1:T(8,128)(2,1)S(1)}, u32[]{:S(2)}, u32[]{:S(2)}) async-start(bf16[512,4,96]{0,2,1:T(8,128)(2,1)} %bitcast.272), calls=%async_computation.8 | async-start | bytes 786432 | tf_op jit(solution)/shard_map/all_to_all | solution.py:52
  436.0 4.0 copy-start.21
  436.0 4.0 copy-start.22
  436.0 4.0 copy-start.32
  436.0 4.0 copy-start.33
  436.0 4.3 copy-start.20
  436.0 4.3 copy-start.30
  436.0 4.3 copy-start.34
Sparse Core Ops, SparseCore 0:
  31.1 31.8 all-gather.6
  64.9 32.7 all-gather.4
  101.6 46.0 reduce-scatter.6
  151.5 46.0 reduce-scatter.4
  255.4 30.8 all-gather.10
  288.0 32.7 all-gather.8
  324.2 46.0 reduce-scatter.10
  373.6 46.0 reduce-scatter.8
where the time goes:
time: 456 us; the launch traced here: 449 us
  matrix products  179 us (39%)
  waiting for transfers between devices  100 us (22%)
  blocking collectives  87.2 us (19%)
  local copies, waits for them, and re-layouts  29.3 us (6%)
  other arithmetic  19.1 us (4%)
  starting transfers between devices  18.8 us (4%)
  between operations  15.2 us (3%)
    dot_general x6, matrix products, contract_first(): lax.dot_general(left, right, (((0,), (0,)), ((), ())), preferred_element_...  66.8 us
    reduce_scatter x2, waiting for transfers between devices, shards(): lax.psum_scatter(lax.dot_general(down_w, hidden, (((0,), (1,)), ((), ()))...  66 us
    all_to_all x4, blocking collectives, deliver(): lax.all_to_all(pack(rows, source_row, filled, scale), 'ep', split_axis=0,...  61.7 us
    dot_general x6, matrix products, contract_last(): lax.dot_general(left, right, (((1,), (1,)), ((), ())), preferred_element_...  56.3 us
    all_gather x4, waiting for transfers between devices, deliver(): result = lax.all_gather(moved, 'rep', axis=1, tiled=True)  33.3 us
    dot_general x2, matrix products, shards(): pre_up = jnp.dot(expert_rows, up_w, preferred_element_type=jnp.float32)  18 us
    all_to_all x4, starting transfers between devices, collect(): lax.all_to_all(columns, 'ep', split_axis=1, concat_axis=1, tiled=True)  17.8 us
    dot_general x2, matrix products, shards(): lax.dot_general(down_w, hidden, (((0,), (1,)), ((), ())), preferred_eleme...  16.3 us
  transfers between devices with their start and end apart: 12, of which 7 were waited for; matrix products, arithmetic and copies ran while one was open for 45% of the time, Pallas kernels for 0%

commit v1 on v0

v1 whole, which is shorter than its diff:
```python
import functools

import jax
import jax.numpy as jnp
from jax import lax
from jax.experimental import pallas as pl
from jax.experimental.pallas import tpu as pltpu
from jax.sharding import PartitionSpec as P


TOP = 2
BF = jnp.bfloat16
F32 = jnp.float32
HI = lax.Precision.HIGHEST
ANY = pl.BlockSpec(memory_space=pl.ANY)


def mm(a, b):
    return jnp.dot(a, b, preferred_element_type=F32)


def mm_nt(a, b, precision=None):
    return lax.dot_general(
        a, b, (((1,), (1,)), ((), ())), preferred_element_type=F32, precision=precision
    )


def mm_tn(a, b, precision=None):
    return lax.dot_general(
        a, b, (((0,), (0,)), ((), ())), preferred_element_type=F32, precision=precision
    )


def call(kernel, grid, scalars, ins, outs, scratch=(), alias=None, flops=0, vmem=48):
    return pallas(kernel, grid, scalars, ins, outs, scratch, alias, flops, vmem)


def pallas(kernel, grid, scalars, ins, outs, scratch, alias, flops, vmem):
    return pl.pallas_call(
        kernel,
        grid_spec=pltpu.PrefetchScalarGridSpec(
            num_scalar_prefetch=len(scalars),
            grid=grid,
            in_specs=[spec for _, spec in ins],
            out_specs=[spec for _, spec in outs],
            scratch_shapes=list(scratch),
        ),
        out_shape=[shape for shape, _ in outs],
        input_output_aliases=alias or {},
        compiler_params=pltpu.CompilerParams(vmem_limit_bytes=vmem << 20),
        cost_estimate=pl.CostEstimate(flops=flops, bytes_accessed=flops // 1000, transcendentals=0),
    )(*scalars, *[array for array, _ in ins])


def whole(array):
    rank = len(array.shape)
    return pl.BlockSpec(array.shape, lambda *_: (0,) * rank)


def shape(dims, kind):
    return jax.ShapeDtypeStruct(dims, kind)


def rows_iota(rows, cols):
    return lax.broadcasted_iota(jnp.int32, (rows, cols), 0)


def slots_of(ids, step, experts, capacity, tok_rows):
    first = ids[TOP * step : TOP * step + 1, :]
    second = ids[TOP * step + 1 : TOP * step + 2, :]
    numbers = rows_iota(max(8, experts), tok_rows)
    hit_first = numbers == first
    hit_second = numbers == second
    named = (hit_first | hit_second).astype(F32)
    earlier = rows_iota(tok_rows, tok_rows) < lax.broadcasted_iota(
        jnp.int32, (tok_rows, tok_rows), 1
    )
    before = mm(named.astype(BF), earlier.astype(F32).astype(BF))
    place_first = jnp.sum(jnp.where(hit_first, before, 0.0), axis=0, keepdims=True)
    place_second = jnp.sum(jnp.where(hit_second, before, 0.0), axis=0, keepdims=True)
    return (
        first * capacity + place_first.astype(jnp.int32),
        second * capacity + place_second.astype(jnp.int32),
    )


def match(slots, step, expert, capacity, tok_rows):
    numbers = rows_iota(capacity, tok_rows) + expert * capacity
    return (
        numbers == slots[TOP * step : TOP * step + 1, :],
        numbers == slots[TOP * step + 1 : TOP * step + 2, :],
    )


def ones_of(mask):
    return mask.astype(F32).astype(BF)


def pack_tokens(me, ids, tokens, router, *outs, micro, experts, capacity):
    packed, partial, slots_out = outs[:-2], outs[-2], outs[-1]
    tok_rows = tokens.shape[1]
    listed = ids[...]
    for step in range(micro):
        first, second = slots_of(listed, step, experts, capacity, tok_rows)
        slots_out[TOP * step : TOP * step + 1, :] = first
        slots_out[TOP * step + 1 : TOP * step + 2, :] = second
        partial[experts * step : experts * (step + 1), :] = mm_nt(router[...], tokens[step])
    slots = slots_out[...]
    for turn in range(experts):
        for step in range(micro):
            a, b = match(slots, step, lax.rem(me[0] + turn, experts), capacity, tok_rows)
            packed[turn][step] = mm(ones_of(a | b), tokens[step]).astype(BF)


def pack_cots(me, ids, slots, logits, cots, *outs, micro, experts, capacity):
    packed, gates = outs[:-1], outs[-1]
    tok_rows = cots.shape[1]
    for step in range(micro):
        chosen = []
        for k in range(TOP):
            row = TOP * step + k
            named = rows_iota(experts, tok_rows) == ids[row : row + 1, :]
            part = logits[experts * step : experts * (step + 1), :]
            chosen.append(jnp.sum(jnp.where(named, part, 0.0), axis=0, keepdims=True))
        spread = chosen[0] - chosen[1]
        gates[TOP * step : TOP * step + 1, :] = jax.nn.sigmoid(spread)
        gates[TOP * step + 1 : TOP * step + 2, :] = jax.nn.sigmoid(-spread)
    listed = slots[...]
    for step in range(micro):
        for turn in range(experts):
            a, b = match(listed, step, lax.rem(me[0] + turn, experts), capacity, tok_rows)
            weight = jnp.where(a, gates[TOP * step : TOP * step + 1, :], 0.0) + jnp.where(
                b, gates[TOP * step + 1 : TOP * step + 2, :], 0.0
            )
            weight = jnp.sum(weight, axis=1, keepdims=True)
            packed[turn][step] = (mm(ones_of(a | b), cots[step]) * weight).astype(BF)


def assemble(rank, pieces, plan, out):
    slots, width = pieces[0].shape[1:]
    for piece, (step, numbers) in zip(pieces, plan):
        for i, k in enumerate(numbers):
            at = pl.multiple_of(jnp.bitwise_xor(rank, k) * width, 128)
            out[step * slots : (step + 1) * slots, pl.ds(at, width)] = piece[i]


def pre_kernel(rank, *refs, plan):
    pieces = refs[: len(plan)]
    gate_w, up_w, _, rows, hidden, pre_gate, pre_up = refs[len(plan) :]

    @pl.when(pl.program_id(0) == 0)
    def _():
        assemble(rank[0], pieces, plan, rows)

    pre_tile(rows, gate_w, up_w, hidden, pre_gate, pre_up)


def pre_rest_kernel(rows, gate_w, up_w, _a, _b, _c, _d, hidden, pre_gate, pre_up):
    pre_tile(rows, gate_w, up_w, hidden, pre_gate, pre_up)


def pre_tile(rows, gate_w, up_w, hidden, pre_gate, pre_up):
    gate = mm(rows[...], gate_w[...])
    up = mm(rows[...], up_w[...])
    pre_gate[...] = gate
    pre_up[...] = up
    hidden[...] = (gate * jax.nn.sigmoid(gate) * up).astype(BF)


def grad_kernel(rank, *refs, plan):
    pieces = refs[: len(plan)]
    down_w, hidden, pre_gate, pre_up, _, rows, gate_grad, up_grad, dots, acc = refs[len(plan) :]
    at = pl.program_id(0)

    @pl.when(at == 0)
    def _():
        assemble(rank[0], pieces, plan, rows)
        acc[...] = jnp.zeros_like(acc)

    grad = mm_nt(rows[...], down_w[...])
    gate = pre_gate[...]
    sig = jax.nn.sigmoid(gate)
    gate_grad[...] = (grad * pre_up[...] * (sig * (1.0 + gate * (1.0 - sig)))).astype(BF)
    up_grad[...] = (grad * (gate * sig)).astype(BF)
    product = grad * hidden[...].astype(F32)
    total = acc[...]
    for i in range(product.shape[1] // 128):
        total = total + product[:, 128 * i : 128 * (i + 1)]
    acc[...] = total

    @pl.when(at == pl.num_programs(0) - 1)
    def _():
        dots[...] = mm_nt(jnp.ones((8, 128), F32), acc[...], HI)


def spread(total, plan, outs):
    slots = outs[0].shape[1]
    for i, places in enumerate(plan):

        @pl.when(pl.program_id(0) == i)
        def _():
            for step, (which, at) in enumerate(places):
                outs[which][at] = total[step * slots : (step + 1) * slots, :]


def out_send_kernel(rank, hidden, down_w, _, out):
    out[...] = mm(hidden[...], down_w[...]).astype(BF)


def out_keep_kernel(rank, hidden, down_w, recv, _, *outs, plan):
    total = (mm(hidden[...], down_w[...]) + recv[...].astype(F32)).astype(BF)
    spread(total, plan, outs)


def in_send_kernel(rank, gate_g, up_g, gate_w, up_w, _, out):
    out[...] = (mm_nt(gate_g[...], gate_w[...]) + mm_nt(up_g[...], up_w[...])).astype(BF)


def in_keep_kernel(rank, gate_g, up_g, gate_w, up_w, recv, _, *outs, plan):
    total = mm_nt(gate_g[...], gate_w[...]) + mm_nt(up_g[...], up_w[...])
    spread((total + recv[...].astype(F32)).astype(BF), plan, outs)


def add_kernel(kept, recv, kept_out, sent_out):
    half = kept_out.shape[0]
    for i in range(2 * half):
        out = kept_out if i < half else sent_out
        out[i % half] = (kept[i].astype(F32) + recv[i].astype(F32)).astype(BF)


def sum_kernel(*refs, micro):
    ins, outs = refs[: 2 * micro], refs[2 * micro :]
    rows = outs[0].shape[1]
    for i, out in enumerate(outs):
        for step in range(micro):
            kept = ins[2 * step][0, i * rows : (i + 1) * rows, :].astype(F32)
            recv = ins[2 * step + 1][0, i * rows : (i + 1) * rows, :].astype(F32)
            out[step] = (kept + recv).astype(BF)


def weight_kernel(left, right, _, out):
    out[0] = mm_tn(left[...], right[...]).astype(BF)


def column_of(gates, tok_rows):
    eye = (
        rows_iota(tok_rows, tok_rows) == lax.broadcasted_iota(jnp.int32, (tok_rows, tok_rows), 1)
    ).astype(F32)
    return mm_nt(eye, gates, HI)


def mix_kernel(me, slots, gates, *refs, micro, experts, capacity):
    blocks, out = refs[:-1], refs[-1]
    tok_rows = out.shape[1]
    columns = column_of(gates[...], tok_rows)
    listed = slots[...]
    for step in range(micro):
        picked = [0.0] * TOP
        for turn in range(experts):
            hot = match(listed, step, lax.rem(me[0] + turn, experts), capacity, tok_rows)
            block = blocks[turn][step]
            for k in range(TOP):
                picked[k] = picked[k] + mm_tn(ones_of(hot[k]), block)
        total = 0.0
        for k in range(TOP):
            total = total + columns[:, TOP * step + k : TOP * step + k + 1] * picked[k]
        out[step] = total.astype(BF)


def logit_kernel(me, ids, slots, gates, tokens, dots, logit_grad, router, *, micro, experts, capacity):
    tok_rows = tokens.shape[1]
    listed = slots[...]
    total = 0.0
    for step in range(micro):
        scaled = [0.0] * TOP
        for turn in range(experts):
            hot = match(listed, step, lax.rem(me[0] + turn, experts), capacity, tok_rows)
            for k in range(TOP):
                scaled[k] = scaled[k] + lax.dot_general(
                    dots[turn], hot[k].astype(F32), (((1,), (0,)), ((), ())),
                    preferred_element_type=F32, precision=HI,
                )[step : step + 1, :]
        delta = (
            scaled[0] * gates[TOP * step + 1 : TOP * step + 2, :]
            - scaled[1] * gates[TOP * step : TOP * step + 1, :]
        )
        rows = logit_grad.shape[0] // micro
        numbers = rows_iota(rows, tok_rows)
        first = numbers == ids[TOP * step : TOP * step + 1, :]
        second = numbers == ids[TOP * step + 1 : TOP * step + 2, :]
        grad = jnp.where(first, delta, 0.0) - jnp.where(second, delta, 0.0)
        logit_grad[step * rows : (step + 1) * rows, :] = grad
        total = total + lax.dot_general(
            grad, tokens[step].astype(F32), (((1,), (0,)), ((), ())),
            preferred_element_type=F32, precision=HI,
        )
    router[...] = total


def unpack_kernel(me, slots, logit_grad, router, *refs, micro, experts, capacity):
    blocks, out = refs[:-1], refs[-1]
    tok_rows = out.shape[1]
    listed = slots[...]
    rows = logit_grad.shape[0] // micro
    for step in range(micro):
        total = mm_tn(
            logit_grad[step * rows : step * rows + experts, :], router[...].astype(F32), HI
        )
        for turn in range(experts):
            a, b = match(listed, step, lax.rem(me[0] + turn, experts), capacity, tok_rows)
            total = total + mm_tn(ones_of(a | b), blocks[turn][step])
        out[step] = total.astype(BF)


def layer(tokens, expert_ids, router_weight, w_gate, w_up, w_down, cotangent):
    micro, tok_rows, width = tokens.shape
    experts = router_weight.shape[1]
    ranks = lax.axis_size("rep")
    places = lax.axis_size("ep")
    assert places == experts and ranks & (ranks - 1) == 0 and ranks > 2
    half = ranks // 2
    capacity = min(tok_rows, 3 * tok_rows * TOP // (2 * experts))
    slots_n = places * capacity
    gate_w, up_w, down_w = w_gate[0], w_up[0], w_down[0]
    features, units = gate_w.shape
    rank = lax.axis_index("rep").reshape(1)
    me = lax.axis_index("ep").reshape(1)
    sizes = dict(micro=micro, experts=experts, capacity=capacity)

    def swap(value, bits):
        return lax.ppermute(value, "rep", [(i, i ^ bits) for i in range(ranks)])

    def shift(value, turn):
        return lax.ppermute(value, "ep", [(i, (i + turn) % places) for i in range(places)])

    def full(array):
        return (array, whole(array))

    ids = jnp.transpose(expert_ids, (0, 2, 1)).reshape(micro * TOP, tok_rows)
    router = router_weight.T

    block = shape((micro, capacity, width), BF)
    token_rows = shape((micro * TOP, tok_rows), jnp.int32)
    logit_rows = shape((micro * experts, tok_rows), F32)
    *packed, logits, slots = call(
        functools.partial(pack_tokens, **sizes), (1,), [me],
        [full(ids), full(tokens), full(router)],
        [full(block)] * experts + [full(logit_rows), full(token_rows)],
        flops=10**8,
    )
    bits = 1
    while bits < ranks:
        logits = logits + swap(logits, bits)
        bits *= 2
    *cots, gates = call(
        functools.partial(pack_cots, **sizes), (1,), [me],
        [full(ids), full(slots), full(logits), full(cotangent)],
        [full(block)] * experts + [full(shape((micro * TOP, tok_rows), F32))],
        flops=10**8,
    )
    chip_bits = [1 << i for i in range(1, ranks.bit_length() - 1)]
    order = [chip_bits[m % len(chip_bits) :] + chip_bits[: m % len(chip_bits)] for m in range(micro)]

    def deliver(blocks):
        got = [blocks[0]] + [shift(blocks[turn], turn) for turn in range(1, places)]
        pieces, plan = [], []
        held, numbers = [], []
        for step in range(micro):
            held.append(jnp.concatenate([part[step : step + 1] for part in got], axis=1))
            numbers.append([0])
        for stage in range(len(chip_bits)):
            for step in range(micro):
                bit = order[step][stage]
                recv = swap(held[step], bit)
                there = [k ^ bit for k in numbers[step]]
                if stage == len(chip_bits) - 1:
                    pieces += [held[step], recv]
                    plan += [(step, numbers[step]), (step, there)]
                else:
                    held[step] = jnp.concatenate([held[step], recv], axis=0)
                    numbers[step] = numbers[step] + there
        for i in range(len(pieces)):
            pieces.append(swap(pieces[i], 1))
            plan.append((plan[i][0], [k ^ 1 for k in plan[i][1]]))
        return pieces, plan

    token_pieces, plan = deliver(packed)
    cot_pieces, _ = deliver(cots)

    tile = min(256, units // 2)
    steps = units // tile
    part = steps // 2
    all_rows = micro * slots_n
    work = 2 * all_rows * features * units
    columns = pl.BlockSpec((all_rows, tile), lambda i, *_: (0, i))
    rows_shape = shape((all_rows, features), BF)
    units_shape = shape((all_rows, units), BF)
    wide_shape = shape((all_rows, units), F32)

    weight = pl.BlockSpec((features, tile), lambda i, *_: (0, i))
    rows_in, *firsts = call(
        functools.partial(pre_kernel, plan=plan), (part,), [rank],
        [full(p) for p in token_pieces] + [(gate_w, weight), (up_w, weight), (cots[0], ANY)],
        [full(rows_shape), (units_shape, columns)] + [(wide_shape, columns)] * 2,
        flops=work,
    )
    weight = pl.BlockSpec((features, tile), lambda i: (0, i + part))
    later = pl.BlockSpec((all_rows, tile), lambda i: (0, i + part))
    hidden, pre_gate, pre_up = call(
        pre_rest_kernel, (part,), [],
        [full(rows_in), (gate_w, weight), (up_w, weight)]
        + [(array, ANY) for array in firsts] + [(gates, ANY)],
        [(units_shape, later)] + [(wide_shape, later)] * 2,
        alias={3: 0, 4: 1, 5: 2},
        flops=work,
    )
    sent = shape((half, all_rows, width), BF)
    kept = shape((half // 2, slots_n, width), BF)
    by_step = pl.BlockSpec((None, all_rows, width), lambda i, *_: (i, 0, 0))
    lists = []
    for step in range(micro):
        numbers = [0]
        for bit in order[step]:
            numbers = numbers + [k ^ bit for k in numbers]
        lists.append(numbers)
    homes = []
    for i in range(half):
        at = [lists[step].index(2 * i) for step in range(micro)]
        homes.append(
            [(2 * step + at[step] // (half // 2), at[step] % (half // 2)) for step in range(micro)]
        )

    def wide(odd):
        return pl.BlockSpec((units, width), lambda i, r: (0, jnp.bitwise_xor(r[0], 2 * i + odd)))

    def tall(odd):
        return pl.BlockSpec((width, units), lambda i, r: (jnp.bitwise_xor(r[0], 2 * i + odd), 0))

    def reduce(parts):
        parts = list(parts)
        for stage in reversed(range(len(chip_bits))):
            for step in range(micro):
                mine, theirs = parts[2 * step], parts[2 * step + 1]
                recv = swap(theirs, order[step][stage])
                if stage == 0:
                    parts[2 * step + 1] = recv
                else:
                    smaller = shape((mine.shape[0] // 2,) + mine.shape[1:], BF)
                    parts[2 * step], parts[2 * step + 1] = call(
                        add_kernel, (1,), [], [full(mine), full(recv)], [full(smaller)] * 2, flops=10**7
                    )
        blocks = call(
            functools.partial(sum_kernel, micro=micro), (1,), [],
            [full(part) for part in parts], [full(block)] * places, flops=10**7,
        )
        return [blocks[0]] + [shift(blocks[turn], -turn) for turn in range(1, places)]

    (out_sent,) = call(
        out_send_kernel, (half,), [rank],
        [full(hidden), (down_w, wide(1)), (hidden, ANY)], [(sent, by_step)], flops=work // 2,
    )
    out_parts = call(
        functools.partial(out_keep_kernel, plan=homes), (half,), [rank],
        [full(hidden), (down_w, wide(0)), (swap(out_sent, 1), by_step), (hidden, ANY)],
        [full(kept)] * (2 * micro), flops=work // 2,
    )
    out_blocks = reduce(out_parts)

    weight = pl.BlockSpec((tile, features), lambda i, *_: (i, 0))
    rows_cot, gate_g, up_g, dots = call(
        functools.partial(grad_kernel, plan=plan), (steps,), [rank],
        [full(p) for p in cot_pieces]
        + [(down_w, weight), (hidden, columns), (pre_gate, columns), (pre_up, columns)]
        + [(out_parts[0], ANY)],
        [full(rows_shape), (units_shape, columns), (units_shape, columns)]
        + [full(shape((8, all_rows), F32))],
        scratch=[pltpu.VMEM((all_rows, 128), F32)],
        flops=work,
    )
    (in_sent,) = call(
        in_send_kernel, (half,), [rank],
        [full(gate_g), full(up_g), (gate_w, tall(1)), (up_w, tall(1)), (dots, ANY)],
        [(sent, by_step)], flops=work,
    )
    in_parts = call(
        functools.partial(in_keep_kernel, plan=homes), (half,), [rank],
        [full(gate_g), full(up_g), (gate_w, tall(0)), (up_w, tall(0))]
        + [(swap(in_sent, 1), by_step), (in_sent, ANY)],
        [full(kept)] * (2 * micro), flops=work,
    )
    in_blocks = reduce(in_parts)
    span = min(512, features)
    rows_span = pl.BlockSpec((all_rows, span), lambda i: (0, i))
    down_spec = pl.BlockSpec((1, units, span), lambda i: (0, 0, i))
    (down_grad,) = call(
        weight_kernel, (features // span,), [],
        [full(hidden), (rows_cot, rows_span), (in_parts[0], ANY)],
        [(shape((1, units, features), BF), down_spec)],
        flops=work,
    )
    last, grads = down_grad, []
    for g in (gate_g, up_g):
        (last,) = call(
            weight_kernel, (features // span,), [],
            [(rows_in, rows_span), full(g), (last, ANY)],
            [(shape((1, features, units), BF), pl.BlockSpec((1, span, units), lambda i: (0, i, 0)))],
            flops=work,
        )
        grads.append(last)
    gate_grad, up_grad = grads

    scaled = dots[0].reshape(micro, places, capacity)
    scaled = jnp.pad(scaled, ((0, 8 - micro), (0, 0), (0, 0)))
    home = jnp.stack([scaled[:, 0]] + [shift(scaled[:, turn], -turn) for turn in range(1, places)])
    bits = 1
    while bits < ranks:
        home = home + swap(home, bits)
        bits *= 2
    (mixed,) = call(
        functools.partial(mix_kernel, **sizes), (1,), [me],
        [full(slots), full(gates)] + [full(b) for b in out_blocks],
        [full(shape(tokens.shape, BF))], flops=10**8,
    )
    padded = max(8, experts)
    logit_grad, router_grad = call(
        functools.partial(logit_kernel, **sizes), (1,), [me],
        [full(ids), full(slots), full(gates), full(tokens), full(home)],
        [full(shape((micro * padded, tok_rows), F32)), full(shape((padded, width), F32))],
        flops=10**8,
    )
    bits = 1
    while bits < places:
        theirs = lax.ppermute(router_grad, "ep", [(i, i ^ bits) for i in range(places)])
        router_grad = router_grad + theirs
        bits *= 2
    (token_grad,) = call(
        functools.partial(unpack_kernel, **sizes), (1,), [me],
        [full(slots), full(logit_grad), full(router)] + [full(b) for b in in_blocks],
        [full(shape(tokens.shape, BF))], flops=10**8,
    )
    return mixed, token_grad, gate_grad, up_grad, down_grad, router_grad[:experts].T


def solution(mesh):
    in_specs = (
        P(None, "ep", "rep"),
        P(None, "ep", None),
        P("rep", None),
        P("ep", None, "rep"),
        P("ep", None, "rep"),
        P("ep", "rep", None),
        P(None, "ep", "rep"),
    )
    out_specs = (
        P(None, "ep", "rep"),
        P(None, "ep", "rep"),
        P("ep", None, "rep"),
        P("ep", None, "rep"),
        P("ep", "rep", None),
        P("rep", None),
    )
    return jax.shard_map(layer, mesh=mesh, in_specs=in_specs, out_specs=out_specs, check_vma=False)
```

time: 456 us -> 302 us (0.66); the launches traced: 449 us -> 301 us
  matrix products: 179 us -> 0 us
  Pallas kernels: 0 us -> 117 us
  blocking collectives: 87.2 us -> 0 us
  starting transfers between devices: 18.8 us -> 66.8 us
  other arithmetic: 19.1 us -> 0.95 us
  local copies, waits for them, and re-layouts: 29.3 us -> 14.7 us
  between operations: 15.2 us -> 0.98 us
    dot_general x24 -> x0, matrix products: 179 us -> none  [the longest x6 66.8 us: contract_first(): lax.dot_general(left, right, (((0,), (0,)), ((), ())), preferred_element_...]
    pallas_call x0 -> x21, Pallas kernels: none -> 117 us  [pallas(): pl.pallas_call(kernel, grid_spec=pltpu.PrefetchScalarGridSpec(num_scalar_...]
    ppermute x0 -> x49, waiting for transfers between devices: none -> 100 us  [the longest x32 69.2 us: swap(): return lax.ppermute(value, 'rep', [(i, i ^ bits) for i in range(ranks)])]
    ppermute x0 -> x49, starting transfers between devices: none -> 66.8 us  [the longest x15 32.7 us: shift(): lax.ppermute(value, 'ep', [(i, (i + turn) % places) for i in range(places)])]
    reduce_scatter x4 -> x0, waiting for transfers between devices: 66.2 us -> none  [the longest x2 66 us: shards(): lax.psum_scatter(lax.dot_general(down_w, hidden, (((0,), (1,)), ((), ()))...]
    all_to_all x4 -> x0, blocking collectives: 61.7 us -> none  [deliver(): lax.all_to_all(pack(rows, source_row, filled, scale), 'ep', split_axis=0,...]
    all_gather x4 -> x0, waiting for transfers between devices: 33.3 us -> none  [deliver(): result = lax.all_gather(moved, 'rep', axis=1, tiled=True)]
    psum x2 -> x0, blocking collectives: 25.5 us -> none  [the longest x1 12.9 us: shards(): lax.psum(jnp.dot(tokens[step], router_weight, preferred_element_type=jnp....]
  transfers between devices with their start and end apart: 12 -> 49, of which waited for: 7 -> 21; matrix products, arithmetic and copies ran while one was open for 45% -> 0% of each run, Pallas kernels for 0% -> 19%
where the time goes in v1:
time: 302 us; the launch traced here: 301 us
  Pallas kernels  117 us (39%)
  waiting for transfers between devices  100 us (33%)
  starting transfers between devices  66.8 us (22%)
  local copies, waits for them, and re-layouts  14.7 us (5%)
    pallas_call x21, Pallas kernels, pallas(): pl.pallas_call(kernel, grid_spec=pltpu.PrefetchScalarGridSpec(num_scalar_...  117 us
    ppermute x32, waiting for transfers between devices, swap(): return lax.ppermute(value, 'rep', [(i, i ^ bits) for i in range(ranks)])  69.2 us
    ppermute x15, starting transfers between devices, shift(): lax.ppermute(value, 'ep', [(i, (i + turn) % places) for i in range(places)])  32.7 us
    ppermute x15, waiting for transfers between devices, shift(): lax.ppermute(value, 'ep', [(i, (i + turn) % places) for i in range(places)])  29.3 us
    ppermute x32, starting transfers between devices, swap(): return lax.ppermute(value, 'rep', [(i, i ^ bits) for i in range(ranks)])  26.3 us
    unnamed x42, local copies, waits for them, and re-layouts  14.5 us
    ppermute x2, starting transfers between devices, layer(): lax.ppermute(router_grad, 'ep', [(i, i ^ bits) for i in range(places)])  7.77 us
  transfers between devices with their start and end apart: 49, of which 21 were waited for; matrix products, arithmetic and copies ran while one was open for 0% of the time, Pallas kernels for 19%

profile of v1, /device:TPU:0, one launch (start us, length us, event | category | flops | bytes accessed | tf_op | source)
XLA Modules:
  0.0 300.8 jit_solution(16419189595309525775)
XLA Ops:
  3.5 3.1 %collective-permute-start.3 = (bf16[2,96,512]{2,1,0:T(8,128)(2,1)S(1)}, bf16[2,96,512]{2,1,0:T(8,128)(2,1)S(1)}, u32[]{:S(2)}, u32[]{:S(2)}) collective-permute-start(bf16[2,96,512]{2,1,0:T(8,128)(2,1)S(1)} %get-tuple-element.58), channel_id=1, source_target_pairs={{0,1},{1,2},{2,3},{3,0},{4,5},{5,6},{6,7},{7,4},{8,9},{9,10},{10,1... | collective-permute-start | bytes 589832 | tf_op jit(solution)/shard_map/ppermute | solution.py:334
  6.6 2.6 collective-permute-start.4
  9.2 1.3 collective-permute-start.5
  10.6 4.0 %collective-permute-done.3 = bf16[2,96,512]{2,1,0:T(8,128)(2,1)S(1)} collective-permute-done((bf16[2,96,512]{2,1,0:T(8,128)(2,1)S(1)}, bf16[2,96,512]{2,1,0:T(8,128)(2,1)S(1)}, u32[]{:S(2)}, u32[]{:S(2)}) %collective-permute-start.3) | collective-permute-done | bytes 196640 | tf_op jit(solution)/shard_map/ppermute | solution.py:334
  14.5 7.6 %collective-permute-done.4 = bf16[2,96,512]{2,1,0:T(8,128)(2,1)S(1)} collective-permute-done((bf16[2,96,512]{2,1,0:T(8,128)(2,1)S(1)}, bf16[2,96,512]{2,1,0:T(8,128)(2,1)S(1)}, u32[]{:S(2)}, u32[]{:S(2)}) %collective-permute-start.4) | collective-permute-done | bytes 196640 | tf_op jit(solution)/shard_map/ppermute | solution.py:334
  22.2 1.6 collective-permute-start.8
  23.8 1.6 collective-permute-start.6
  25.3 7.8 %collective-permute-done.8 = bf16[1,384,512]{2,1,0:T(8,128)(2,1)S(1)} collective-permute-done((bf16[1,384,512]{2,1,0:T(8,128)(2,1)S(1)}, bf16[1,384,512]{2,1,0:T(8,128)(2,1)S(1)}, u32[]{:S(2)}, u32[]{:S(2)}) %collective-permute-start.8) | collective-permute-done | bytes 393248 | tf_op jit(solution)/shard_map/ppermute | solution.py:331
  33.2 1.5 collective-permute-start.9
  34.8 1.6 collective-permute-start.7
  36.9 14.9 %collective-permute-done.9.refs_3_ = bf16[2,384,512]{2,1,0:T(8,128)(2,1)S(1)} collective-permute-done((bf16[2,384,512]{2,1,0:T(8,128)(2,1)S(1)}, bf16[2,384,512]{2,1,0:T(8,128)(2,1)S(1)}, u32[]{:S(2)}, u32[]{:S(2)}) %collective-permute-start.9) | collective-permute-done | bytes 786464 | tf_op jit(solution)/shard_map/ppermute | solution.py:331
  51.8 1.4 collective-permute-done.7.refs_1_
  53.7 2.1 collective-permute-done
  55.8 1.2 collective-permute-start.1
  57.1 2.4 collective-permute-done.1
  59.5 1.5 collective-permute-start.2
  61.0 2.1 collective-permute-done.2
  64.4 13.6 %shard_map.120 = (bf16[768,4096]{1,0:T(8,128)(2,1)}, bf16[768,1024]{1,0:T(8,128)(2,1)}, f32[768,1024]{1,0:T(8,128)}, f32[768,1024]{1,0:T(8,128)}) custom-call(s32[1]{0:T(128)} %bitcast.5.rank, bf16[2,384,512]{2,1,0:T(8,128)(2,1)S(1)} %pad_maximum_fusion.refs_0_, bf16[2,384,512]{2,1,0:T(8,128)(2,1)} %collective-permute-done.7.refs_1_, ...), custom_call_target="tpu_custom_call" | custom-call | flops 6442450944 | bytes 6442450 | tf_op jit(solution)/shard_map/pallas_call | solution.py:39
  78.0 1.4 copy-done
  79.4 1.9 copy-done.7
  81.3 12.7 %shard_map.121 = (bf16[768,1024]{1,0:T(8,128)(2,1)S(1)}, f32[768,1024]{1,0:T(8,128)S(1)}, f32[768,1024]{1,0:T(8,128)}) custom-call(bf16[768,4096]{1,0:T(8,128)(2,1)} %get-tuple-element.62.rows.left, bf16[4096,1024]{1,0:T(8,128)(2,1)} %bitcast.31, bf16[4096,1024]{1,0:T(8,128)(2,1)} %bitcast.35, ...), custom_call_target="tpu_custom_call", output_to_operand_aliasing={{0}: (3, {}), {1}: (4, {}), {2}: (5, {})} | custom-call | flops 6442450944 | bytes 6442450 | tf_op jit(solution)/shard_map/pallas_call | solution.py:39
  93.9 1.7 copy-done.8
  95.6 6.1 %shard_map.122 = bf16[4,768,512]{2,1,0:T(8,128)(2,1)S(1)} custom-call(s32[1]{0:T(128)} %bitcast.5.rank, bf16[768,1024]{1,0:T(8,128)(2,1)S(1)} %get-tuple-element.66.hidden._.refs_9_.left, bf16[1024,4096]{1,0:T(8,128)(2,1)} %bitcast.27, bf16[768,1024]{1,0:T(8,128)(2,1)S(1)} %get-tuple-element.66.hidden._.refs_9_.left), custom_call_target="tpu_custom_call" | custom-call | flops 3221225472 | bytes 3221225 | tf_op jit(solution)/shard_map/pallas_call | solution.py:39
  101.8 4.9 %collective-permute-start.22 = (bf16[2,96,512]{2,1,0:T(8,128)(2,1)S(1)}, bf16[2,96,512]{2,1,0:T(8,128)(2,1)S(1)}, u32[]{:S(2)}, u32[]{:S(2)}) collective-permute-start(bf16[2,96,512]{2,1,0:T(8,128)(2,1)S(1)} %get-tuple-element.79), channel_id=1, source_target_pairs={{0,1},{1,2},{2,3},{3,0},{4,5},{5,6},{6,7},{7,4},{8,9},{9,10},{10,1... | collective-permute-start | bytes 589832 | tf_op jit(solution)/shard_map/ppermute | solution.py:334
  106.6 2.4 collective-permute-start.24
  109.1 2.8 collective-permute-done.22
  111.9 7.7 %collective-permute-done.23 = bf16[2,96,512]{2,1,0:T(8,128)(2,1)S(1)} collective-permute-done((bf16[2,96,512]{2,1,0:T(8,128)(2,1)S(1)}, bf16[2,96,512]{2,1,0:T(8,128)(2,1)S(1)}, u32[]{:S(2)}, u32[]{:S(2)}) %collective-permute-start.23) | collective-permute-done | bytes 196640 | tf_op jit(solution)/shard_map/ppermute | solution.py:334
  119.9 1.6 collective-permute-start.27
  122.6 8.2 %collective-permute-done.27 = bf16[1,384,512]{2,1,0:T(8,128)(2,1)S(1)} collective-permute-done((bf16[1,384,512]{2,1,0:T(8,128)(2,1)S(1)}, bf16[1,384,512]{2,1,0:T(8,128)(2,1)S(1)}, u32[]{:S(2)}, u32[]{:S(2)}) %collective-permute-start.27) | collective-permute-done | bytes 393248 | tf_op jit(solution)/shard_map/ppermute | solution.py:331
  130.9 1.6 collective-permute-start.28
  132.5 1.0 collective-permute-start.26
  134.1 15.3 %collective-permute-done.28.refs_3_ = bf16[2,384,512]{2,1,0:T(8,128)(2,1)S(1)} collective-permute-done((bf16[2,384,512]{2,1,0:T(8,128)(2,1)S(1)}, bf16[2,384,512]{2,1,0:T(8,128)(2,1)S(1)}, u32[]{:S(2)}, u32[]{:S(2)}) %collective-permute-start.28) | collective-permute-done | bytes 786464 | tf_op jit(solution)/shard_map/ppermute | solution.py:331
  149.3 1.5 collective-permute-done.26.refs_1_
  150.9 1.7 copy-done.18
  152.5 7.4 %shard_map.123 = (bf16[2,384,512]{2,1,0:T(8,128)(2,1)S(1)}, bf16[2,384,512]{2,1,0:T(8,128)(2,1)}, bf16[2,384,512]{2,1,0:T(8,128)(2,1)S(1)}, bf16[2,384,512]{2,1,0:T(8,128)(2,1)}) custom-call(s32[1]{0:T(128)} %bitcast.5.rank, bf16[768,1024]{1,0:T(8,128)(2,1)S(1)} %get-tuple-element.66.hidden._.refs_9_.left, bf16[1024,4096]{1,0:T(8,128)(2,1)} %bitcast.28, ...), custom_call_target="tpu_custom_call" | custom-call | flops 3221225472 | bytes 3221225 | tf_op jit(solution)/shard_map/pallas_call | solution.py:39
  161.8 14.9 %shard_map.128 = (bf16[768,4096]{1,0:T(8,128)(2,1)}, bf16[768,1024]{1,0:T(8,128)(2,1)}, bf16[768,1024]{1,0:T(8,128)(2,1)}, f32[8,768]{1,0:T(8,128)S(1)}) custom-call(s32[1]{0:T(128)} %bitcast.5.rank, bf16[2,384,512]{2,1,0:T(8,128)(2,1)S(1)} %pad_maximum_fusion.2.refs_0_, bf16[2,384,512]{2,1,0:T(8,128)(2,1)S(1)} %collective-permute-done.26.refs_1_, ...), custom_call_target="tpu_custom_call" | custom-call | flops 6442450944 | bytes 6442450 | tf_op jit(solution)/shard_map/pallas_call | solution.py:39
  176.7 1.4 copy-done.3
  178.1 1.4 copy-done.5
  179.5 9.9 %shard_map.130._ = bf16[4,768,512]{2,1,0:T(8,128)(2,1)} custom-call(s32[1]{0:T(128)} %bitcast.5.rank, bf16[768,1024]{1,0:T(8,128)(2,1)S(1)} %copy-done.5, bf16[768,1024]{1,0:T(8,128)(2,1)S(1)} %copy-done.3, bf16[4096,1024]{1,0:T(8,128)(2,1)} %bitcast.32, bf16[4096,1024]{1,0:T(8,128)(2,1)} %bitcast.36, f32[8,768]{1,0:T(8,128)S(1)} %get-tuple-element.84._), custom_call_target="tpu_custom_call" | custom-call | flops 6442450944 | bytes 6442450 | tf_op jit(solution)/shard_map/pallas_call | solution.py:39
  190.7 1.0 collective-permute-start.17
  191.9 7.5 %collective-permute-start.33 = (f32[8,96]{1,0:T(8,128)S(1)}, f32[8,96]{1,0:T(8,128)S(1)}, u32[]{:S(2)}, u32[]{:S(2)}) collective-permute-start(f32[8,96]{1,0:T(8,128)S(1)} %get-tuple-element.119), channel_id=1, source_target_pairs={{0,3},{1,0},{2,1},{3,2},{4,7},{5,4},{6,5},{7,6},{8,11},{9,8},{10,9... | collective-permute-start | bytes 9224 | tf_op jit(solution)/shard_map/ppermute | solution.py:334
  199.4 1.3 collective-permute-done.33
  200.7 3.2 %collective-permute-done.34 = f32[8,96]{1,0:T(8,128)S(1)} collective-permute-done((f32[8,96]{1,0:T(8,128)S(1)}, f32[8,96]{1,0:T(8,128)S(1)}, u32[]{:S(2)}, u32[]{:S(2)}) %collective-permute-start.34) | collective-permute-done | bytes 3104 | tf_op jit(solution)/shard_map/ppermute | solution.py:334
  203.9 2.5 collective-permute-done.35
  206.5 3.1 %collective-permute-done.15.recv = bf16[2,384,512]{2,1,0:T(8,128)(2,1)S(1)} collective-permute-done((bf16[2,384,512]{2,1,0:T(8,128)(2,1)}, bf16[2,384,512]{2,1,0:T(8,128)(2,1)S(1)}, u32[]{:S(2)}, u32[]{:S(2)}) %collective-permute-start.15) | collective-permute-done | bytes 786464 | tf_op jit(solution)/shard_map/ppermute | solution.py:331
  210.7 1.2 collective-permute-start.18
  212.0 1.1 collective-permute-start.37
  213.0 7.4 %collective-permute-done.37 = f32[4,8,96]{2,1,0:T(8,128)S(1)} collective-permute-done((f32[4,8,96]{2,1,0:T(8,128)S(1)}, f32[4,8,96]{2,1,0:T(8,128)S(1)}, u32[]{:S(2)}, u32[]{:S(2)}) %collective-permute-start.37) | collective-permute-done | bytes 12320 | tf_op jit(solution)/shard_map/ppermute | solution.py:331
  221.2 2.9 collective-permute-done.38
  224.1 1.0 shard_map.129
  225.2 4.8 %collective-permute-start.47 = (f32[8,512]{1,0:T(8,128)S(1)}, f32[8,512]{1,0:T(8,128)S(1)}, u32[]{:S(2)}, u32[]{:S(2)}) collective-permute-start(f32[8,512]{1,0:T(8,128)S(1)} %get-tuple-element.101), channel_id=1, source_target_pairs={{0,1},{1,0},{2,3},{3,2},{4,5},{5,4},{6,7},{7,6},{8,9},{9,8},{10,11... | collective-permute-start | bytes 49160 | tf_op jit(solution)/shard_map/ppermute | solution.py:533
  230.0 1.7 collective-permute-done.47
  231.7 2.9 collective-permute-start.48
  234.8 4.4 %collective-permute-start.19 = (bf16[2,96,512]{2,1,0:T(8,128)(2,1)S(1)}, bf16[2,96,512]{2,1,0:T(8,128)(2,1)S(1)}, u32[]{:S(2)}, u32[]{:S(2)}) collective-permute-start(bf16[2,96,512]{2,1,0:T(8,128)(2,1)S(1)} %get-tuple-element.76), channel_id=1, source_target_pairs={{0,3},{1,0},{2,1},{3,2},{4,7},{5,4},{6,5},{7,6},{8,11},{9,8},{10,9... | collective-permute-start | bytes 589832 | tf_op jit(solution)/shard_map/ppermute | solution.py:334
  239.3 2.0 collective-permute-start.20
  241.3 10.5 %shard_map.131 = (bf16[2,384,512]{2,1,0:T(8,128)(2,1)S(1)}, bf16[2,384,512]{2,1,0:T(8,128)(2,1)S(1)}, bf16[2,384,512]{2,1,0:T(8,128)(2,1)S(1)}, bf16[2,384,512]{2,1,0:T(8,128)(2,1)S(1)}) custom-call(s32[1]{0:T(128)} %bitcast.5.rank, bf16[768,1024]{1,0:T(8,128)(2,1)S(1)} %copy-done.6, bf16[768,1024]{1,0:T(8,128)(2,1)} %get-tuple-element.87.up_g.right, ...), custom_call_target="tpu_custom_call" | custom-call | flops 6442450944 | bytes 6442450 | tf_op jit(solution)/shard_map/pallas_call | solution.py:39
  251.8 1.3 collective-permute-start.40
  253.1 1.1 collective-permute-start.42
  254.8 1.5 shard_map.127
  256.3 12.0 %shard_map.136._ = bf16[1,1024,4096]{2,1,0:T(8,128)(2,1)} custom-call(bf16[768,1024]{1,0:T(8,128)(2,1)S(1)} %copy-done.2, bf16[768,4096]{1,0:T(8,128)(2,1)} %get-tuple-element.100.right, bf16[2,384,512]{2,1,0:T(8,128)(2,1)S(1)} %get-tuple-element.88.kept._), custom_call_target="tpu_custom_call" | custom-call | flops 6442450944 | bytes 6442450 | tf_op jit(solution)/shard_map/pallas_call | solution.py:39
  270.6 12.0 %shard_map.137._ = bf16[1,4096,1024]{2,1,0:T(8,128)(2,1)} custom-call(bf16[768,4096]{1,0:T(8,128)(2,1)} %get-tuple-element.62.rows.left, bf16[768,1024]{1,0:T(8,128)(2,1)S(1)} %copy-done.6, bf16[1,1024,4096]{2,1,0:T(8,128)(2,1)} %shard_map.136._), custom_call_target="tpu_custom_call" | custom-call | flops 6442450944 | bytes 6442450 | tf_op jit(solution)/shard_map/pallas_call | solution.py:39
  282.8 3.8 %collective-permute-start.44 = (bf16[2,96,512]{2,1,0:T(8,128)(2,1)S(1)}, bf16[2,96,512]{2,1,0:T(8,128)(2,1)S(1)}, u32[]{:S(2)}, u32[]{:S(2)}) collective-permute-start(bf16[2,96,512]{2,1,0:T(8,128)(2,1)S(1)} %get-tuple-element.97), channel_id=1, source_target_pairs={{0,3},{1,0},{2,1},{3,2},{4,7},{5,4},{6,5},{7,6},{8,11},{9,8},{10,9... | collective-permute-start | bytes 589832 | tf_op jit(solution)/shard_map/ppermute | solution.py:334
  287.2 12.0 %shard_map.138 = bf16[1,4096,1024]{2,1,0:T(8,128)(2,1)} custom-call(bf16[768,4096]{1,0:T(8,128)(2,1)} %get-tuple-element.62.rows.left, bf16[768,1024]{1,0:T(8,128)(2,1)S(1)} %copy-done.4, bf16[1,4096,1024]{2,1,0:T(8,128)(2,1)} %shard_map.137._), custom_call_target="tpu_custom_call" | custom-call | flops 6442450944 | bytes 6442450 | tf_op jit(solution)/shard_map/pallas_call | solution.py:39
  299.2 1.6 shard_map.135
  (126 shorter events, 16.5 us)
Async XLA Ops:
  3.5 11.0 %collective-permute-start.3 = (bf16[2,96,512]{2,1,0:T(8,128)(2,1)S(1)}, bf16[2,96,512]{2,1,0:T(8,128)(2,1)S(1)}, u32[]{:S(2)}, u32[]{:S(2)}) collective-permute-start(bf16[2,96,512]{2,1,0:T(8,128)(2,1)S(1)} %get-tuple-element.58), channel_id=1, source_target_pairs={{0,1},{1,2},{2,3},{3,0},{4,5},{5,6},{6,7},{7,4},{8,9},{9,10},{10,1... | collective-permute-start | bytes 589832 | tf_op jit(solution)/shard_map/ppermute | solution.py:334
  6.6 15.5 %collective-permute-start.4 = (bf16[2,96,512]{2,1,0:T(8,128)(2,1)S(1)}, bf16[2,96,512]{2,1,0:T(8,128)(2,1)S(1)}, u32[]{:S(2)}, u32[]{:S(2)}) collective-permute-start(bf16[2,96,512]{2,1,0:T(8,128)(2,1)S(1)} %get-tuple-element.59), channel_id=1, source_target_pairs={{0,2},{1,3},{2,0},{3,1},{4,6},{5,7},{6,4},{7,5},{8,10},{9,11},{10,... | collective-permute-start | bytes 589832 | tf_op jit(solution)/shard_map/ppermute | solution.py:334
  9.2 12.9 %collective-permute-start.5 = (bf16[2,96,512]{2,1,0:T(8,128)(2,1)S(1)}, bf16[2,96,512]{2,1,0:T(8,128)(2,1)S(1)}, u32[]{:S(2)}, u32[]{:S(2)}) collective-permute-start(bf16[2,96,512]{2,1,0:T(8,128)(2,1)S(1)} %get-tuple-element.60), channel_id=1, source_target_pairs={{0,3},{1,0},{2,1},{3,2},{4,7},{5,4},{6,5},{7,6},{8,11},{9,8},{10,9... | collective-permute-start | bytes 589832 | tf_op jit(solution)/shard_map/ppermute | solution.py:334
  22.2 11.0 %collective-permute-start.8 = (bf16[1,384,512]{2,1,0:T(8,128)(2,1)S(1)}, bf16[1,384,512]{2,1,0:T(8,128)(2,1)S(1)}, u32[]{:S(2)}, u32[]{:S(2)}) collective-permute-start(bf16[1,384,512]{2,1,0:T(8,128)(2,1)S(1)} %pad_maximum_fusion.5), channel_id=1, source_target_pairs={{0,16},{4,20},{8,24},{12,28},{16,0},{20,4},{24,8},{28,12},{1,17},{... | collective-permute-start | bytes 1179656 | tf_op jit(solution)/shard_map/ppermute | solution.py:331
  23.7 39.3 %copy-start.13 = (bf16[2,128,512]{2,1,0:T(8,128)(2,1)S(1)}, bf16[2,128,512]{2,1,0:T(8,128)(2,1)}, u32[]{:S(2)}) copy-start(bf16[2,128,512]{2,1,0:T(8,128)(2,1)} %cots.1) | copy-start | bytes 786436
  23.8 39.3 %copy-start.17 = (s32[2,128,2]{1,2,0:T(2,128)S(1)}, s32[2,128,2]{1,2,0:T(2,128)}, u32[]{:S(2)}) copy-start(s32[2,128,2]{1,2,0:T(2,128)} %param.8) | copy-start | bytes 6148
  23.8 11.0 %collective-permute-start.6 = (bf16[1,384,512]{2,1,0:T(8,128)(2,1)S(1)}, bf16[1,384,512]{2,1,0:T(8,128)(2,1)S(1)}, u32[]{:S(2)}, u32[]{:S(2)}) collective-permute-start(bf16[1,384,512]{2,1,0:T(8,128)(2,1)S(1)} %pad_maximum_fusion.4), channel_id=1, source_target_pairs={{0,8},{4,12},{8,0},{12,4},{16,24},{20,28},{24,16},{28,20},{1,9},{5... | collective-permute-start | bytes 1179656 | tf_op jit(solution)/shard_map/ppermute | solution.py:331
  33.2 18.6 %collective-permute-start.9 = (bf16[2,384,512]{2,1,0:T(8,128)(2,1)S(1)}, bf16[2,384,512]{2,1,0:T(8,128)(2,1)S(1)}, u32[]{:S(2)}, u32[]{:S(2)}) collective-permute-start(bf16[2,384,512]{2,1,0:T(8,128)(2,1)S(1)} %pad_maximum_fusion.1.refs_2_), channel_id=1, source_target_pairs={{0,8},{4,12},{8,0},{12,4},{16,24},{20,28},{24,16},{28,20},{1,9},{5... | collective-permute-start | bytes 2359304 | tf_op jit(solution)/shard_map/ppermute | solution.py:331
  34.8 18.4 %collective-permute-start.7 = (bf16[2,384,512]{2,1,0:T(8,128)(2,1)S(1)}, bf16[2,384,512]{2,1,0:T(8,128)(2,1)}, u32[]{:S(2)}, u32[]{:S(2)}) collective-permute-start(bf16[2,384,512]{2,1,0:T(8,128)(2,1)S(1)} %pad_maximum_fusion.refs_0_), channel_id=1, source_target_pairs={{0,16},{4,20},{8,24},{12,28},{16,0},{20,4},{24,8},{28,12},{1,17},{... | collective-permute-start | bytes 2359304 | tf_op jit(solution)/shard_map/ppermute | solution.py:331
  36.4 27.1 %collective-permute-start.12 = (bf16[2,384,512]{2,1,0:T(8,128)(2,1)S(1)}, bf16[2,384,512]{2,1,0:T(8,128)(2,1)}, u32[]{:S(2)}, u32[]{:S(2)}) collective-permute-start(bf16[2,384,512]{2,1,0:T(8,128)(2,1)S(1)} %pad_maximum_fusion.1.refs_2_), channel_id=1, source_target_pairs={{0,4},{4,0},{8,12},{12,8},{16,20},{20,16},{24,28},{28,24},{1,5},{5... | collective-permute-start | bytes 2359304 | tf_op jit(solution)/shard_map/ppermute | solution.py:331
  36.4 27.1 %collective-permute-start.10 = (bf16[2,384,512]{2,1,0:T(8,128)(2,1)S(1)}, bf16[2,384,512]{2,1,0:T(8,128)(2,1)}, u32[]{:S(2)}, u32[]{:S(2)}) collective-permute-start(bf16[2,384,512]{2,1,0:T(8,128)(2,1)S(1)} %pad_maximum_fusion.refs_0_), channel_id=1, source_target_pairs={{0,4},{4,0},{8,12},{12,8},{16,20},{20,16},{24,28},{28,24},{1,5},{5... | collective-permute-start | bytes 2359304 | tf_op jit(solution)/shard_map/ppermute | solution.py:331
  51.8 11.7 %collective-permute-start.13 = (bf16[2,384,512]{2,1,0:T(8,128)(2,1)S(1)}, bf16[2,384,512]{2,1,0:T(8,128)(2,1)S(1)}, u32[]{:S(2)}, u32[]{:S(2)}) collective-permute-start(bf16[2,384,512]{2,1,0:T(8,128)(2,1)S(1)} %collective-permute-done.9.refs_3_), channel_id=1, source_target_pairs={{0,4},{4,0},{8,12},{12,8},{16,20},{20,16},{24,28},{28,24},{1,5},{5... | collective-permute-start | bytes 2359304 | tf_op jit(solution)/shard_map/ppermute | solution.py:331
  53.2 10.3 %collective-permute-start.11 = (bf16[2,384,512]{2,1,0:T(8,128)(2,1)}, bf16[2,384,512]{2,1,0:T(8,128)(2,1)}, u32[]{:S(2)}, u32[]{:S(2)}) collective-permute-start(bf16[2,384,512]{2,1,0:T(8,128)(2,1)} %collective-permute-done.7.refs_1_), channel_id=1, source_target_pairs={{0,4},{4,0},{8,12},{12,8},{16,20},{20,16},{24,28},{28,24},{1,5},{5... | collective-permute-start | bytes 2359304 | tf_op jit(solution)/shard_map/ppermute | solution.py:331
  53.2 2.6 collective-permute-start
  55.8 3.6 %collective-permute-start.1 = (f32[8,128]{1,0:T(8,128)S(1)}, f32[8,128]{1,0:T(8,128)S(1)}, u32[]{:S(2)}, u32[]{:S(2)}) collective-permute-start(f32[8,128]{1,0:T(8,128)S(1)} %add.26), channel_id=1, source_target_pairs={{0,8},{4,12},{8,0},{12,4},{16,24},{20,28},{24,16},{28,20},{1,9},{5... | collective-permute-start | bytes 12296 | tf_op jit(solution)/shard_map/ppermute | solution.py:331
  59.5 3.6 %collective-permute-start.2 = (f32[8,128]{1,0:T(8,128)S(1)}, f32[8,128]{1,0:T(8,128)S(1)}, u32[]{:S(2)}, u32[]{:S(2)}) collective-permute-start(f32[8,128]{1,0:T(8,128)S(1)} %add.27), channel_id=1, source_target_pairs={{0,16},{4,20},{8,24},{12,28},{16,0},{20,4},{24,8},{28,12},{1,17},{... | collective-permute-start | bytes 12296 | tf_op jit(solution)/shard_map/ppermute | solution.py:331
  78.0 1.4 copy-start
  79.4 1.9 copy-start.7
  93.9 1.7 copy-start.8
  95.6 55.3 %copy-start.1 = (bf16[768,1024]{1,0:T(8,128)(2,1)}, bf16[768,1024]{1,0:T(8,128)(2,1)S(1)}, u32[]{:S(2)}) copy-start(bf16[768,1024]{1,0:T(8,128)(2,1)S(1)} %get-tuple-element.66.hidden._.refs_9_.left) | copy-start | bytes 4718596
  101.7 49.2 %collective-permute-start.14 = (bf16[4,768,512]{2,1,0:T(8,128)(2,1)S(1)}, bf16[4,768,512]{2,1,0:T(8,128)(2,1)S(1)}, u32[]{:S(2)}, u32[]{:S(2)}) collective-permute-start(bf16[4,768,512]{2,1,0:T(8,128)(2,1)S(1)} %shard_map.122), channel_id=1, source_target_pairs={{0,4},{4,0},{8,12},{12,8},{16,20},{20,16},{24,28},{28,24},{1,5},{5... | collective-permute-start | bytes 9437192 | tf_op jit(solution)/shard_map/ppermute | solution.py:331
  101.8 10.2 %collective-permute-start.22 = (bf16[2,96,512]{2,1,0:T(8,128)(2,1)S(1)}, bf16[2,96,512]{2,1,0:T(8,128)(2,1)S(1)}, u32[]{:S(2)}, u32[]{:S(2)}) collective-permute-start(bf16[2,96,512]{2,1,0:T(8,128)(2,1)S(1)} %get-tuple-element.79), channel_id=1, source_target_pairs={{0,1},{1,2},{2,3},{3,0},{4,5},{5,6},{6,7},{7,4},{8,9},{9,10},{10,1... | collective-permute-start | bytes 589832 | tf_op jit(solution)/shard_map/ppermute | solution.py:334
  106.6 13.0 %collective-permute-start.23 = (bf16[2,96,512]{2,1,0:T(8,128)(2,1)S(1)}, bf16[2,96,512]{2,1,0:T(8,128)(2,1)S(1)}, u32[]{:S(2)}, u32[]{:S(2)}) collective-permute-start(bf16[2,96,512]{2,1,0:T(8,128)(2,1)S(1)} %get-tuple-element.80), channel_id=1, source_target_pairs={{0,2},{1,3},{2,0},{3,1},{4,6},{5,7},{6,4},{7,5},{8,10},{9,11},{10,... | collective-permute-start | bytes 589832 | tf_op jit(solution)/shard_map/ppermute | solution.py:334
  106.6 13.2 %collective-permute-start.24 = (bf16[2,96,512]{2,1,0:T(8,128)(2,1)S(1)}, bf16[2,96,512]{2,1,0:T(8,128)(2,1)S(1)}, u32[]{:S(2)}, u32[]{:S(2)}) collective-permute-start(bf16[2,96,512]{2,1,0:T(8,128)(2,1)S(1)} %get-tuple-element.81), channel_id=1, source_target_pairs={{0,3},{1,0},{2,1},{3,2},{4,7},{5,4},{6,5},{7,6},{8,11},{9,8},{10,9... | collective-permute-start | bytes 589832 | tf_op jit(solution)/shard_map/ppermute | solution.py:334
  119.9 10.9 %collective-permute-start.27 = (bf16[1,384,512]{2,1,0:T(8,128)(2,1)S(1)}, bf16[1,384,512]{2,1,0:T(8,128)(2,1)S(1)}, u32[]{:S(2)}, u32[]{:S(2)}) collective-permute-start(bf16[1,384,512]{2,1,0:T(8,128)(2,1)S(1)} %pad_maximum_fusion.7), channel_id=1, source_target_pairs={{0,16},{4,20},{8,24},{12,28},{16,0},{20,4},{24,8},{28,12},{1,17},{... | collective-permute-start | bytes 1179656 | tf_op jit(solution)/shard_map/ppermute | solution.py:331
  121.6 10.9 %collective-permute-start.25 = (bf16[1,384,512]{2,1,0:T(8,128)(2,1)S(1)}, bf16[1,384,512]{2,1,0:T(8,128)(2,1)S(1)}, u32[]{:S(2)}, u32[]{:S(2)}) collective-permute-start(bf16[1,384,512]{2,1,0:T(8,128)(2,1)S(1)} %pad_maximum_fusion.6), channel_id=1, source_target_pairs={{0,8},{4,12},{8,0},{12,4},{16,24},{20,28},{24,16},{28,20},{1,9},{5... | collective-permute-start | bytes 1179656 | tf_op jit(solution)/shard_map/ppermute | solution.py:331
  130.9 18.5 %collective-permute-start.28 = (bf16[2,384,512]{2,1,0:T(8,128)(2,1)S(1)}, bf16[2,384,512]{2,1,0:T(8,128)(2,1)S(1)}, u32[]{:S(2)}, u32[]{:S(2)}) collective-permute-start(bf16[2,384,512]{2,1,0:T(8,128)(2,1)S(1)} %pad_maximum_fusion.3.refs_2_), channel_id=1, source_target_pairs={{0,8},{4,12},{8,0},{12,4},{16,24},{20,28},{24,16},{28,20},{1,9},{5... | collective-permute-start | bytes 2359304 | tf_op jit(solution)/shard_map/ppermute | solution.py:331
  132.5 18.3 %collective-permute-start.26 = (bf16[2,384,512]{2,1,0:T(8,128)(2,1)S(1)}, bf16[2,384,512]{2,1,0:T(8,128)(2,1)S(1)}, u32[]{:S(2)}, u32[]{:S(2)}) collective-permute-start(bf16[2,384,512]{2,1,0:T(8,128)(2,1)S(1)} %pad_maximum_fusion.2.refs_0_), channel_id=1, source_target_pairs={{0,16},{4,20},{8,24},{12,28},{16,0},{20,4},{24,8},{28,12},{1,17},{... | collective-permute-start | bytes 2359304 | tf_op jit(solution)/shard_map/ppermute | solution.py:331
  133.5 27.3 %collective-permute-start.31 = (bf16[2,384,512]{2,1,0:T(8,128)(2,1)S(1)}, bf16[2,384,512]{2,1,0:T(8,128)(2,1)S(1)}, u32[]{:S(2)}, u32[]{:S(2)}) collective-permute-start(bf16[2,384,512]{2,1,0:T(8,128)(2,1)S(1)} %pad_maximum_fusion.3.refs_2_), channel_id=1, source_target_pairs={{0,4},{4,0},{8,12},{12,8},{16,20},{20,16},{24,28},{28,24},{1,5},{5... | collective-permute-start | bytes 2359304 | tf_op jit(solution)/shard_map/ppermute | solution.py:331
  133.5 27.3 %collective-permute-start.29 = (bf16[2,384,512]{2,1,0:T(8,128)(2,1)S(1)}, bf16[2,384,512]{2,1,0:T(8,128)(2,1)S(1)}, u32[]{:S(2)}, u32[]{:S(2)}) collective-permute-start(bf16[2,384,512]{2,1,0:T(8,128)(2,1)S(1)} %pad_maximum_fusion.2.refs_0_), channel_id=1, source_target_pairs={{0,4},{4,0},{8,12},{12,8},{16,20},{20,16},{24,28},{28,24},{1,5},{5... | collective-permute-start | bytes 2359304 | tf_op jit(solution)/shard_map/ppermute | solution.py:331
  149.3 11.5 %collective-permute-start.32 = (bf16[2,384,512]{2,1,0:T(8,128)(2,1)S(1)}, bf16[2,384,512]{2,1,0:T(8,128)(2,1)S(1)}, u32[]{:S(2)}, u32[]{:S(2)}) collective-permute-start(bf16[2,384,512]{2,1,0:T(8,128)(2,1)S(1)} %collective-permute-done.28.refs_3_), channel_id=1, source_target_pairs={{0,4},{4,0},{8,12},{12,8},{16,20},{20,16},{24,28},{28,24},{1,5},{5... | collective-permute-start | bytes 2359304 | tf_op jit(solution)/shard_map/ppermute | solution.py:331
  150.9 10.0 %collective-permute-start.30 = (bf16[2,384,512]{2,1,0:T(8,128)(2,1)S(1)}, bf16[2,384,512]{2,1,0:T(8,128)(2,1)S(1)}, u32[]{:S(2)}, u32[]{:S(2)}) collective-permute-start(bf16[2,384,512]{2,1,0:T(8,128)(2,1)S(1)} %collective-permute-done.26.refs_1_), channel_id=1, source_target_pairs={{0,4},{4,0},{8,12},{12,8},{16,20},{20,16},{24,28},{28,24},{1,5},{5... | collective-permute-start | bytes 2359304 | tf_op jit(solution)/shard_map/ppermute | solution.py:331
  150.9 1.7 copy-start.18
  176.7 1.4 copy-start.3
  178.1 1.4 copy-start.5
  179.5 30.1 %copy-start.10 = (bf16[2,384,512]{2,1,0:T(8,128)(2,1)S(1)}, bf16[2,384,512]{2,1,0:T(8,128)(2,1)}, u32[]{:S(2)}) copy-start(bf16[2,384,512]{2,1,0:T(8,128)(2,1)} %copy-done.9) | copy-start | bytes 2359300
  189.4 51.9 %collective-permute-start.39 = (bf16[4,768,512]{2,1,0:T(8,128)(2,1)}, bf16[4,768,512]{2,1,0:T(8,128)(2,1)}, u32[]{:S(2)}, u32[]{:S(2)}) collective-permute-start(bf16[4,768,512]{2,1,0:T(8,128)(2,1)} %shard_map.130._), channel_id=1, source_target_pairs={{0,4},{4,0},{8,12},{12,8},{16,20},{20,16},{24,28},{28,24},{1,5},{5... | collective-permute-start | bytes 9437192 | tf_op jit(solution)/shard_map/ppermute | solution.py:331
  189.9 19.7 %collective-permute-start.15 = (bf16[2,384,512]{2,1,0:T(8,128)(2,1)}, bf16[2,384,512]{2,1,0:T(8,128)(2,1)S(1)}, u32[]{:S(2)}, u32[]{:S(2)}) collective-permute-start(bf16[2,384,512]{2,1,0:T(8,128)(2,1)} %get-tuple-element.68), channel_id=1, source_target_pairs={{0,16},{4,20},{8,24},{12,28},{16,0},{20,4},{24,8},{28,12},{1,17},{... | collective-permute-start | bytes 2359304 | tf_op jit(solution)/shard_map/ppermute | solution.py:331
  190.7 19.8 %collective-permute-start.17 = (bf16[2,384,512]{2,1,0:T(8,128)(2,1)}, bf16[2,384,512]{2,1,0:T(8,128)(2,1)S(1)}, u32[]{:S(2)}, u32[]{:S(2)}) collective-permute-start(bf16[2,384,512]{2,1,0:T(8,128)(2,1)} %get-tuple-element.72), channel_id=1, source_target_pairs={{0,8},{4,12},{8,0},{12,4},{16,24},{20,28},{24,16},{28,20},{1,9},{5... | collective-permute-start | bytes 2359304 | tf_op jit(solution)/shard_map/ppermute | solution.py:331
  191.9 8.8 %collective-permute-start.33 = (f32[8,96]{1,0:T(8,128)S(1)}, f32[8,96]{1,0:T(8,128)S(1)}, u32[]{:S(2)}, u32[]{:S(2)}) collective-permute-start(f32[8,96]{1,0:T(8,128)S(1)} %get-tuple-element.119), channel_id=1, source_target_pairs={{0,3},{1,0},{2,1},{3,2},{4,7},{5,4},{6,5},{7,6},{8,11},{9,8},{10,9... | collective-permute-start | bytes 9224 | tf_op jit(solution)/shard_map/ppermute | solution.py:334
  199.4 4.5 %collective-permute-start.34 = (f32[8,96]{1,0:T(8,128)S(1)}, f32[8,96]{1,0:T(8,128)S(1)}, u32[]{:S(2)}, u32[]{:S(2)}) collective-permute-start(f32[8,96]{1,0:T(8,128)S(1)} %get-tuple-element.120), channel_id=1, source_target_pairs={{0,2},{1,3},{2,0},{3,1},{4,6},{5,7},{6,4},{7,5},{8,10},{9,11},{10,... | collective-permute-start | bytes 9224 | tf_op jit(solution)/shard_map/ppermute | solution.py:334
  200.7 5.7 %collective-permute-start.35 = (f32[8,96]{1,0:T(8,128)S(1)}, f32[8,96]{1,0:T(8,128)S(1)}, u32[]{:S(2)}, u32[]{:S(2)}) collective-permute-start(f32[8,96]{1,0:T(8,128)S(1)} %get-tuple-element.121), channel_id=1, source_target_pairs={{0,1},{1,2},{2,3},{3,0},{4,5},{5,6},{6,7},{7,4},{8,9},{9,10},{10,1... | collective-permute-start | bytes 9224 | tf_op jit(solution)/shard_map/ppermute | solution.py:334
  206.4 17.7 %copy-start.15 = (bf16[2,128,512]{2,1,0:T(8,128)(2,1)S(1)}, bf16[2,128,512]{2,1,0:T(8,128)(2,1)}, u32[]{:S(2)}) copy-start(bf16[2,128,512]{2,1,0:T(8,128)(2,1)} %tokens.3) | copy-start | bytes 786436
  206.4 5.5 %collective-permute-start.36 = (f32[4,8,96]{2,1,0:T(8,128)S(1)}, f32[4,8,96]{2,1,0:T(8,128)S(1)}, u32[]{:S(2)}, u32[]{:S(2)}) collective-permute-start(f32[4,8,96]{2,1,0:T(8,128)S(1)} %pad_maximum_fusion.8), channel_id=1, source_target_pairs={{0,4},{4,0},{8,12},{12,8},{16,20},{20,16},{24,28},{28,24},{1,5},{5... | collective-permute-start | bytes 36872 | tf_op jit(solution)/shard_map/ppermute | solution.py:331
  209.8 24.9 %collective-permute-start.16 = (bf16[1,384,512]{2,1,0:T(8,128)(2,1)S(1)}, bf16[1,384,512]{2,1,0:T(8,128)(2,1)S(1)}, u32[]{:S(2)}, u32[]{:S(2)}) collective-permute-start(bf16[1,384,512]{2,1,0:T(8,128)(2,1)S(1)} %get-tuple-element.70), channel_id=1, source_target_pairs={{0,8},{4,12},{8,0},{12,4},{16,24},{20,28},{24,16},{28,20},{1,9},{5... | collective-permute-start | bytes 1179656 | tf_op jit(solution)/shard_map/ppermute | solution.py:331
  210.5 30.8 %copy-start.6 = (bf16[768,1024]{1,0:T(8,128)(2,1)S(1)}, bf16[768,1024]{1,0:T(8,128)(2,1)}, u32[]{:S(2)}) copy-start(bf16[768,1024]{1,0:T(8,128)(2,1)} %get-tuple-element.86.gate_g.right) | copy-start | bytes 4718596
  210.7 24.0 %collective-permute-start.18 = (bf16[1,384,512]{2,1,0:T(8,128)(2,1)S(1)}, bf16[1,384,512]{2,1,0:T(8,128)(2,1)S(1)}, u32[]{:S(2)}, u32[]{:S(2)}) collective-permute-start(bf16[1,384,512]{2,1,0:T(8,128)(2,1)S(1)} %get-tuple-element.74), channel_id=1, source_target_pairs={{0,16},{4,20},{8,24},{12,28},{16,0},{20,4},{24,8},{28,12},{1,17},{... | collective-permute-start | bytes 1179656 | tf_op jit(solution)/shard_map/ppermute | solution.py:331
  212.0 8.4 %collective-permute-start.37 = (f32[4,8,96]{2,1,0:T(8,128)S(1)}, f32[4,8,96]{2,1,0:T(8,128)S(1)}, u32[]{:S(2)}, u32[]{:S(2)}) collective-permute-start(f32[4,8,96]{2,1,0:T(8,128)S(1)} %fusion.5), channel_id=1, source_target_pairs={{0,8},{4,12},{8,0},{12,4},{16,24},{20,28},{24,16},{28,20},{1,9},{5... | collective-permute-start | bytes 36872 | tf_op jit(solution)/shard_map/ppermute | solution.py:331
  220.4 3.7 %collective-permute-start.38 = (f32[4,8,96]{2,1,0:T(8,128)S(1)}, f32[4,8,96]{2,1,0:T(8,128)S(1)}, u32[]{:S(2)}, u32[]{:S(2)}) collective-permute-start(f32[4,8,96]{2,1,0:T(8,128)S(1)} %fusion.14), channel_id=1, source_target_pairs={{0,16},{4,20},{8,24},{12,28},{16,0},{20,4},{24,8},{28,12},{1,17},{... | collective-permute-start | bytes 36872 | tf_op jit(solution)/shard_map/ppermute | solution.py:331
  225.2 6.6 %collective-permute-start.47 = (f32[8,512]{1,0:T(8,128)S(1)}, f32[8,512]{1,0:T(8,128)S(1)}, u32[]{:S(2)}, u32[]{:S(2)}) collective-permute-start(f32[8,512]{1,0:T(8,128)S(1)} %get-tuple-element.101), channel_id=1, source_target_pairs={{0,1},{1,0},{2,3},{3,2},{4,5},{5,4},{6,7},{7,6},{8,9},{9,8},{10,11... | collective-permute-start | bytes 49160 | tf_op jit(solution)/shard_map/ppermute | solution.py:533
  231.7 21.4 %collective-permute-start.48 = (f32[8,512]{1,0:T(8,128)S(1)}, f32[8,512]{1,0:T(8,128)S(1)}, u32[]{:S(2)}, u32[]{:S(2)}) collective-permute-start(f32[8,512]{1,0:T(8,128)S(1)} %add.32), channel_id=1, source_target_pairs={{0,2},{1,3},{2,0},{3,1},{4,6},{5,7},{6,4},{7,5},{8,10},{9,11},{10,... | collective-permute-start | bytes 49160 | tf_op jit(solution)/shard_map/ppermute | solution.py:533
  234.8 20.0 %collective-permute-start.19 = (bf16[2,96,512]{2,1,0:T(8,128)(2,1)S(1)}, bf16[2,96,512]{2,1,0:T(8,128)(2,1)S(1)}, u32[]{:S(2)}, u32[]{:S(2)}) collective-permute-start(bf16[2,96,512]{2,1,0:T(8,128)(2,1)S(1)} %get-tuple-element.76), channel_id=1, source_target_pairs={{0,3},{1,0},{2,1},{3,2},{4,7},{5,4},{6,5},{7,6},{8,11},{9,8},{10,9... | collective-permute-start | bytes 589832 | tf_op jit(solution)/shard_map/ppermute | solution.py:334
  239.3 15.5 %collective-permute-start.20 = (bf16[2,96,512]{2,1,0:T(8,128)(2,1)S(1)}, bf16[2,96,512]{2,1,0:T(8,128)(2,1)S(1)}, u32[]{:S(2)}, u32[]{:S(2)}) collective-permute-start(bf16[2,96,512]{2,1,0:T(8,128)(2,1)S(1)} %get-tuple-element.77), channel_id=1, source_target_pairs={{0,2},{1,3},{2,0},{3,1},{4,6},{5,7},{6,4},{7,5},{8,10},{9,11},{10,... | collective-permute-start | bytes 589832 | tf_op jit(solution)/shard_map/ppermute | solution.py:334
  241.3 15.1 %copy-start.2 = (bf16[768,1024]{1,0:T(8,128)(2,1)S(1)}, bf16[768,1024]{1,0:T(8,128)(2,1)}, u32[]{:S(2)}) copy-start(bf16[768,1024]{1,0:T(8,128)(2,1)} %copy-done.1) | copy-start | bytes 4718596
  241.3 13.5 %collective-permute-start.21 = (bf16[2,96,512]{2,1,0:T(8,128)(2,1)S(1)}, bf16[2,96,512]{2,1,0:T(8,128)(2,1)S(1)}, u32[]{:S(2)}, u32[]{:S(2)}) collective-permute-start(bf16[2,96,512]{2,1,0:T(8,128)(2,1)S(1)} %get-tuple-element.78), channel_id=1, source_target_pairs={{0,1},{1,2},{2,3},{3,0},{4,5},{5,6},{6,7},{7,4},{8,9},{9,10},{10,1... | collective-permute-start | bytes 589832 | tf_op jit(solution)/shard_map/ppermute | solution.py:334
  251.8 16.5 %collective-permute-start.40 = (bf16[2,384,512]{2,1,0:T(8,128)(2,1)S(1)}, bf16[2,384,512]{2,1,0:T(8,128)(2,1)S(1)}, u32[]{:S(2)}, u32[]{:S(2)}) collective-permute-start(bf16[2,384,512]{2,1,0:T(8,128)(2,1)S(1)} %get-tuple-element.89), channel_id=1, source_target_pairs={{0,16},{4,20},{8,24},{12,28},{16,0},{20,4},{24,8},{28,12},{1,17},{... | collective-permute-start | bytes 2359304 | tf_op jit(solution)/shard_map/ppermute | solution.py:331
  253.1 16.4 %collective-permute-start.42 = (bf16[2,384,512]{2,1,0:T(8,128)(2,1)S(1)}, bf16[2,384,512]{2,1,0:T(8,128)(2,1)S(1)}, u32[]{:S(2)}, u32[]{:S(2)}) collective-permute-start(bf16[2,384,512]{2,1,0:T(8,128)(2,1)S(1)} %get-tuple-element.93), channel_id=1, source_target_pairs={{0,8},{4,12},{8,0},{12,4},{16,24},{20,28},{24,16},{28,20},{1,9},{5... | collective-permute-start | bytes 2359304 | tf_op jit(solution)/shard_map/ppermute | solution.py:331
  268.5 14.1 %collective-permute-start.41 = (bf16[1,384,512]{2,1,0:T(8,128)(2,1)S(1)}, bf16[1,384,512]{2,1,0:T(8,128)(2,1)S(1)}, u32[]{:S(2)}, u32[]{:S(2)}) collective-permute-start(bf16[1,384,512]{2,1,0:T(8,128)(2,1)S(1)} %get-tuple-element.91), channel_id=1, source_target_pairs={{0,8},{4,12},{8,0},{12,4},{16,24},{20,28},{24,16},{28,20},{1,9},{5... | collective-permute-start | bytes 1179656 | tf_op jit(solution)/shard_map/ppermute | solution.py:331
  269.7 12.8 %collective-permute-start.43 = (bf16[1,384,512]{2,1,0:T(8,128)(2,1)S(1)}, bf16[1,384,512]{2,1,0:T(8,128)(2,1)S(1)}, u32[]{:S(2)}, u32[]{:S(2)}) collective-permute-start(bf16[1,384,512]{2,1,0:T(8,128)(2,1)S(1)} %get-tuple-element.95), channel_id=1, source_target_pairs={{0,16},{4,20},{8,24},{12,28},{16,0},{20,4},{24,8},{28,12},{1,17},{... | collective-permute-start | bytes 1179656 | tf_op jit(solution)/shard_map/ppermute | solution.py:331
  282.6 4.6 %copy-start.4 = (bf16[768,1024]{1,0:T(8,128)(2,1)S(1)}, bf16[768,1024]{1,0:T(8,128)(2,1)}, u32[]{:S(2)}) copy-start(bf16[768,1024]{1,0:T(8,128)(2,1)} %get-tuple-element.87.up_g.right) | copy-start | bytes 4718596
  282.8 16.4 %collective-permute-start.44 = (bf16[2,96,512]{2,1,0:T(8,128)(2,1)S(1)}, bf16[2,96,512]{2,1,0:T(8,128)(2,1)S(1)}, u32[]{:S(2)}, u32[]{:S(2)}) collective-permute-start(bf16[2,96,512]{2,1,0:T(8,128)(2,1)S(1)} %get-tuple-element.97), channel_id=1, source_target_pairs={{0,3},{1,0},{2,1},{3,2},{4,7},{5,4},{6,5},{7,6},{8,11},{9,8},{10,9... | collective-permute-start | bytes 589832 | tf_op jit(solution)/shard_map/ppermute | solution.py:334
  286.5 12.6 %collective-permute-start.45 = (bf16[2,96,512]{2,1,0:T(8,128)(2,1)S(1)}, bf16[2,96,512]{2,1,0:T(8,128)(2,1)S(1)}, u32[]{:S(2)}, u32[]{:S(2)}) collective-permute-start(bf16[2,96,512]{2,1,0:T(8,128)(2,1)S(1)} %get-tuple-element.98), channel_id=1, source_target_pairs={{0,2},{1,3},{2,0},{3,1},{4,6},{5,7},{6,4},{7,5},{8,10},{9,11},{10,... | collective-permute-start | bytes 589832 | tf_op jit(solution)/shard_map/ppermute | solution.py:334
  286.5 12.7 %copy-start.12 = (bf16[512,4]{0,1:T(4,128)(2,1)S(1)}, bf16[512,4]{0,1:T(4,128)(2,1)}, u32[]{:S(2)}) copy-start(bf16[512,4]{0,1:T(4,128)(2,1)} %param.9) | copy-start | bytes 12292
  286.5 12.6 %collective-permute-start.46 = (bf16[2,96,512]{2,1,0:T(8,128)(2,1)S(1)}, bf16[2,96,512]{2,1,0:T(8,128)(2,1)S(1)}, u32[]{:S(2)}, u32[]{:S(2)}) collective-permute-start(bf16[2,96,512]{2,1,0:T(8,128)(2,1)S(1)} %get-tuple-element.99), channel_id=1, source_target_pairs={{0,1},{1,2},{2,3},{3,0},{4,5},{5,6},{6,7},{7,4},{8,9},{9,10},{10,1... | collective-permute-start | bytes 589832 | tf_op jit(solution)/shard_map/ppermute | solution.py:334
  (6 other events, 5.0 us)

commit v2 on v1

--- a/solution.py
+++ b/solution.py
@@ -1,3 +1,4 @@
+import contextlib
 import functools
 
 import jax
@@ -31,7 +32,7 @@
     )
 
 
-def call(kernel, grid, scalars, ins, outs, scratch=(), alias=None, flops=0, vmem=48):
+def call(kernel, grid, scalars, ins, outs, scratch=(), alias=None, flops=0, vmem=20):
     return pallas(kernel, grid, scalars, ins, outs, scratch, alias, flops, vmem)
 
 
@@ -138,25 +139,34 @@
 
 def assemble(rank, pieces, plan, out):
     slots, width = pieces[0].shape[1:]
-    for piece, (step, numbers) in zip(pieces, plan):
-        for i, k in enumerate(numbers):
+    for piece, entries in zip(pieces, plan):
+        for i, (step, k) in enumerate(entries):
             at = pl.multiple_of(jnp.bitwise_xor(rank, k) * width, 128)
             out[step * slots : (step + 1) * slots, pl.ds(at, width)] = piece[i]
 
 
-def pre_kernel(rank, *refs, plan):
-    pieces = refs[: len(plan)]
-    gate_w, up_w, _, rows, hidden, pre_gate, pre_up = refs[len(plan) :]
+@contextlib.contextmanager
+def keep_rows(rank, pieces, plan, rows, rows_out, sem):
+    copy = pltpu.make_async_copy(rows, rows_out, sem)
 
     @pl.when(pl.program_id(0) == 0)
     def _():
         assemble(rank[0], pieces, plan, rows)
-
-    pre_tile(rows, gate_w, up_w, hidden, pre_gate, pre_up)
-
-
-def pre_rest_kernel(rows, gate_w, up_w, _a, _b, _c, _d, hidden, pre_gate, pre_up):
-    pre_tile(rows, gate_w, up_w, hidden, pre_gate, pre_up)
+        copy.start()
+
+    yield
+
+    @pl.when(pl.program_id(0) == pl.num_programs(0) - 1)
+    def _():
+        copy.wait()
+
+
+def pre_kernel(rank, *refs, plan):
+    pieces = refs[: len(plan)]
+    gate_w, up_w, rows_out, hidden, pre_gate, pre_up, rows, sem = refs[len(plan) :]
+
+    with keep_rows(rank, pieces, plan, rows, rows_out, sem):
+        pre_tile(rows, gate_w, up_w, hidden, pre_gate, pre_up)
 
 
 def pre_tile(rows, gate_w, up_w, hidden, pre_gate, pre_up):
@@ -169,28 +179,30 @@
 
 def grad_kernel(rank, *refs, plan):
     pieces = refs[: len(plan)]
-    down_w, hidden, pre_gate, pre_up, _, rows, gate_grad, up_grad, dots, acc = refs[len(plan) :]
+    down_w, hidden, pre_gate, pre_up, _, rows_out, gate_grad, up_grad, dots, rows, acc, sem = refs[
+        len(plan) :
+    ]
     at = pl.program_id(0)
 
     @pl.when(at == 0)
     def _():
-        assemble(rank[0], pieces, plan, rows)
         acc[...] = jnp.zeros_like(acc)
 
-    grad = mm_nt(rows[...], down_w[...])
-    gate = pre_gate[...]
-    sig = jax.nn.sigmoid(gate)
-    gate_grad[...] = (grad * pre_up[...] * (sig * (1.0 + gate * (1.0 - sig)))).astype(BF)
-    up_grad[...] = (grad * (gate * sig)).astype(BF)
-    product = grad * hidden[...].astype(F32)
-    total = acc[...]
-    for i in range(product.shape[1] // 128):
-        total = total + product[:, 128 * i : 128 * (i + 1)]
-    acc[...] = total
-
-    @pl.when(at == pl.num_programs(0) - 1)
-    def _():
-        dots[...] = mm_nt(jnp.ones((8, 128), F32), acc[...], HI)
+    with keep_rows(rank, pieces, plan, rows, rows_out, sem):
+        grad = mm_nt(rows[...], down_w[...])
+        gate = pre_gate[...]
+        sig = jax.nn.sigmoid(gate)
+        gate_grad[...] = (grad * pre_up[...] * (sig * (1.0 + gate * (1.0 - sig)))).astype(BF)
+        up_grad[...] = (grad * (gate * sig)).astype(BF)
+        product = grad * hidden[...].astype(F32)
+        total = acc[...]
+        for i in range(product.shape[1] // 128):
+            total = total + product[:, 128 * i : 128 * (i + 1)]
+        acc[...] = total
+
+        @pl.when(at == pl.num_programs(0) - 1)
+        def _():
+            dots[...] = mm_nt(jnp.ones((8, 128), F32), acc[...], HI)
 
 
 def spread(total, plan, outs):
@@ -207,9 +219,10 @@
     out[...] = mm(hidden[...], down_w[...]).astype(BF)
 
 
-def out_keep_kernel(rank, hidden, down_w, recv, _, *outs, plan):
+def out_keep_kernel(rank, hidden, down_w, recv, _, *outs):
     total = (mm(hidden[...], down_w[...]) + recv[...].astype(F32)).astype(BF)
-    spread(total, plan, outs)
+    for i, out in enumerate(outs):
+        pl.when(pl.program_id(0) == i)(functools.partial(out.__setitem__, Ellipsis, total))
 
 
 def in_send_kernel(rank, gate_g, up_g, gate_w, up_w, _, out):
@@ -238,8 +251,28 @@
             out[step] = (kept + recv).astype(BF)
 
 
-def weight_kernel(left, right, _, out):
-    out[0] = mm_tn(left[...], right[...]).astype(BF)
+def sum_all_kernel(*refs):
+    outs = [ref for ref in refs if len(ref.shape) == 3]
+    terms = refs[: len(refs) - len(outs)]
+    micro, rows, _ = outs[0].shape
+    for step in range(micro):
+        for i, out in enumerate(outs):
+            at = (step * len(outs) + i) * rows
+            total = terms[0][at : at + rows, :].astype(F32)
+            for term in terms[1:]:
+                total = total + term[at : at + rows, :].astype(F32)
+            out[step] = total.astype(BF)
+
+
+def weight_in_kernel(rows, gate_g, up_g, *refs):
+    gate_out, up_out = refs[-2:]
+    left = rows[...]
+    gate_out[0] = mm_tn(left, gate_g[...]).astype(BF)
+    up_out[0] = mm_tn(left, up_g[...]).astype(BF)
+
+
+def weight_down_kernel(hidden, cots, _, out):
+    out[0] = mm_tn(hidden[...], cots[...]).astype(BF)
 
 
 def column_of(gates, tok_rows):
@@ -333,6 +366,9 @@
     def shift(value, turn):
         return lax.ppermute(value, "ep", [(i, (i + turn) % places) for i in range(places)])
 
+    def far(array):
+        return pltpu.with_memory_space_constraint(array, pltpu.HBM)
+
     def full(array):
         return (array, whole(array))
 
@@ -361,35 +397,49 @@
     chip_bits = [1 << i for i in range(1, ranks.bit_length() - 1)]
     order = [chip_bits[m % len(chip_bits) :] + chip_bits[: m % len(chip_bits)] for m in range(micro)]
 
-    def deliver(blocks):
-        got = [blocks[0]] + [shift(blocks[turn], turn) for turn in range(1, places)]
+    def dispatch(blocks):
+        got = [blocks[0]]
+        for turn in range(1, places):
+            got.append(shift(blocks[turn], turn))
+        return got
+
+    def to_partner(pieces, plan):
+        for i in range(len(pieces)):
+            pieces.append(swap(pieces[i], 1))
+            plan.append([(step, k ^ 1) for step, k in plan[i]])
+        return pieces, plan
+
+    def gather_by_steps(blocks):
+        got = dispatch(blocks)
         pieces, plan = [], []
         held, numbers = [], []
         for step in range(micro):
             held.append(jnp.concatenate([part[step : step + 1] for part in got], axis=1))
-            numbers.append([0])
+            numbers.append([(step, 0)])
         for stage in range(len(chip_bits)):
             for step in range(micro):
                 bit = order[step][stage]
                 recv = swap(held[step], bit)
-                there = [k ^ bit for k in numbers[step]]
+                there = [(step, k ^ bit) for _, k in numbers[step]]
                 if stage == len(chip_bits) - 1:
                     pieces += [held[step], recv]
-                    plan += [(step, numbers[step]), (step, there)]
+                    plan += [numbers[step], there]
                 else:
                     held[step] = jnp.concatenate([held[step], recv], axis=0)
                     numbers[step] = numbers[step] + there
-        for i in range(len(pieces)):
-            pieces.append(swap(pieces[i], 1))
-            plan.append((plan[i][0], [k ^ 1 for k in plan[i][1]]))
-        return pieces, plan
-
-    token_pieces, plan = deliver(packed)
-    cot_pieces, _ = deliver(cots)
-
-    tile = min(256, units // 2)
+        return to_partner(pieces, plan)
+
+    def gather_at_once(blocks):
+        own = jnp.concatenate(dispatch(blocks), axis=1)
+        pieces = [own] + [swap(own, 2 * k) for k in range(1, half)]
+        plan = [[(step, 2 * k) for step in range(micro)] for k in range(half)]
+        return to_partner(pieces, plan)
+
+    token_pieces, token_plan = gather_by_steps(packed)
+    cot_pieces, cot_plan = gather_at_once(cots)
+
+    tile = min(256, units)
     steps = units // tile
-    part = steps // 2
     all_rows = micro * slots_n
     work = 2 * all_rows * features * units
     columns = pl.BlockSpec((all_rows, tile), lambda i, *_: (0, i))
@@ -398,21 +448,13 @@
     wide_shape = shape((all_rows, units), F32)
 
     weight = pl.BlockSpec((features, tile), lambda i, *_: (0, i))
-    rows_in, *firsts = call(
-        functools.partial(pre_kernel, plan=plan), (part,), [rank],
-        [full(p) for p in token_pieces] + [(gate_w, weight), (up_w, weight), (cots[0], ANY)],
-        [full(rows_shape), (units_shape, columns)] + [(wide_shape, columns)] * 2,
-        flops=work,
-    )
-    weight = pl.BlockSpec((features, tile), lambda i: (0, i + part))
-    later = pl.BlockSpec((all_rows, tile), lambda i: (0, i + part))
-    hidden, pre_gate, pre_up = call(
-        pre_rest_kernel, (part,), [],
-        [full(rows_in), (gate_w, weight), (up_w, weight)]
-        + [(array, ANY) for array in firsts] + [(gates, ANY)],
-        [(units_shape, later)] + [(wide_shape, later)] * 2,
-        alias={3: 0, 4: 1, 5: 2},
-        flops=work,
+    rows_in, hidden, pre_gate, pre_up = call(
+        functools.partial(pre_kernel, plan=token_plan), (steps,), [rank],
+        [full(p) for p in token_pieces] + [(far(gate_w), weight), (far(up_w), weight)],
+        [(rows_shape, ANY), (units_shape, columns)] + [(wide_shape, columns)] * 2,
+        scratch=[pltpu.VMEM((all_rows, features), BF), pltpu.SemaphoreType.DMA],
+        flops=2 * work,
+        vmem=36,
     )
     sent = shape((half, all_rows, width), BF)
     kept = shape((half // 2, slots_n, width), BF)
@@ -453,61 +495,73 @@
             functools.partial(sum_kernel, micro=micro), (1,), [],
             [full(part) for part in parts], [full(block)] * places, flops=10**7,
         )
+        return send_home(blocks)
+
+    def send_home(blocks):
         return [blocks[0]] + [shift(blocks[turn], -turn) for turn in range(1, places)]
 
     (out_sent,) = call(
         out_send_kernel, (half,), [rank],
-        [full(hidden), (down_w, wide(1)), (hidden, ANY)], [(sent, by_step)], flops=work // 2,
+        [full(hidden), (far(down_w), wide(1)), (hidden, ANY)], [(sent, by_step)], flops=work // 2,
     )
     out_parts = call(
-        functools.partial(out_keep_kernel, plan=homes), (half,), [rank],
-        [full(hidden), (down_w, wide(0)), (swap(out_sent, 1), by_step), (hidden, ANY)],
-        [full(kept)] * (2 * micro), flops=work // 2,
-    )
-    out_blocks = reduce(out_parts)
+        out_keep_kernel, (half,), [rank],
+        [full(hidden), (far(down_w), wide(0)), (swap(out_sent, 1), by_step), (hidden, ANY)],
+        [full(shape((all_rows, width), BF))] * half, flops=work // 2,
+    )
+    out_terms = [out_parts[0]] + [swap(out_parts[k], 2 * k) for k in range(1, half)]
+    out_blocks = send_home(
+        call(sum_all_kernel, (1,), [], [full(t) for t in out_terms], [full(block)] * places, flops=10**7)
+    )
 
     weight = pl.BlockSpec((tile, features), lambda i, *_: (i, 0))
     rows_cot, gate_g, up_g, dots = call(
-        functools.partial(grad_kernel, plan=plan), (steps,), [rank],
+        functools.partial(grad_kernel, plan=cot_plan), (steps,), [rank],
         [full(p) for p in cot_pieces]
-        + [(down_w, weight), (hidden, columns), (pre_gate, columns), (pre_up, columns)]
+        + [(far(down_w), weight), (hidden, columns), (pre_gate, columns), (pre_up, columns)]
         + [(out_parts[0], ANY)],
-        [full(rows_shape), (units_shape, columns), (units_shape, columns)]
+        [(rows_shape, ANY), (units_shape, columns), (units_shape, columns)]
         + [full(shape((8, all_rows), F32))],
-        scratch=[pltpu.VMEM((all_rows, 128), F32)],
+        scratch=[pltpu.VMEM((all_rows, features), BF), pltpu.VMEM((all_rows, 128), F32), pltpu.SemaphoreType.DMA],
         flops=work,
+        vmem=36,
     )
     (in_sent,) = call(
         in_send_kernel, (half,), [rank],
-        [full(gate_g), full(up_g), (gate_w, tall(1)), (up_w, tall(1)), (dots, ANY)],
+        [full(gate_g), full(up_g), (far(gate_w), tall(1)), (far(up_w), tall(1)), (dots, ANY)],
         [(sent, by_step)], flops=work,
     )
     in_parts = call(
         functools.partial(in_keep_kernel, plan=homes), (half,), [rank],
-        [full(gate_g), full(up_g), (gate_w, tall(0)), (up_w, tall(0))]
+        [full(gate_g), full(up_g), (far(gate_w), tall(0)), (far(up_w), tall(0))]
         + [(swap(in_sent, 1), by_step), (in_sent, ANY)],
-        [full(kept)] * (2 * micro), flops=work,
+        [full(kept)] * (2 * micro), flops=work, vmem=26,
     )
     in_blocks = reduce(in_parts)
     span = min(512, features)
     rows_span = pl.BlockSpec((all_rows, span), lambda i: (0, i))
+    part = features // span // 2
+    grads = [in_parts[0]]
+    for base in (0, part):
+        weight_spec = pl.BlockSpec((1, span, units), lambda i, base=base: (0, i + base, 0))
+        rows_part = pl.BlockSpec((all_rows, span), lambda i, base=base: (0, i + base))
+        grads = call(
+            weight_in_kernel, (part,), [],
+            [(far(rows_in), rows_part), full(gate_g), full(up_g)] + [(far(g) if base else g, ANY) for g in grads],
+            [(pltpu.HBM((1, features, units), BF), weight_spec)] * 2,
+            alias={3: 0, 4: 1} if base else None,
+            flops=work,
+        )
+    gate_grad, up_grad = grads
+    span = min(1024, features)
+    rows_span = pl.BlockSpec((all_rows, span), lambda i: (0, i))
     down_spec = pl.BlockSpec((1, units, span), lambda i: (0, 0, i))
     (down_grad,) = call(
-        weight_kernel, (features // span,), [],
-        [full(hidden), (rows_cot, rows_span), (in_parts[0], ANY)],
-        [(shape((1, units, features), BF), down_spec)],
+        weight_down_kernel, (features // span,), [],
+        [full(hidden), (far(rows_cot), rows_span), (dots, ANY)],
+        [(pltpu.HBM((1, units, features), BF), down_spec)],
         flops=work,
     )
-    last, grads = down_grad, []
-    for g in (gate_g, up_g):
-        (last,) = call(
-            weight_kernel, (features // span,), [],
-            [(rows_in, rows_span), full(g), (last, ANY)],
-            [(shape((1, features, units), BF), pl.BlockSpec((1, span, units), lambda i: (0, i, 0)))],
-            flops=work,
-        )
-        grads.append(last)
-    gate_grad, up_grad = grads
 
     scaled = dots[0].reshape(micro, places, capacity)
     scaled = jnp.pad(scaled, ((0, 8 - micro), (0, 0), (0, 0)))

time: 302 us -> 286 us (0.947)
  Pallas kernels: 117 us -> 96.6 us
  waiting for transfers between devices: 100 us -> 118 us
  starting transfers between devices: 66.8 us -> 58.4 us
  local copies, waits for them, and re-layouts: 14.7 us -> 10.7 us
    pallas_call x21 -> x18, Pallas kernels: 117 us -> 96.6 us  [pallas(): pl.pallas_call(kernel, grid_spec=pltpu.PrefetchScalarGridSpec(num_scalar_...]
    ppermute x15, waiting for transfers between devices: 29.3 us -> 39.3 us  [shift(): lax.ppermute(value, 'ep', [(i, (i + turn) % places) for i in range(places)])]
    ppermute x32 -> x30, waiting for transfers between devices: 69.2 us -> 78.3 us  [swap(): return lax.ppermute(value, 'rep', [(i, i ^ bits) for i in range(ranks)])]
    ppermute x2, starting transfers between devices: 7.77 us -> 3.43 us  [layer(): lax.ppermute(router_grad, 'ep', [(i, i ^ bits) for i in range(places)])]
    unnamed x42 -> x39, local copies, waits for them, and re-layouts: 14.5 us -> 10.5 us
    ppermute x15, starting transfers between devices: 32.7 us -> 29.2 us  [shift(): lax.ppermute(value, 'ep', [(i, (i + turn) % places) for i in range(places)])]
    ppermute x32 -> x30, starting transfers between devices: 26.3 us -> 25.7 us  [swap(): return lax.ppermute(value, 'rep', [(i, i ^ bits) for i in range(ranks)])]
  transfers between devices with their start and end apart: 49 -> 47, of which waited for: 21 -> 23; matrix products, arithmetic and copies ran while one was open for 0% -> 0% of each run, Pallas kernels for 19% -> 17%
where the time goes in v2:
time: 286 us; the launch traced here: 285 us
  waiting for transfers between devices  118 us (41%)
  Pallas kernels  96.6 us (34%)
  starting transfers between devices  58.4 us (20%)
  local copies, waits for them, and re-layouts  10.7 us (4%)
    pallas_call x18, Pallas kernels, pallas(): pl.pallas_call(kernel, grid_spec=pltpu.PrefetchScalarGridSpec(num_scalar_...  96.6 us
    ppermute x30, waiting for transfers between devices, swap(): return lax.ppermute(value, 'rep', [(i, i ^ bits) for i in range(ranks)])  78.3 us
    ppermute x15, waiting for transfers between devices, shift(): lax.ppermute(value, 'ep', [(i, (i + turn) % places) for i in range(places)])  39.3 us
    ppermute x15, starting transfers between devices, shift(): lax.ppermute(value, 'ep', [(i, (i + turn) % places) for i in range(places)])  29.2 us
    ppermute x30, starting transfers between devices, swap(): return lax.ppermute(value, 'rep', [(i, i ^ bits) for i in range(ranks)])  25.7 us
    unnamed x39, local copies, waits for them, and re-layouts  10.5 us
  transfers between devices with their start and end apart: 47, of which 23 were waited for; matrix products, arithmetic and copies ran while one was open for 0% of the time, Pallas kernels for 17%

profile of v2, /device:TPU:0, one launch (start us, length us, event | category | flops | bytes accessed | tf_op | source)
XLA Modules:
  0.0 285.5 jit_solution(10198900543737541766)
XLA Ops:
  1.3 0.9 copy-done.14
  3.5 5.1 %collective-permute-start.5 = (bf16[2,96,512]{2,1,0:T(8,128)(2,1)S(1)}, bf16[2,96,512]{2,1,0:T(8,128)(2,1)S(1)}, u32[]{:S(2)}, u32[]{:S(2)}) collective-permute-start(bf16[2,96,512]{2,1,0:T(8,128)(2,1)S(1)} %get-tuple-element.57), channel_id=1, source_target_pairs={{0,3},{1,0},{2,1},{3,2},{4,7},{5,4},{6,5},{7,6},{8,11},{9,8},{10,9... | collective-permute-start | bytes 589832 | tf_op jit(solution)/shard_map/ppermute | solution.py:367
  8.6 1.0 collective-permute-start.3
  9.7 4.3 %collective-permute-done.5 = bf16[2,96,512]{2,1,0:T(8,128)(2,1)S(1)} collective-permute-done((bf16[2,96,512]{2,1,0:T(8,128)(2,1)S(1)}, bf16[2,96,512]{2,1,0:T(8,128)(2,1)S(1)}, u32[]{:S(2)}, u32[]{:S(2)}) %collective-permute-start.5) | collective-permute-done | bytes 196640 | tf_op jit(solution)/shard_map/ppermute | solution.py:367
  14.0 11.3 %collective-permute-done.4 = bf16[2,96,512]{2,1,0:T(8,128)(2,1)S(1)} collective-permute-done((bf16[2,96,512]{2,1,0:T(8,128)(2,1)S(1)}, bf16[2,96,512]{2,1,0:T(8,128)(2,1)S(1)}, u32[]{:S(2)}, u32[]{:S(2)}) %collective-permute-start.4) | collective-permute-done | bytes 196640 | tf_op jit(solution)/shard_map/ppermute | solution.py:367
  25.4 1.6 collective-permute-start.6
  27.0 1.6 collective-permute-start.8
  28.6 7.0 %collective-permute-done.6 = bf16[1,384,512]{2,1,0:T(8,128)(2,1)S(1)} collective-permute-done((bf16[1,384,512]{2,1,0:T(8,128)(2,1)S(1)}, bf16[1,384,512]{2,1,0:T(8,128)(2,1)S(1)}, u32[]{:S(2)}, u32[]{:S(2)}) %collective-permute-start.6) | collective-permute-done | bytes 393248 | tf_op jit(solution)/shard_map/ppermute | solution.py:364
  35.7 1.6 collective-permute-start.7
  37.3 1.6 collective-permute-start.9
  39.4 14.4 %collective-permute-done.7.refs_1_ = bf16[2,384,512]{2,1,0:T(8,128)(2,1)S(1)} collective-permute-done((bf16[2,384,512]{2,1,0:T(8,128)(2,1)S(1)}, bf16[2,384,512]{2,1,0:T(8,128)(2,1)S(1)}, u32[]{:S(2)}, u32[]{:S(2)}) %collective-permute-start.7) | collective-permute-done | bytes 786464 | tf_op jit(solution)/shard_map/ppermute | solution.py:364
  56.2 1.1 collective-permute-done.13.refs_7_
  57.3 1.1 copy-done.10
  58.4 1.1 copy-done.12
  59.6 18.2 %shard_map.120 = (bf16[768,4096]{1,0:T(8,128)(2,1)}, bf16[768,1024]{1,0:T(8,128)(2,1)S(1)}, f32[768,1024]{1,0:T(8,128)S(1)}, f32[768,1024]{1,0:T(8,128)S(1)}) custom-call(s32[1]{0:T(128)} %bitcast.5.rank, bf16[2,384,512]{2,1,0:T(8,128)(2,1)S(1)} %pad_maximum_fusion.refs_0_, bf16[2,384,512]{2,1,0:T(8,128)(2,1)S(1)} %copy-done.10, ...), custom_call_target="tpu_custom_call" | custom-call | flops 12884901888 | bytes 12884901 | tf_op jit(solution)/shard_map/pallas_call | solution.py:40
  77.8 5.5 %shard_map.121 = bf16[4,768,512]{2,1,0:T(8,128)(2,1)S(1)} custom-call(s32[1]{0:T(128)} %bitcast.5.rank, bf16[768,1024]{1,0:T(8,128)(2,1)S(1)} %get-tuple-element.58.hidden._.refs_9_, bf16[1024,4096]{1,0:T(8,128)(2,1)} %bitcast.27, bf16[768,1024]{1,0:T(8,128)(2,1)S(1)} %get-tuple-element.58.hidden._.refs_9_), custom_call_target="tpu_custom_call" | custom-call | flops 3221225472 | bytes 3221225 | tf_op jit(solution)/shard_map/pallas_call | solution.py:40
  83.9 5.2 %collective-permute-done = f32[8,128]{1,0:T(8,128)S(1)} collective-permute-done((f32[8,128]{1,0:T(8,128)S(1)}, f32[8,128]{1,0:T(8,128)S(1)}, u32[]{:S(2)}, u32[]{:S(2)}) %collective-permute-start) | collective-permute-done | bytes 4128 | tf_op jit(solution)/shard_map/ppermute | solution.py:364
  89.0 1.4 collective-permute-start.1
  90.4 2.2 collective-permute-done.1
  92.6 1.5 collective-permute-start.2
  94.2 2.1 collective-permute-done.2
  96.6 1.1 collective-permute-start.21
  97.8 2.0 collective-permute-start.22
  99.8 2.8 collective-permute-start.23
  102.6 3.7 %collective-permute-done.21 = bf16[2,96,512]{2,1,0:T(8,128)(2,1)S(1)} collective-permute-done((bf16[2,96,512]{2,1,0:T(8,128)(2,1)S(1)}, bf16[2,96,512]{2,1,0:T(8,128)(2,1)S(1)}, u32[]{:S(2)}, u32[]{:S(2)}) %collective-permute-start.21) | collective-permute-done | bytes 196640 | tf_op jit(solution)/shard_map/ppermute | solution.py:367
  106.3 5.5 %collective-permute-done.22 = bf16[2,96,512]{2,1,0:T(8,128)(2,1)S(1)} collective-permute-done((bf16[2,96,512]{2,1,0:T(8,128)(2,1)S(1)}, bf16[2,96,512]{2,1,0:T(8,128)(2,1)S(1)}, u32[]{:S(2)}, u32[]{:S(2)}) %collective-permute-start.22) | collective-permute-done | bytes 196640 | tf_op jit(solution)/shard_map/ppermute | solution.py:367
  111.9 1.3 collective-permute-start.24
  113.2 1.4 collective-permute-start.25
  115.4 16.9 %collective-permute-done.24.refs_1_ = bf16[2,384,512]{2,1,0:T(8,128)(2,1)S(1)} collective-permute-done((bf16[2,384,512]{2,1,0:T(8,128)(2,1)S(1)}, bf16[2,384,512]{2,1,0:T(8,128)(2,1)S(1)}, u32[]{:S(2)}, u32[]{:S(2)}) %collective-permute-start.24) | collective-permute-done | bytes 786464 | tf_op jit(solution)/shard_map/ppermute | solution.py:364
  132.4 16.8 %collective-permute-done.25.refs_2_ = bf16[2,384,512]{2,1,0:T(8,128)(2,1)S(1)} collective-permute-done((bf16[2,384,512]{2,1,0:T(8,128)(2,1)S(1)}, bf16[2,384,512]{2,1,0:T(8,128)(2,1)S(1)}, u32[]{:S(2)}, u32[]{:S(2)}) %collective-permute-start.25) | collective-permute-done | bytes 786464 | tf_op jit(solution)/shard_map/ppermute | solution.py:364
  149.6 5.7 %shard_map.122 = (bf16[768,512]{1,0:T(8,128)(2,1)S(1)}, bf16[768,512]{1,0:T(8,128)(2,1)S(1)}, bf16[768,512]{1,0:T(8,128)(2,1)S(1)}, bf16[768,512]{1,0:T(8,128)(2,1)S(1)}) custom-call(s32[1]{0:T(128)} %bitcast.5.rank, bf16[768,1024]{1,0:T(8,128)(2,1)S(1)} %get-tuple-element.58.hidden._.refs_9_, bf16[1024,4096]{1,0:T(8,128)(2,1)} %bitcast.28, ...), custom_call_target="tpu_custom_call" | custom-call | flops 3221225472 | bytes 3221225 | tf_op jit(solution)/shard_map/pallas_call | solution.py:40
  158.1 11.5 %shard_map.125 = (bf16[768,4096]{1,0:T(8,128)(2,1)}, bf16[768,1024]{1,0:T(8,128)(2,1)S(1)}, bf16[768,1024]{1,0:T(8,128)(2,1)S(1)}, f32[8,768]{1,0:T(8,128)S(1)}) custom-call(s32[1]{0:T(128)} %bitcast.5.rank, bf16[2,384,512]{2,1,0:T(8,128)(2,1)S(1)} %constant_dynamic-update-slice_fusion.refs_0_, bf16[2,384,512]{2,1,0:T(8,128)(2,1)S(1)} %collective-permute-done.24.refs_1_, ...), custom_call_target="tpu_custom_call" | custom-call | flops 6442450944 | bytes 6442450 | tf_op jit(solution)/shard_map/pallas_call | solution.py:40
  169.7 10.5 %shard_map.127._ = bf16[4,768,512]{2,1,0:T(8,128)(2,1)} custom-call(s32[1]{0:T(128)} %bitcast.5.rank, bf16[768,1024]{1,0:T(8,128)(2,1)S(1)} %get-tuple-element.75.gate_g, bf16[768,1024]{1,0:T(8,128)(2,1)S(1)} %get-tuple-element.76.up_g, bf16[4096,1024]{1,0:T(8,128)(2,1)} %bitcast.31, bf16[4096,1024]{1,0:T(8,128)(2,1)} %bitcast.34, ...), custom_call_target="tpu_custom_call" | custom-call | flops 6442450944 | bytes 6442450 | tf_op jit(solution)/shard_map/pallas_call | solution.py:40
  180.3 4.8 %collective-permute-start.33 = (f32[8,96]{1,0:T(8,128)S(1)}, f32[8,96]{1,0:T(8,128)S(1)}, u32[]{:S(2)}, u32[]{:S(2)}) collective-permute-start(f32[8,96]{1,0:T(8,128)S(1)} %get-tuple-element.107), channel_id=1, source_target_pairs={{0,1},{1,2},{2,3},{3,0},{4,5},{5,6},{6,7},{7,4},{8,9},{9,10},{10,1... | collective-permute-start | bytes 9224 | tf_op jit(solution)/shard_map/ppermute | solution.py:367
  185.8 1.7 collective-permute-start.31
  187.6 2.1 collective-permute-done.32
  189.7 1.2 collective-permute-done.34
  190.9 1.1 collective-permute-start.35
  192.9 1.7 collective-permute-done.35
  194.6 1.6 collective-permute-start.36
  196.3 2.1 collective-permute-done.36
  198.4 1.0 shard_map.126
  200.0 1.6 collective-permute-start.16
  201.6 1.1 collective-permute-start.17
  203.2 2.9 %collective-permute-start.46 = (f32[8,512]{1,0:T(8,128)S(1)}, f32[8,512]{1,0:T(8,128)S(1)}, u32[]{:S(2)}, u32[]{:S(2)}) collective-permute-start(f32[8,512]{1,0:T(8,128)S(1)} %add.32), channel_id=1, source_target_pairs={{0,2},{1,3},{2,0},{3,1},{4,6},{5,7},{6,4},{7,5},{8,10},{9,11},{10,... | collective-permute-start | bytes 49160 | tf_op jit(solution)/shard_map/ppermute | solution.py:587
  206.1 1.4 copy-done.1
  207.5 9.6 %shard_map.128 = (bf16[2,384,512]{2,1,0:T(8,128)(2,1)S(1)}, bf16[2,384,512]{2,1,0:T(8,128)(2,1)S(1)}, bf16[2,384,512]{2,1,0:T(8,128)(2,1)S(1)}, bf16[2,384,512]{2,1,0:T(8,128)(2,1)S(1)}) custom-call(s32[1]{0:T(128)} %bitcast.5.rank, bf16[768,1024]{1,0:T(8,128)(2,1)S(1)} %get-tuple-element.75.gate_g, bf16[768,1024]{1,0:T(8,128)(2,1)S(1)} %copy-done.1, ...), custom_call_target="tpu_custom_call" | custom-call | flops 6442450944 | bytes 6442450 | tf_op jit(solution)/shard_map/pallas_call | solution.py:40
  218.0 1.6 collective-permute-start.40
  219.5 10.6 %shard_map.135 = bf16[1,1024,4096]{2,1,0:T(8,128)(2,1)} custom-call(bf16[768,1024]{1,0:T(8,128)(2,1)S(1)} %get-tuple-element.58.hidden._.refs_9_, bf16[768,4096]{1,0:T(8,128)(2,1)} %get-tuple-element.94.cots, f32[8,768]{1,0:T(8,128)S(1)} %get-tuple-element.73._), custom_call_target="tpu_custom_call" | custom-call | flops 6442450944 | bytes 6442450 | tf_op jit(solution)/shard_map/pallas_call | solution.py:40
  230.1 7.3 %collective-permute-done.16.refs_2_ = bf16[768,512]{1,0:T(8,128)(2,1)S(1)} collective-permute-done((bf16[768,512]{1,0:T(8,128)(2,1)}, bf16[768,512]{1,0:T(8,128)(2,1)S(1)}, u32[]{:S(2)}, u32[]{:S(2)}) %collective-permute-start.16) | collective-permute-done | bytes 786464 | tf_op jit(solution)/shard_map/ppermute | solution.py:364
  237.8 2.9 %collective-permute-start.18 = (bf16[2,96,512]{2,1,0:T(8,128)(2,1)S(1)}, bf16[2,96,512]{2,1,0:T(8,128)(2,1)S(1)}, u32[]{:S(2)}, u32[]{:S(2)}) collective-permute-start(bf16[2,96,512]{2,1,0:T(8,128)(2,1)S(1)} %get-tuple-element.64), channel_id=1, source_target_pairs={{0,3},{1,0},{2,1},{3,2},{4,7},{5,4},{6,5},{7,6},{8,11},{9,8},{10,9... | collective-permute-start | bytes 589832 | tf_op jit(solution)/shard_map/ppermute | solution.py:367
  241.3 1.9 collective-permute-start.20
  243.8 2.8 collective-permute-done.18.refs_1_
  246.7 6.4 %collective-permute-done.19.refs_2_ = bf16[2,96,512]{2,1,0:T(8,128)(2,1)S(1)} collective-permute-done((bf16[2,96,512]{2,1,0:T(8,128)(2,1)S(1)}, bf16[2,96,512]{2,1,0:T(8,128)(2,1)S(1)}, u32[]{:S(2)}, u32[]{:S(2)}) %collective-permute-start.19) | collective-permute-done | bytes 196640 | tf_op jit(solution)/shard_map/ppermute | solution.py:367
  253.0 1.5 shard_map.124
  254.7 1.0 collective-permute-start.39
  255.9 1.1 collective-permute-start.41
  257.1 9.5 %shard_map.133 = (bf16[1,4096,1024]{2,1,0:T(8,128)(2,1)}, bf16[1,4096,1024]{2,1,0:T(8,128)(2,1)}) custom-call(bf16[768,4096]{1,0:T(8,128)(2,1)} %get-tuple-element.89.rows, bf16[768,1024]{1,0:T(8,128)(2,1)S(1)} %get-tuple-element.75.gate_g, bf16[768,1024]{1,0:T(8,128)(2,1)S(1)} %copy-done.1, bf16[2,384,512]{2,1,0:T(8,128)(2,1)S(1)} %get-tuple-element.77.kept.refs_0_), custom_call_target="tpu_custom_call" | custom-call | flops 6442450944 | bytes 6442450 | tf_op jit(solution)/shard_map/pallas_call | solution.py:40
  266.8 1.2 collective-permute-start.42
  268.0 1.3 collective-permute-start.43
  269.3 1.9 collective-permute-start.44
  271.2 9.5 %shard_map.134 = (bf16[1,4096,1024]{2,1,0:T(8,128)(2,1)}, bf16[1,4096,1024]{2,1,0:T(8,128)(2,1)}) custom-call(bf16[768,4096]{1,0:T(8,128)(2,1)} %get-tuple-element.89.rows, bf16[768,1024]{1,0:T(8,128)(2,1)S(1)} %get-tuple-element.75.gate_g, bf16[768,1024]{1,0:T(8,128)(2,1)S(1)} %copy-done.1, ...), custom_call_target="tpu_custom_call", output_to_operand_aliasing={{0}: (3, {}), {1}: (4, {})} | custom-call | flops 6442450944 | bytes 6442450 | tf_op jit(solution)/shard_map/pallas_call | solution.py:40
  280.7 3.2 %collective-permute-done.43.refs_2_ = bf16[2,96,512]{2,1,0:T(8,128)(2,1)S(1)} collective-permute-done((bf16[2,96,512]{2,1,0:T(8,128)(2,1)S(1)}, bf16[2,96,512]{2,1,0:T(8,128)(2,1)S(1)}, u32[]{:S(2)}, u32[]{:S(2)}) %collective-permute-start.43) | collective-permute-done | bytes 196640 | tf_op jit(solution)/shard_map/ppermute | solution.py:367
  283.9 1.6 shard_map.132
  (109 shorter events, 15.9 us)
Async XLA Ops:
  0.6 0.7 copy-start.4
  1.3 0.9 copy-start.14
  3.5 10.5 %collective-permute-start.5 = (bf16[2,96,512]{2,1,0:T(8,128)(2,1)S(1)}, bf16[2,96,512]{2,1,0:T(8,128)(2,1)S(1)}, u32[]{:S(2)}, u32[]{:S(2)}) collective-permute-start(bf16[2,96,512]{2,1,0:T(8,128)(2,1)S(1)} %get-tuple-element.57), channel_id=1, source_target_pairs={{0,3},{1,0},{2,1},{3,2},{4,7},{5,4},{6,5},{7,6},{8,11},{9,8},{10,9... | collective-permute-start | bytes 589832 | tf_op jit(solution)/shard_map/ppermute | solution.py:367
  8.6 16.7 %collective-permute-start.4 = (bf16[2,96,512]{2,1,0:T(8,128)(2,1)S(1)}, bf16[2,96,512]{2,1,0:T(8,128)(2,1)S(1)}, u32[]{:S(2)}, u32[]{:S(2)}) collective-permute-start(bf16[2,96,512]{2,1,0:T(8,128)(2,1)S(1)} %get-tuple-element.56), channel_id=1, source_target_pairs={{0,2},{1,3},{2,0},{3,1},{4,6},{5,7},{6,4},{7,5},{8,10},{9,11},{10,... | collective-permute-start | bytes 589832 | tf_op jit(solution)/shard_map/ppermute | solution.py:367
  8.6 16.7 %collective-permute-start.3 = (bf16[2,96,512]{2,1,0:T(8,128)(2,1)S(1)}, bf16[2,96,512]{2,1,0:T(8,128)(2,1)S(1)}, u32[]{:S(2)}, u32[]{:S(2)}) collective-permute-start(bf16[2,96,512]{2,1,0:T(8,128)(2,1)S(1)} %get-tuple-element.55), channel_id=1, source_target_pairs={{0,1},{1,2},{2,3},{3,0},{4,5},{5,6},{6,7},{7,4},{8,9},{9,10},{10,1... | collective-permute-start | bytes 589832 | tf_op jit(solution)/shard_map/ppermute | solution.py:367
  25.4 10.2 %collective-permute-start.6 = (bf16[1,384,512]{2,1,0:T(8,128)(2,1)S(1)}, bf16[1,384,512]{2,1,0:T(8,128)(2,1)S(1)}, u32[]{:S(2)}, u32[]{:S(2)}) collective-permute-start(bf16[1,384,512]{2,1,0:T(8,128)(2,1)S(1)} %pad_maximum_fusion.2), channel_id=1, source_target_pairs={{0,8},{4,12},{8,0},{12,4},{16,24},{20,28},{24,16},{28,20},{1,9},{5... | collective-permute-start | bytes 1179656 | tf_op jit(solution)/shard_map/ppermute | solution.py:364
  27.0 10.3 %collective-permute-start.8 = (bf16[1,384,512]{2,1,0:T(8,128)(2,1)S(1)}, bf16[1,384,512]{2,1,0:T(8,128)(2,1)S(1)}, u32[]{:S(2)}, u32[]{:S(2)}) collective-permute-start(bf16[1,384,512]{2,1,0:T(8,128)(2,1)S(1)} %pad_maximum_fusion.3), channel_id=1, source_target_pairs={{0,16},{4,20},{8,24},{12,28},{16,0},{20,4},{24,8},{28,12},{1,17},{... | collective-permute-start | bytes 1179656 | tf_op jit(solution)/shard_map/ppermute | solution.py:364
  35.7 18.1 %collective-permute-start.7 = (bf16[2,384,512]{2,1,0:T(8,128)(2,1)S(1)}, bf16[2,384,512]{2,1,0:T(8,128)(2,1)S(1)}, u32[]{:S(2)}, u32[]{:S(2)}) collective-permute-start(bf16[2,384,512]{2,1,0:T(8,128)(2,1)S(1)} %pad_maximum_fusion.refs_0_), channel_id=1, source_target_pairs={{0,16},{4,20},{8,24},{12,28},{16,0},{20,4},{24,8},{28,12},{1,17},{... | collective-permute-start | bytes 2359304 | tf_op jit(solution)/shard_map/ppermute | solution.py:364
  37.3 17.5 %collective-permute-start.9 = (bf16[2,384,512]{2,1,0:T(8,128)(2,1)S(1)}, bf16[2,384,512]{2,1,0:T(8,128)(2,1)S(1)}, u32[]{:S(2)}, u32[]{:S(2)}) collective-permute-start(bf16[2,384,512]{2,1,0:T(8,128)(2,1)S(1)} %pad_maximum_fusion.1.refs_2_), channel_id=1, source_target_pairs={{0,8},{4,12},{8,0},{12,4},{16,24},{20,28},{24,16},{28,20},{1,9},{5... | collective-permute-start | bytes 2359304 | tf_op jit(solution)/shard_map/ppermute | solution.py:364
  38.8 17.2 %collective-permute-start.10 = (bf16[2,384,512]{2,1,0:T(8,128)(2,1)S(1)}, bf16[2,384,512]{2,1,0:T(8,128)(2,1)}, u32[]{:S(2)}, u32[]{:S(2)}) collective-permute-start(bf16[2,384,512]{2,1,0:T(8,128)(2,1)S(1)} %pad_maximum_fusion.refs_0_), channel_id=1, source_target_pairs={{0,4},{4,0},{8,12},{12,8},{16,20},{20,16},{24,28},{28,24},{1,5},{5... | collective-permute-start | bytes 2359304 | tf_op jit(solution)/shard_map/ppermute | solution.py:364
  38.8 17.2 %collective-permute-start.12 = (bf16[2,384,512]{2,1,0:T(8,128)(2,1)S(1)}, bf16[2,384,512]{2,1,0:T(8,128)(2,1)}, u32[]{:S(2)}, u32[]{:S(2)}) collective-permute-start(bf16[2,384,512]{2,1,0:T(8,128)(2,1)S(1)} %pad_maximum_fusion.1.refs_2_), channel_id=1, source_target_pairs={{0,4},{4,0},{8,12},{12,8},{16,20},{20,16},{24,28},{28,24},{1,5},{5... | collective-permute-start | bytes 2359304 | tf_op jit(solution)/shard_map/ppermute | solution.py:364
  53.8 2.4 collective-permute-start.11
  53.8 0.9 copy-start.9
  54.8 2.5 collective-permute-start.13
  55.1 0.9 copy-start.11
  57.3 1.1 copy-start.10
  58.4 1.1 copy-start.12
  77.7 18.5 %copy-start.13 = (bf16[2,128,512]{2,1,0:T(8,128)(2,1)S(1)}, bf16[2,128,512]{2,1,0:T(8,128)(2,1)}, u32[]{:S(2)}) copy-start(bf16[2,128,512]{2,1,0:T(8,128)(2,1)} %cots.1) | copy-start | bytes 786436
  77.7 18.5 %copy-start.17 = (s32[2,128,2]{1,2,0:T(2,128)S(1)}, s32[2,128,2]{1,2,0:T(2,128)}, u32[]{:S(2)}) copy-start(s32[2,128,2]{1,2,0:T(2,128)} %param.8) | copy-start | bytes 6148
  83.3 66.4 %collective-permute-start.14 = (bf16[4,768,512]{2,1,0:T(8,128)(2,1)S(1)}, bf16[4,768,512]{2,1,0:T(8,128)(2,1)S(1)}, u32[]{:S(2)}, u32[]{:S(2)}) collective-permute-start(bf16[4,768,512]{2,1,0:T(8,128)(2,1)S(1)} %shard_map.121), channel_id=1, source_target_pairs={{0,4},{4,0},{8,12},{12,8},{16,20},{20,16},{24,28},{28,24},{1,5},{5... | collective-permute-start | bytes 9437192 | tf_op jit(solution)/shard_map/ppermute | solution.py:364
  83.6 5.4 %collective-permute-start = (f32[8,128]{1,0:T(8,128)S(1)}, f32[8,128]{1,0:T(8,128)S(1)}, u32[]{:S(2)}, u32[]{:S(2)}) collective-permute-start(f32[8,128]{1,0:T(8,128)S(1)} %get-tuple-element.52), channel_id=1, source_target_pairs={{0,4},{4,0},{8,12},{12,8},{16,20},{20,16},{24,28},{28,24},{1,5},{5... | collective-permute-start | bytes 12296 | tf_op jit(solution)/shard_map/ppermute | solution.py:364
  89.0 3.6 %collective-permute-start.1 = (f32[8,128]{1,0:T(8,128)S(1)}, f32[8,128]{1,0:T(8,128)S(1)}, u32[]{:S(2)}, u32[]{:S(2)}) collective-permute-start(f32[8,128]{1,0:T(8,128)S(1)} %add.26), channel_id=1, source_target_pairs={{0,8},{4,12},{8,0},{12,4},{16,24},{20,28},{24,16},{28,20},{1,9},{5... | collective-permute-start | bytes 12296 | tf_op jit(solution)/shard_map/ppermute | solution.py:364
  92.6 3.6 %collective-permute-start.2 = (f32[8,128]{1,0:T(8,128)S(1)}, f32[8,128]{1,0:T(8,128)S(1)}, u32[]{:S(2)}, u32[]{:S(2)}) collective-permute-start(f32[8,128]{1,0:T(8,128)S(1)} %add.27), channel_id=1, source_target_pairs={{0,16},{4,20},{8,24},{12,28},{16,0},{20,4},{24,8},{28,12},{1,17},{... | collective-permute-start | bytes 12296 | tf_op jit(solution)/shard_map/ppermute | solution.py:364
  96.6 9.7 %collective-permute-start.21 = (bf16[2,96,512]{2,1,0:T(8,128)(2,1)S(1)}, bf16[2,96,512]{2,1,0:T(8,128)(2,1)S(1)}, u32[]{:S(2)}, u32[]{:S(2)}) collective-permute-start(bf16[2,96,512]{2,1,0:T(8,128)(2,1)S(1)} %get-tuple-element.68), channel_id=1, source_target_pairs={{0,1},{1,2},{2,3},{3,0},{4,5},{5,6},{6,7},{7,4},{8,9},{9,10},{10,1... | collective-permute-start | bytes 589832 | tf_op jit(solution)/shard_map/ppermute | solution.py:367
  97.8 14.1 %collective-permute-start.22 = (bf16[2,96,512]{2,1,0:T(8,128)(2,1)S(1)}, bf16[2,96,512]{2,1,0:T(8,128)(2,1)S(1)}, u32[]{:S(2)}, u32[]{:S(2)}) collective-permute-start(bf16[2,96,512]{2,1,0:T(8,128)(2,1)S(1)} %get-tuple-element.69), channel_id=1, source_target_pairs={{0,2},{1,3},{2,0},{3,1},{4,6},{5,7},{6,4},{7,5},{8,10},{9,11},{10,... | collective-permute-start | bytes 589832 | tf_op jit(solution)/shard_map/ppermute | solution.py:367
  99.8 12.1 %collective-permute-start.23 = (bf16[2,96,512]{2,1,0:T(8,128)(2,1)S(1)}, bf16[2,96,512]{2,1,0:T(8,128)(2,1)S(1)}, u32[]{:S(2)}, u32[]{:S(2)}) collective-permute-start(bf16[2,96,512]{2,1,0:T(8,128)(2,1)S(1)} %get-tuple-element.70), channel_id=1, source_target_pairs={{0,3},{1,0},{2,1},{3,2},{4,7},{5,4},{6,5},{7,6},{8,11},{9,8},{10,9... | collective-permute-start | bytes 589832 | tf_op jit(solution)/shard_map/ppermute | solution.py:367
  111.9 20.5 %collective-permute-start.24 = (bf16[2,384,512]{2,1,0:T(8,128)(2,1)S(1)}, bf16[2,384,512]{2,1,0:T(8,128)(2,1)S(1)}, u32[]{:S(2)}, u32[]{:S(2)}) collective-permute-start(bf16[2,384,512]{2,1,0:T(8,128)(2,1)S(1)} %constant_dynamic-update-slice_fusion.refs_0_), channel_id=1, source_target_pairs={{0,8},{4,12},{8,0},{12,4},{16,24},{20,28},{24,16},{28,20},{1,9},{5... | collective-permute-start | bytes 2359304 | tf_op jit(solution)/shard_map/ppermute | solution.py:364
  113.2 35.9 %collective-permute-start.25 = (bf16[2,384,512]{2,1,0:T(8,128)(2,1)S(1)}, bf16[2,384,512]{2,1,0:T(8,128)(2,1)S(1)}, u32[]{:S(2)}, u32[]{:S(2)}) collective-permute-start(bf16[2,384,512]{2,1,0:T(8,128)(2,1)S(1)} %constant_dynamic-update-slice_fusion.refs_0_), channel_id=1, source_target_pairs={{0,16},{4,20},{8,24},{12,28},{16,0},{20,4},{24,8},{28,12},{1,17},{... | collective-permute-start | bytes 2359304 | tf_op jit(solution)/shard_map/ppermute | solution.py:364
  114.6 34.5 %collective-permute-start.26 = (bf16[2,384,512]{2,1,0:T(8,128)(2,1)S(1)}, bf16[2,384,512]{2,1,0:T(8,128)(2,1)S(1)}, u32[]{:S(2)}, u32[]{:S(2)}) collective-permute-start(bf16[2,384,512]{2,1,0:T(8,128)(2,1)S(1)} %constant_dynamic-update-slice_fusion.refs_0_), channel_id=1, source_target_pairs={{0,24},{4,28},{8,16},{12,20},{16,8},{20,12},{24,0},{28,4},{1,25},{... | collective-permute-start | bytes 2359304 | tf_op jit(solution)/shard_map/ppermute | solution.py:364
  115.4 42.7 %collective-permute-start.27 = (bf16[2,384,512]{2,1,0:T(8,128)(2,1)S(1)}, bf16[2,384,512]{2,1,0:T(8,128)(2,1)S(1)}, u32[]{:S(2)}, u32[]{:S(2)}) collective-permute-start(bf16[2,384,512]{2,1,0:T(8,128)(2,1)S(1)} %constant_dynamic-update-slice_fusion.refs_0_), channel_id=1, source_target_pairs={{0,4},{4,0},{8,12},{12,8},{16,20},{20,16},{24,28},{28,24},{1,5},{5... | collective-permute-start | bytes 2359304 | tf_op jit(solution)/shard_map/ppermute | solution.py:364
  132.4 25.8 %collective-permute-start.28 = (bf16[2,384,512]{2,1,0:T(8,128)(2,1)S(1)}, bf16[2,384,512]{2,1,0:T(8,128)(2,1)S(1)}, u32[]{:S(2)}, u32[]{:S(2)}) collective-permute-start(bf16[2,384,512]{2,1,0:T(8,128)(2,1)S(1)} %collective-permute-done.24.refs_1_), channel_id=1, source_target_pairs={{0,4},{4,0},{8,12},{12,8},{16,20},{20,16},{24,28},{28,24},{1,5},{5... | collective-permute-start | bytes 2359304 | tf_op jit(solution)/shard_map/ppermute | solution.py:364
  149.1 9.0 %collective-permute-start.29 = (bf16[2,384,512]{2,1,0:T(8,128)(2,1)S(1)}, bf16[2,384,512]{2,1,0:T(8,128)(2,1)S(1)}, u32[]{:S(2)}, u32[]{:S(2)}) collective-permute-start(bf16[2,384,512]{2,1,0:T(8,128)(2,1)S(1)} %collective-permute-done.25.refs_2_), channel_id=1, source_target_pairs={{0,4},{4,0},{8,12},{12,8},{16,20},{20,16},{24,28},{28,24},{1,5},{5... | collective-permute-start | bytes 2359304 | tf_op jit(solution)/shard_map/ppermute | solution.py:364
  149.1 9.0 %collective-permute-start.30 = (bf16[2,384,512]{2,1,0:T(8,128)(2,1)S(1)}, bf16[2,384,512]{2,1,0:T(8,128)(2,1)S(1)}, u32[]{:S(2)}, u32[]{:S(2)}) collective-permute-start(bf16[2,384,512]{2,1,0:T(8,128)(2,1)S(1)} %collective-permute-done.26.refs_3_), channel_id=1, source_target_pairs={{0,4},{4,0},{8,12},{12,8},{16,20},{20,16},{24,28},{28,24},{1,5},{5... | collective-permute-start | bytes 2359304 | tf_op jit(solution)/shard_map/ppermute | solution.py:364
  155.4 0.9 copy-start.6
  156.3 0.9 copy-start.7
  157.2 0.9 copy-start.8
  158.1 11.6 %copy-start.2 = (bf16[768,512]{1,0:T(8,128)(2,1)}, bf16[768,512]{1,0:T(8,128)(2,1)S(1)}, u32[]{:S(2)}) copy-start(bf16[768,512]{1,0:T(8,128)(2,1)S(1)} %get-tuple-element.59.refs_0_.refs_12_) | copy-start | bytes 2359300
  169.7 10.5 %copy-start = (bf16[768,1024]{1,0:T(8,128)(2,1)}, bf16[768,1024]{1,0:T(8,128)(2,1)S(1)}, u32[]{:S(2)}) copy-start(bf16[768,1024]{1,0:T(8,128)(2,1)S(1)} %get-tuple-element.76.up_g) | copy-start | bytes 4718596
  169.7 28.7 %copy-start.15 = (bf16[2,128,512]{2,1,0:T(8,128)(2,1)S(1)}, bf16[2,128,512]{2,1,0:T(8,128)(2,1)}, u32[]{:S(2)}) copy-start(bf16[2,128,512]{2,1,0:T(8,128)(2,1)} %tokens.3) | copy-start | bytes 786436
  180.2 25.9 %collective-permute-start.37 = (bf16[4,768,512]{2,1,0:T(8,128)(2,1)}, bf16[4,768,512]{2,1,0:T(8,128)(2,1)}, u32[]{:S(2)}, u32[]{:S(2)}) collective-permute-start(bf16[4,768,512]{2,1,0:T(8,128)(2,1)} %shard_map.127._), channel_id=1, source_target_pairs={{0,4},{4,0},{8,12},{12,8},{16,20},{20,16},{24,28},{28,24},{1,5},{5... | collective-permute-start | bytes 9437192 | tf_op jit(solution)/shard_map/ppermute | solution.py:364
  180.3 7.2 %collective-permute-start.33 = (f32[8,96]{1,0:T(8,128)S(1)}, f32[8,96]{1,0:T(8,128)S(1)}, u32[]{:S(2)}, u32[]{:S(2)}) collective-permute-start(f32[8,96]{1,0:T(8,128)S(1)} %get-tuple-element.107), channel_id=1, source_target_pairs={{0,1},{1,2},{2,3},{3,0},{4,5},{5,6},{6,7},{7,4},{8,9},{9,10},{10,1... | collective-permute-start | bytes 9224 | tf_op jit(solution)/shard_map/ppermute | solution.py:367
  185.1 4.5 %collective-permute-start.32 = (f32[8,96]{1,0:T(8,128)S(1)}, f32[8,96]{1,0:T(8,128)S(1)}, u32[]{:S(2)}, u32[]{:S(2)}) collective-permute-start(f32[8,96]{1,0:T(8,128)S(1)} %get-tuple-element.106), channel_id=1, source_target_pairs={{0,2},{1,3},{2,0},{3,1},{4,6},{5,7},{6,4},{7,5},{8,10},{9,11},{10,... | collective-permute-start | bytes 9224 | tf_op jit(solution)/shard_map/ppermute | solution.py:367
  185.8 3.8 %collective-permute-start.31 = (f32[8,96]{1,0:T(8,128)S(1)}, f32[8,96]{1,0:T(8,128)S(1)}, u32[]{:S(2)}, u32[]{:S(2)}) collective-permute-start(f32[8,96]{1,0:T(8,128)S(1)} %get-tuple-element.105), channel_id=1, source_target_pairs={{0,3},{1,0},{2,1},{3,2},{4,7},{5,4},{6,5},{7,6},{8,11},{9,8},{10,9... | collective-permute-start | bytes 9224 | tf_op jit(solution)/shard_map/ppermute | solution.py:367
  189.6 1.2 collective-permute-start.34
  190.9 3.7 %collective-permute-start.35 = (f32[4,8,96]{2,1,0:T(8,128)S(1)}, f32[4,8,96]{2,1,0:T(8,128)S(1)}, u32[]{:S(2)}, u32[]{:S(2)}) collective-permute-start(f32[4,8,96]{2,1,0:T(8,128)S(1)} %fusion.5), channel_id=1, source_target_pairs={{0,8},{4,12},{8,0},{12,4},{16,24},{20,28},{24,16},{28,20},{1,9},{5... | collective-permute-start | bytes 36872 | tf_op jit(solution)/shard_map/ppermute | solution.py:364
  192.0 25.9 %collective-permute-start.15 = (bf16[768,512]{1,0:T(8,128)(2,1)}, bf16[768,512]{1,0:T(8,128)(2,1)S(1)}, u32[]{:S(2)}, u32[]{:S(2)}) collective-permute-start(bf16[768,512]{1,0:T(8,128)(2,1)} %copy-done.8), channel_id=1, source_target_pairs={{0,8},{4,12},{8,0},{12,4},{16,24},{20,28},{24,16},{28,20},{1,9},{5... | collective-permute-start | bytes 2359304 | tf_op jit(solution)/shard_map/ppermute | solution.py:364
  194.6 3.7 %collective-permute-start.36 = (f32[4,8,96]{2,1,0:T(8,128)S(1)}, f32[4,8,96]{2,1,0:T(8,128)S(1)}, u32[]{:S(2)}, u32[]{:S(2)}) collective-permute-start(f32[4,8,96]{2,1,0:T(8,128)S(1)} %fusion.10), channel_id=1, source_target_pairs={{0,16},{4,20},{8,24},{12,28},{16,0},{20,4},{24,8},{28,12},{1,17},{... | collective-permute-start | bytes 36872 | tf_op jit(solution)/shard_map/ppermute | solution.py:364
  199.4 3.8 %collective-permute-start.45 = (f32[8,512]{1,0:T(8,128)S(1)}, f32[8,512]{1,0:T(8,128)S(1)}, u32[]{:S(2)}, u32[]{:S(2)}) collective-permute-start(f32[8,512]{1,0:T(8,128)S(1)} %get-tuple-element.95), channel_id=1, source_target_pairs={{0,1},{1,0},{2,3},{3,2},{4,5},{5,4},{6,7},{7,6},{8,9},{9,8},{10,11... | collective-permute-start | bytes 49160 | tf_op jit(solution)/shard_map/ppermute | solution.py:587
  200.0 37.5 %collective-permute-start.16 = (bf16[768,512]{1,0:T(8,128)(2,1)}, bf16[768,512]{1,0:T(8,128)(2,1)S(1)}, u32[]{:S(2)}, u32[]{:S(2)}) collective-permute-start(bf16[768,512]{1,0:T(8,128)(2,1)} %copy-done.7), channel_id=1, source_target_pairs={{0,16},{4,20},{8,24},{12,28},{16,0},{20,4},{24,8},{28,12},{1,17},{... | collective-permute-start | bytes 2359304 | tf_op jit(solution)/shard_map/ppermute | solution.py:364
  201.6 35.9 %collective-permute-start.17 = (bf16[768,512]{1,0:T(8,128)(2,1)}, bf16[768,512]{1,0:T(8,128)(2,1)S(1)}, u32[]{:S(2)}, u32[]{:S(2)}) collective-permute-start(bf16[768,512]{1,0:T(8,128)(2,1)} %copy-done.6), channel_id=1, source_target_pairs={{0,24},{4,28},{8,16},{12,20},{16,8},{20,12},{24,0},{28,4},{1,25},{... | collective-permute-start | bytes 2359304 | tf_op jit(solution)/shard_map/ppermute | solution.py:364
  203.2 38.1 %collective-permute-start.46 = (f32[8,512]{1,0:T(8,128)S(1)}, f32[8,512]{1,0:T(8,128)S(1)}, u32[]{:S(2)}, u32[]{:S(2)}) collective-permute-start(f32[8,512]{1,0:T(8,128)S(1)} %add.32), channel_id=1, source_target_pairs={{0,2},{1,3},{2,0},{3,1},{4,6},{5,7},{6,4},{7,5},{8,10},{9,11},{10,... | collective-permute-start | bytes 49160 | tf_op jit(solution)/shard_map/ppermute | solution.py:587
  206.1 1.4 copy-start.1
  217.1 37.5 %collective-permute-start.38 = (bf16[2,384,512]{2,1,0:T(8,128)(2,1)S(1)}, bf16[2,384,512]{2,1,0:T(8,128)(2,1)S(1)}, u32[]{:S(2)}, u32[]{:S(2)}) collective-permute-start(bf16[2,384,512]{2,1,0:T(8,128)(2,1)S(1)} %get-tuple-element.78), channel_id=1, source_target_pairs={{0,16},{4,20},{8,24},{12,28},{16,0},{20,4},{24,8},{28,12},{1,17},{... | collective-permute-start | bytes 2359304 | tf_op jit(solution)/shard_map/ppermute | solution.py:364
  218.0 37.8 %collective-permute-start.40 = (bf16[2,384,512]{2,1,0:T(8,128)(2,1)S(1)}, bf16[2,384,512]{2,1,0:T(8,128)(2,1)S(1)}, u32[]{:S(2)}, u32[]{:S(2)}) collective-permute-start(bf16[2,384,512]{2,1,0:T(8,128)(2,1)S(1)} %get-tuple-element.82), channel_id=1, source_target_pairs={{0,8},{4,12},{8,0},{12,4},{16,24},{20,28},{24,16},{28,20},{1,9},{5... | collective-permute-start | bytes 2359304 | tf_op jit(solution)/shard_map/ppermute | solution.py:364
  219.5 17.9 %copy-start.3 = (bf16[768,512]{1,0:T(8,128)(2,1)S(1)}, bf16[768,512]{1,0:T(8,128)(2,1)}, u32[]{:S(2)}) copy-start(bf16[768,512]{1,0:T(8,128)(2,1)} %copy-done.2) | copy-start | bytes 2359300
  237.8 8.8 %collective-permute-start.18 = (bf16[2,96,512]{2,1,0:T(8,128)(2,1)S(1)}, bf16[2,96,512]{2,1,0:T(8,128)(2,1)S(1)}, u32[]{:S(2)}, u32[]{:S(2)}) collective-permute-start(bf16[2,96,512]{2,1,0:T(8,128)(2,1)S(1)} %get-tuple-element.64), channel_id=1, source_target_pairs={{0,3},{1,0},{2,1},{3,2},{4,7},{5,4},{6,5},{7,6},{8,11},{9,8},{10,9... | collective-permute-start | bytes 589832 | tf_op jit(solution)/shard_map/ppermute | solution.py:367
  240.8 12.3 %collective-permute-start.19 = (bf16[2,96,512]{2,1,0:T(8,128)(2,1)S(1)}, bf16[2,96,512]{2,1,0:T(8,128)(2,1)S(1)}, u32[]{:S(2)}, u32[]{:S(2)}) collective-permute-start(bf16[2,96,512]{2,1,0:T(8,128)(2,1)S(1)} %get-tuple-element.65), channel_id=1, source_target_pairs={{0,2},{1,3},{2,0},{3,1},{4,6},{5,7},{6,4},{7,5},{8,10},{9,11},{10,... | collective-permute-start | bytes 589832 | tf_op jit(solution)/shard_map/ppermute | solution.py:367
  241.3 11.8 %collective-permute-start.20 = (bf16[2,96,512]{2,1,0:T(8,128)(2,1)S(1)}, bf16[2,96,512]{2,1,0:T(8,128)(2,1)S(1)}, u32[]{:S(2)}, u32[]{:S(2)}) collective-permute-start(bf16[2,96,512]{2,1,0:T(8,128)(2,1)S(1)} %get-tuple-element.66), channel_id=1, source_target_pairs={{0,1},{1,2},{2,3},{3,0},{4,5},{5,6},{6,7},{7,4},{8,9},{9,10},{10,1... | collective-permute-start | bytes 589832 | tf_op jit(solution)/shard_map/ppermute | solution.py:367
  254.7 11.8 %collective-permute-start.39 = (bf16[1,384,512]{2,1,0:T(8,128)(2,1)S(1)}, bf16[1,384,512]{2,1,0:T(8,128)(2,1)S(1)}, u32[]{:S(2)}, u32[]{:S(2)}) collective-permute-start(bf16[1,384,512]{2,1,0:T(8,128)(2,1)S(1)} %get-tuple-element.80), channel_id=1, source_target_pairs={{0,8},{4,12},{8,0},{12,4},{16,24},{20,28},{24,16},{28,20},{1,9},{5... | collective-permute-start | bytes 1179656 | tf_op jit(solution)/shard_map/ppermute | solution.py:364
  255.9 10.6 %collective-permute-start.41 = (bf16[1,384,512]{2,1,0:T(8,128)(2,1)S(1)}, bf16[1,384,512]{2,1,0:T(8,128)(2,1)S(1)}, u32[]{:S(2)}, u32[]{:S(2)}) collective-permute-start(bf16[1,384,512]{2,1,0:T(8,128)(2,1)S(1)} %get-tuple-element.84), channel_id=1, source_target_pairs={{0,16},{4,20},{8,24},{12,28},{16,0},{20,4},{24,8},{28,12},{1,17},{... | collective-permute-start | bytes 1179656 | tf_op jit(solution)/shard_map/ppermute | solution.py:364
  266.8 14.0 %collective-permute-start.42 = (bf16[2,96,512]{2,1,0:T(8,128)(2,1)S(1)}, bf16[2,96,512]{2,1,0:T(8,128)(2,1)S(1)}, u32[]{:S(2)}, u32[]{:S(2)}) collective-permute-start(bf16[2,96,512]{2,1,0:T(8,128)(2,1)S(1)} %get-tuple-element.86), channel_id=1, source_target_pairs={{0,3},{1,0},{2,1},{3,2},{4,7},{5,4},{6,5},{7,6},{8,11},{9,8},{10,9... | collective-permute-start | bytes 589832 | tf_op jit(solution)/shard_map/ppermute | solution.py:367
  268.0 15.9 %collective-permute-start.43 = (bf16[2,96,512]{2,1,0:T(8,128)(2,1)S(1)}, bf16[2,96,512]{2,1,0:T(8,128)(2,1)S(1)}, u32[]{:S(2)}, u32[]{:S(2)}) collective-permute-start(bf16[2,96,512]{2,1,0:T(8,128)(2,1)S(1)} %get-tuple-element.87), channel_id=1, source_target_pairs={{0,2},{1,3},{2,0},{3,1},{4,6},{5,7},{6,4},{7,5},{8,10},{9,11},{10,... | collective-permute-start | bytes 589832 | tf_op jit(solution)/shard_map/ppermute | solution.py:367
  269.3 14.6 %collective-permute-start.44 = (bf16[2,96,512]{2,1,0:T(8,128)(2,1)S(1)}, bf16[2,96,512]{2,1,0:T(8,128)(2,1)S(1)}, u32[]{:S(2)}, u32[]{:S(2)}) collective-permute-start(bf16[2,96,512]{2,1,0:T(8,128)(2,1)S(1)} %get-tuple-element.88), channel_id=1, source_target_pairs={{0,1},{1,2},{2,3},{3,0},{4,5},{5,6},{6,7},{7,4},{8,9},{9,10},{10,1... | collective-permute-start | bytes 589832 | tf_op jit(solution)/shard_map/ppermute | solution.py:367
  271.2 12.7 %copy-start.5 = (bf16[512,4]{0,1:T(4,128)(2,1)S(1)}, bf16[512,4]{0,1:T(4,128)(2,1)}, u32[]{:S(2)}) copy-start(bf16[512,4]{0,1:T(4,128)(2,1)} %param.9) | copy-start | bytes 12292
  (1 other events, 0.7 us)

commit v3 on v2

--- a/solution.py
+++ b/solution.py
@@ -138,11 +138,11 @@
 
 
 def assemble(rank, pieces, plan, out):
-    slots, width = pieces[0].shape[1:]
     for piece, entries in zip(pieces, plan):
-        for i, (step, k) in enumerate(entries):
+        slots, width = piece.shape[1:]
+        for i, (row, k) in enumerate(entries):
             at = pl.multiple_of(jnp.bitwise_xor(rank, k) * width, 128)
-            out[step * slots : (step + 1) * slots, pl.ds(at, width)] = piece[i]
+            out[row : row + slots, pl.ds(at, width)] = piece[i]
 
 
 @contextlib.contextmanager
@@ -380,7 +380,7 @@
     logit_rows = shape((micro * experts, tok_rows), F32)
     *packed, logits, slots = call(
         functools.partial(pack_tokens, **sizes), (1,), [me],
-        [full(ids), full(tokens), full(router)],
+        [full(far(ids)), full(far(tokens)), full(far(router))],
         [full(block)] * experts + [full(logit_rows), full(token_rows)],
         flops=10**8,
     )
@@ -406,33 +406,34 @@
     def to_partner(pieces, plan):
         for i in range(len(pieces)):
             pieces.append(swap(pieces[i], 1))
-            plan.append([(step, k ^ 1) for step, k in plan[i]])
+            plan.append([(row, k ^ 1) for row, k in plan[i]])
         return pieces, plan
 
     def gather_by_steps(blocks):
         got = dispatch(blocks)
         pieces, plan = [], []
-        held, numbers = [], []
-        for step in range(micro):
-            held.append(jnp.concatenate([part[step : step + 1] for part in got], axis=1))
-            numbers.append([(step, 0)])
-        for stage in range(len(chip_bits)):
+        for parts, base in ((got[:1], 0), (got[1:], capacity)):
+            held, numbers = [], []
             for step in range(micro):
-                bit = order[step][stage]
-                recv = swap(held[step], bit)
-                there = [(step, k ^ bit) for _, k in numbers[step]]
-                if stage == len(chip_bits) - 1:
-                    pieces += [held[step], recv]
-                    plan += [numbers[step], there]
-                else:
-                    held[step] = jnp.concatenate([held[step], recv], axis=0)
-                    numbers[step] = numbers[step] + there
+                held.append(jnp.concatenate([part[step : step + 1] for part in parts], axis=1))
+                numbers.append([(step * slots_n + base, 0)])
+            for stage in range(len(chip_bits)):
+                for step in range(micro):
+                    bit = order[step][stage]
+                    recv = swap(held[step], bit)
+                    there = [(row, k ^ bit) for row, k in numbers[step]]
+                    if stage == len(chip_bits) - 1:
+                        pieces += [held[step], recv]
+                        plan += [numbers[step], there]
+                    else:
+                        held[step] = jnp.concatenate([held[step], recv], axis=0)
+                        numbers[step] = numbers[step] + there
         return to_partner(pieces, plan)
 
     def gather_at_once(blocks):
         own = jnp.concatenate(dispatch(blocks), axis=1)
         pieces = [own] + [swap(own, 2 * k) for k in range(1, half)]
-        plan = [[(step, 2 * k) for step in range(micro)] for k in range(half)]
+        plan = [[(step * slots_n, 2 * k) for step in range(micro)] for k in range(half)]
         return to_partner(pieces, plan)
 
     token_pieces, token_plan = gather_by_steps(packed)

time: 286 us -> 296 us (1.035)
  local copies, waits for them, and re-layouts: 10.7 us -> 14.5 us
  starting transfers between devices: 58.4 us -> 62.1 us
    unnamed x39 -> x49, local copies, waits for them, and re-layouts: 10.5 us -> 14.3 us
    ppermute x30 -> x38, starting transfers between devices: 25.7 us -> 29.2 us  [swap(): return lax.ppermute(value, 'rep', [(i, i ^ bits) for i in range(ranks)])]
    ppermute x30 -> x38, waiting for transfers between devices: 78.3 us -> 80.4 us  [swap(): return lax.ppermute(value, 'rep', [(i, i ^ bits) for i in range(ranks)])]
  transfers between devices with their start and end apart: 47 -> 55, of which waited for: 23 -> 24; matrix products, arithmetic and copies ran while one was open for 0% -> 0% of each run, Pallas kernels for 17% -> 16%
where the time goes in v3:
time: 296 us; the launch traced here: 295 us
  waiting for transfers between devices  120 us (41%)
  Pallas kernels  97.3 us (33%)
  starting transfers between devices  62.1 us (21%)
  local copies, waits for them, and re-layouts  14.5 us (5%)
    pallas_call x18, Pallas kernels, pallas(): pl.pallas_call(kernel, grid_spec=pltpu.PrefetchScalarGridSpec(num_scalar_...  97.3 us
    ppermute x38, waiting for transfers between devices, swap(): return lax.ppermute(value, 'rep', [(i, i ^ bits) for i in range(ranks)])  80.4 us
    ppermute x15, waiting for transfers between devices, shift(): lax.ppermute(value, 'ep', [(i, (i + turn) % places) for i in range(places)])  39.1 us
    ppermute x15, starting transfers between devices, shift(): lax.ppermute(value, 'ep', [(i, (i + turn) % places) for i in range(places)])  29.3 us
    ppermute x38, starting transfers between devices, swap(): return lax.ppermute(value, 'rep', [(i, i ^ bits) for i in range(ranks)])  29.2 us
    unnamed x49, local copies, waits for them, and re-layouts  14.3 us
  transfers between devices with their start and end apart: 55, of which 24 were waited for; matrix products, arithmetic and copies ran while one was open for 0% of the time, Pallas kernels for 16%

profile of v3, /device:TPU:0, one launch (start us, length us, event | category | flops | bytes accessed | tf_op | source)
XLA Modules:
  0.0 295.5 jit_solution(5415762574142179456)
XLA Ops:
  0.6 1.5 shard_map.118
  2.1 5.1 %collective-permute-start.9 = (bf16[2,96,512]{2,1,0:T(8,128)(2,1)S(1)}, bf16[2,96,512]{2,1,0:T(8,128)(2,1)S(1)}, u32[]{:S(2)}, u32[]{:S(2)}) collective-permute-start(bf16[2,96,512]{2,1,0:T(8,128)(2,1)S(1)} %get-tuple-element.57), channel_id=1, source_target_pairs={{0,3},{1,0},{2,1},{3,2},{4,7},{5,4},{6,5},{7,6},{8,11},{9,8},{10,9... | collective-permute-start | bytes 589832 | tf_op jit(solution)/shard_map/ppermute | solution.py:367
  8.3 4.3 %collective-permute-done.9 = bf16[2,96,512]{2,1,0:T(8,128)(2,1)S(1)} collective-permute-done((bf16[2,96,512]{2,1,0:T(8,128)(2,1)S(1)}, bf16[2,96,512]{2,1,0:T(8,128)(2,1)S(1)}, u32[]{:S(2)}, u32[]{:S(2)}) %collective-permute-start.9) | collective-permute-done | bytes 196640 | tf_op jit(solution)/shard_map/ppermute | solution.py:367
  12.6 11.3 %collective-permute-done.8 = bf16[2,96,512]{2,1,0:T(8,128)(2,1)S(1)} collective-permute-done((bf16[2,96,512]{2,1,0:T(8,128)(2,1)S(1)}, bf16[2,96,512]{2,1,0:T(8,128)(2,1)S(1)}, u32[]{:S(2)}, u32[]{:S(2)}) %collective-permute-start.8) | collective-permute-done | bytes 196640 | tf_op jit(solution)/shard_map/ppermute | solution.py:367
  24.0 1.6 collective-permute-start.10
  25.6 1.6 collective-permute-start.12
  27.2 4.9 %collective-permute-done.10 = bf16[1,288,512]{2,1,0:T(8,128)(2,1)S(1)} collective-permute-done((bf16[1,288,512]{2,1,0:T(8,128)(2,1)S(1)}, bf16[1,288,512]{2,1,0:T(8,128)(2,1)S(1)}, u32[]{:S(2)}, u32[]{:S(2)}) %collective-permute-start.10) | collective-permute-done | bytes 294944 | tf_op jit(solution)/shard_map/ppermute | solution.py:364
  32.2 1.6 collective-permute-start.11
  33.8 1.6 collective-permute-start.13
  36.0 1.5 collective-permute-start.5
  37.5 11.7 %collective-permute-done.3 = bf16[1,96,512]{2,1,0:T(8,128)(2,1)S(1)} collective-permute-done((bf16[1,96,512]{2,1,0:T(8,128)(2,1)S(1)}, bf16[1,96,512]{2,1,0:T(8,128)(2,1)S(1)}, u32[]{:S(2)}, u32[]{:S(2)}) %collective-permute-start.3) | collective-permute-done | bytes 98336 | tf_op jit(solution)/shard_map/ppermute | solution.py:364
  49.2 1.3 collective-permute-start.4
  51.4 3.6 %collective-permute-done.4.refs_1_ = bf16[2,96,512]{2,1,0:T(8,128)(2,1)S(1)} collective-permute-done((bf16[2,96,512]{2,1,0:T(8,128)(2,1)S(1)}, bf16[2,96,512]{2,1,0:T(8,128)(2,1)S(1)}, u32[]{:S(2)}, u32[]{:S(2)}) %collective-permute-start.4) | collective-permute-done | bytes 196640 | tf_op jit(solution)/shard_map/ppermute | solution.py:364
  54.9 1.3 collective-permute-done.6.refs_3_
  60.2 1.4 collective-permute-done.15.refs_9_
  62.5 1.3 collective-permute-done.17.refs_11_
  65.6 1.1 copy-done.11
  70.3 17.9 %shard_map.120 = (bf16[768,4096]{1,0:T(8,128)(2,1)}, bf16[768,1024]{1,0:T(8,128)(2,1)S(1)}, f32[768,1024]{1,0:T(8,128)S(1)}, f32[768,1024]{1,0:T(8,128)S(1)}) custom-call(s32[1]{0:T(128)} %bitcast.5.rank, bf16[2,96,512]{2,1,0:T(8,128)(2,1)S(1)} %pad_maximum_fusion.4.refs_0_, bf16[2,96,512]{2,1,0:T(8,128)(2,1)S(1)} %collective-permute-done.4.refs_1_, ...), custom_call_target="tpu_custom_call" | custom-call | flops 12884901888 | bytes 12884901 | tf_op jit(solution)/shard_map/pallas_call | solution.py:40
  88.3 5.5 %shard_map.121 = bf16[4,768,512]{2,1,0:T(8,128)(2,1)S(1)} custom-call(s32[1]{0:T(128)} %bitcast.5.rank, bf16[768,1024]{1,0:T(8,128)(2,1)S(1)} %get-tuple-element.58.hidden._.refs_9_, bf16[1024,4096]{1,0:T(8,128)(2,1)} %bitcast.27, bf16[768,1024]{1,0:T(8,128)(2,1)S(1)} %get-tuple-element.58.hidden._.refs_9_), custom_call_target="tpu_custom_call" | custom-call | flops 3221225472 | bytes 3221225 | tf_op jit(solution)/shard_map/pallas_call | solution.py:40
  94.4 5.2 %collective-permute-done = f32[8,128]{1,0:T(8,128)S(1)} collective-permute-done((f32[8,128]{1,0:T(8,128)S(1)}, f32[8,128]{1,0:T(8,128)S(1)}, u32[]{:S(2)}, u32[]{:S(2)}) %collective-permute-start) | collective-permute-done | bytes 4128 | tf_op jit(solution)/shard_map/ppermute | solution.py:364
  100.4 2.8 collective-permute-done.1
  104.0 2.8 collective-permute-done.2
  107.2 1.2 collective-permute-start.29
  108.4 2.0 collective-permute-start.30
  110.4 2.8 collective-permute-start.31
  113.3 3.6 %collective-permute-done.29 = bf16[2,96,512]{2,1,0:T(8,128)(2,1)S(1)} collective-permute-done((bf16[2,96,512]{2,1,0:T(8,128)(2,1)S(1)}, bf16[2,96,512]{2,1,0:T(8,128)(2,1)S(1)}, u32[]{:S(2)}, u32[]{:S(2)}) %collective-permute-start.29) | collective-permute-done | bytes 196640 | tf_op jit(solution)/shard_map/ppermute | solution.py:367
  116.9 5.4 %collective-permute-done.30 = bf16[2,96,512]{2,1,0:T(8,128)(2,1)S(1)} collective-permute-done((bf16[2,96,512]{2,1,0:T(8,128)(2,1)S(1)}, bf16[2,96,512]{2,1,0:T(8,128)(2,1)S(1)}, u32[]{:S(2)}, u32[]{:S(2)}) %collective-permute-start.30) | collective-permute-done | bytes 196640 | tf_op jit(solution)/shard_map/ppermute | solution.py:367
  123.1 1.5 collective-permute-start.33
  124.7 1.2 collective-permute-start.34
  125.9 16.9 %collective-permute-done.32.refs_1_ = bf16[2,384,512]{2,1,0:T(8,128)(2,1)S(1)} collective-permute-done((bf16[2,384,512]{2,1,0:T(8,128)(2,1)S(1)}, bf16[2,384,512]{2,1,0:T(8,128)(2,1)S(1)}, u32[]{:S(2)}, u32[]{:S(2)}) %collective-permute-start.32) | collective-permute-done | bytes 786464 | tf_op jit(solution)/shard_map/ppermute | solution.py:364
  142.8 16.3 %collective-permute-done.33.refs_2_ = bf16[2,384,512]{2,1,0:T(8,128)(2,1)S(1)} collective-permute-done((bf16[2,384,512]{2,1,0:T(8,128)(2,1)S(1)}, bf16[2,384,512]{2,1,0:T(8,128)(2,1)S(1)}, u32[]{:S(2)}, u32[]{:S(2)}) %collective-permute-start.33) | collective-permute-done | bytes 786464 | tf_op jit(solution)/shard_map/ppermute | solution.py:364
  159.6 5.7 %shard_map.122 = (bf16[768,512]{1,0:T(8,128)(2,1)S(1)}, bf16[768,512]{1,0:T(8,128)(2,1)S(1)}, bf16[768,512]{1,0:T(8,128)(2,1)S(1)}, bf16[768,512]{1,0:T(8,128)(2,1)S(1)}) custom-call(s32[1]{0:T(128)} %bitcast.5.rank, bf16[768,1024]{1,0:T(8,128)(2,1)S(1)} %get-tuple-element.58.hidden._.refs_9_, bf16[1024,4096]{1,0:T(8,128)(2,1)} %bitcast.28, ...), custom_call_target="tpu_custom_call" | custom-call | flops 3221225472 | bytes 3221225 | tf_op jit(solution)/shard_map/pallas_call | solution.py:40
  168.1 11.5 %shard_map.125 = (bf16[768,4096]{1,0:T(8,128)(2,1)}, bf16[768,1024]{1,0:T(8,128)(2,1)S(1)}, bf16[768,1024]{1,0:T(8,128)(2,1)S(1)}, f32[8,768]{1,0:T(8,128)S(1)}) custom-call(s32[1]{0:T(128)} %bitcast.5.rank, bf16[2,384,512]{2,1,0:T(8,128)(2,1)S(1)} %constant_dynamic-update-slice_fusion.refs_0_, bf16[2,384,512]{2,1,0:T(8,128)(2,1)S(1)} %collective-permute-done.32.refs_1_, ...), custom_call_target="tpu_custom_call" | custom-call | flops 6442450944 | bytes 6442450 | tf_op jit(solution)/shard_map/pallas_call | solution.py:40
  179.7 10.5 %shard_map.127._ = bf16[4,768,512]{2,1,0:T(8,128)(2,1)} custom-call(s32[1]{0:T(128)} %bitcast.5.rank, bf16[768,1024]{1,0:T(8,128)(2,1)S(1)} %get-tuple-element.75.gate_g, bf16[768,1024]{1,0:T(8,128)(2,1)S(1)} %get-tuple-element.76.up_g, bf16[4096,1024]{1,0:T(8,128)(2,1)} %bitcast.31, bf16[4096,1024]{1,0:T(8,128)(2,1)} %bitcast.34, ...), custom_call_target="tpu_custom_call" | custom-call | flops 6442450944 | bytes 6442450 | tf_op jit(solution)/shard_map/pallas_call | solution.py:40
  190.3 4.8 %collective-permute-start.41 = (f32[8,96]{1,0:T(8,128)S(1)}, f32[8,96]{1,0:T(8,128)S(1)}, u32[]{:S(2)}, u32[]{:S(2)}) collective-permute-start(f32[8,96]{1,0:T(8,128)S(1)} %get-tuple-element.107), channel_id=1, source_target_pairs={{0,1},{1,2},{2,3},{3,0},{4,5},{5,6},{6,7},{7,4},{8,9},{9,10},{10,1... | collective-permute-start | bytes 9224 | tf_op jit(solution)/shard_map/ppermute | solution.py:367
  195.7 1.8 collective-permute-start.39
  197.5 2.1 collective-permute-done.40
  199.7 1.2 collective-permute-done.42
  200.8 1.2 collective-permute-start.43
  202.9 1.7 collective-permute-done.43
  204.6 1.7 collective-permute-start.44
  206.3 2.0 collective-permute-done.44
  209.9 1.7 collective-permute-start.24
  211.6 1.2 collective-permute-start.25
  213.1 3.0 %collective-permute-start.54 = (f32[8,512]{1,0:T(8,128)S(1)}, f32[8,512]{1,0:T(8,128)S(1)}, u32[]{:S(2)}, u32[]{:S(2)}) collective-permute-start(f32[8,512]{1,0:T(8,128)S(1)} %add.32), channel_id=1, source_target_pairs={{0,2},{1,3},{2,0},{3,1},{4,6},{5,7},{6,4},{7,5},{8,10},{9,11},{10,... | collective-permute-start | bytes 49160 | tf_op jit(solution)/shard_map/ppermute | solution.py:588
  216.1 1.4 copy-done.1
  217.5 9.6 %shard_map.128 = (bf16[2,384,512]{2,1,0:T(8,128)(2,1)S(1)}, bf16[2,384,512]{2,1,0:T(8,128)(2,1)S(1)}, bf16[2,384,512]{2,1,0:T(8,128)(2,1)S(1)}, bf16[2,384,512]{2,1,0:T(8,128)(2,1)S(1)}) custom-call(s32[1]{0:T(128)} %bitcast.5.rank, bf16[768,1024]{1,0:T(8,128)(2,1)S(1)} %get-tuple-element.75.gate_g, bf16[768,1024]{1,0:T(8,128)(2,1)S(1)} %copy-done.1, ...), custom_call_target="tpu_custom_call" | custom-call | flops 6442450944 | bytes 6442450 | tf_op jit(solution)/shard_map/pallas_call | solution.py:40
  228.0 1.6 collective-permute-start.48
  229.6 10.6 %shard_map.135 = bf16[1,1024,4096]{2,1,0:T(8,128)(2,1)} custom-call(bf16[768,1024]{1,0:T(8,128)(2,1)S(1)} %get-tuple-element.58.hidden._.refs_9_, bf16[768,4096]{1,0:T(8,128)(2,1)} %get-tuple-element.94.cots, f32[8,768]{1,0:T(8,128)S(1)} %get-tuple-element.73._), custom_call_target="tpu_custom_call" | custom-call | flops 6442450944 | bytes 6442450 | tf_op jit(solution)/shard_map/pallas_call | solution.py:40
  240.2 7.2 %collective-permute-done.24.refs_2_ = bf16[768,512]{1,0:T(8,128)(2,1)S(1)} collective-permute-done((bf16[768,512]{1,0:T(8,128)(2,1)}, bf16[768,512]{1,0:T(8,128)(2,1)S(1)}, u32[]{:S(2)}, u32[]{:S(2)}) %collective-permute-start.24) | collective-permute-done | bytes 786464 | tf_op jit(solution)/shard_map/ppermute | solution.py:364
  247.8 2.9 collective-permute-start.26
  251.2 1.9 collective-permute-start.28
  253.8 2.8 collective-permute-done.26.refs_1_
  256.6 6.4 %collective-permute-done.27.refs_2_ = bf16[2,96,512]{2,1,0:T(8,128)(2,1)S(1)} collective-permute-done((bf16[2,96,512]{2,1,0:T(8,128)(2,1)S(1)}, bf16[2,96,512]{2,1,0:T(8,128)(2,1)S(1)}, u32[]{:S(2)}, u32[]{:S(2)}) %collective-permute-start.27) | collective-permute-done | bytes 196640 | tf_op jit(solution)/shard_map/ppermute | solution.py:367
  263.0 1.5 shard_map.124
  264.7 1.1 collective-permute-start.47
  265.9 1.1 collective-permute-start.49
  267.1 9.5 %shard_map.133 = (bf16[1,4096,1024]{2,1,0:T(8,128)(2,1)}, bf16[1,4096,1024]{2,1,0:T(8,128)(2,1)}) custom-call(bf16[768,4096]{1,0:T(8,128)(2,1)} %get-tuple-element.89.rows, bf16[768,1024]{1,0:T(8,128)(2,1)S(1)} %get-tuple-element.75.gate_g, bf16[768,1024]{1,0:T(8,128)(2,1)S(1)} %copy-done.1, bf16[2,384,512]{2,1,0:T(8,128)(2,1)S(1)} %get-tuple-element.77.kept.refs_0_), custom_call_target="tpu_custom_call" | custom-call | flops 6442450944 | bytes 6442450 | tf_op jit(solution)/shard_map/pallas_call | solution.py:40
  276.7 1.2 collective-permute-start.50
  278.0 1.3 collective-permute-start.51
  279.3 1.9 collective-permute-start.52
  281.2 9.5 %shard_map.134 = (bf16[1,4096,1024]{2,1,0:T(8,128)(2,1)}, bf16[1,4096,1024]{2,1,0:T(8,128)(2,1)}) custom-call(bf16[768,4096]{1,0:T(8,128)(2,1)} %get-tuple-element.89.rows, bf16[768,1024]{1,0:T(8,128)(2,1)S(1)} %get-tuple-element.75.gate_g, bf16[768,1024]{1,0:T(8,128)(2,1)S(1)} %copy-done.1, ...), custom_call_target="tpu_custom_call", output_to_operand_aliasing={{0}: (3, {}), {1}: (4, {})} | custom-call | flops 6442450944 | bytes 6442450 | tf_op jit(solution)/shard_map/pallas_call | solution.py:40
  290.7 3.2 %collective-permute-done.51.refs_2_ = bf16[2,96,512]{2,1,0:T(8,128)(2,1)S(1)} collective-permute-done((bf16[2,96,512]{2,1,0:T(8,128)(2,1)S(1)}, bf16[2,96,512]{2,1,0:T(8,128)(2,1)S(1)}, u32[]{:S(2)}, u32[]{:S(2)}) %collective-permute-start.51) | collective-permute-done | bytes 196640 | tf_op jit(solution)/shard_map/ppermute | solution.py:367
  293.9 1.6 shard_map.132
  (137 shorter events, 26.2 us)
Async XLA Ops:
  2.1 10.5 %collective-permute-start.9 = (bf16[2,96,512]{2,1,0:T(8,128)(2,1)S(1)}, bf16[2,96,512]{2,1,0:T(8,128)(2,1)S(1)}, u32[]{:S(2)}, u32[]{:S(2)}) collective-permute-start(bf16[2,96,512]{2,1,0:T(8,128)(2,1)S(1)} %get-tuple-element.57), channel_id=1, source_target_pairs={{0,3},{1,0},{2,1},{3,2},{4,7},{5,4},{6,5},{7,6},{8,11},{9,8},{10,9... | collective-permute-start | bytes 589832 | tf_op jit(solution)/shard_map/ppermute | solution.py:367
  7.3 16.7 %collective-permute-start.8 = (bf16[2,96,512]{2,1,0:T(8,128)(2,1)S(1)}, bf16[2,96,512]{2,1,0:T(8,128)(2,1)S(1)}, u32[]{:S(2)}, u32[]{:S(2)}) collective-permute-start(bf16[2,96,512]{2,1,0:T(8,128)(2,1)S(1)} %get-tuple-element.56), channel_id=1, source_target_pairs={{0,2},{1,3},{2,0},{3,1},{4,6},{5,7},{6,4},{7,5},{8,10},{9,11},{10,... | collective-permute-start | bytes 589832 | tf_op jit(solution)/shard_map/ppermute | solution.py:367
  7.3 16.7 %collective-permute-start.7 = (bf16[2,96,512]{2,1,0:T(8,128)(2,1)S(1)}, bf16[2,96,512]{2,1,0:T(8,128)(2,1)S(1)}, u32[]{:S(2)}, u32[]{:S(2)}) collective-permute-start(bf16[2,96,512]{2,1,0:T(8,128)(2,1)S(1)} %get-tuple-element.55), channel_id=1, source_target_pairs={{0,1},{1,2},{2,3},{3,0},{4,5},{5,6},{6,7},{7,4},{8,9},{9,10},{10,1... | collective-permute-start | bytes 589832 | tf_op jit(solution)/shard_map/ppermute | solution.py:367
  24.0 8.1 %collective-permute-start.10 = (bf16[1,288,512]{2,1,0:T(8,128)(2,1)S(1)}, bf16[1,288,512]{2,1,0:T(8,128)(2,1)S(1)}, u32[]{:S(2)}, u32[]{:S(2)}) collective-permute-start(bf16[1,288,512]{2,1,0:T(8,128)(2,1)S(1)} %pad_maximum_fusion.2), channel_id=1, source_target_pairs={{0,8},{4,12},{8,0},{12,4},{16,24},{20,28},{24,16},{28,20},{1,9},{5... | collective-permute-start | bytes 884744 | tf_op jit(solution)/shard_map/ppermute | solution.py:364
  25.6 8.1 %collective-permute-start.12 = (bf16[1,288,512]{2,1,0:T(8,128)(2,1)S(1)}, bf16[1,288,512]{2,1,0:T(8,128)(2,1)S(1)}, u32[]{:S(2)}, u32[]{:S(2)}) collective-permute-start(bf16[1,288,512]{2,1,0:T(8,128)(2,1)S(1)} %pad_maximum_fusion.3), channel_id=1, source_target_pairs={{0,16},{4,20},{8,24},{12,28},{16,0},{20,4},{24,8},{28,12},{1,17},{... | collective-permute-start | bytes 884744 | tf_op jit(solution)/shard_map/ppermute | solution.py:364
  32.2 25.2 %collective-permute-start.11 = (bf16[2,288,512]{2,1,0:T(8,128)(2,1)S(1)}, bf16[2,288,512]{2,1,0:T(8,128)(2,1)S(1)}, u32[]{:S(2)}, u32[]{:S(2)}) collective-permute-start(bf16[2,288,512]{2,1,0:T(8,128)(2,1)S(1)} %pad_maximum_fusion.refs_4_), channel_id=1, source_target_pairs={{0,16},{4,20},{8,24},{12,28},{16,0},{20,4},{24,8},{28,12},{1,17},{... | collective-permute-start | bytes 1769480 | tf_op jit(solution)/shard_map/ppermute | solution.py:364
  33.8 24.4 %collective-permute-start.13 = (bf16[2,288,512]{2,1,0:T(8,128)(2,1)S(1)}, bf16[2,288,512]{2,1,0:T(8,128)(2,1)S(1)}, u32[]{:S(2)}, u32[]{:S(2)}) collective-permute-start(bf16[2,288,512]{2,1,0:T(8,128)(2,1)S(1)} %pad_maximum_fusion.1.refs_6_), channel_id=1, source_target_pairs={{0,8},{4,12},{8,0},{12,4},{16,24},{20,28},{24,16},{28,20},{1,9},{5... | collective-permute-start | bytes 1769480 | tf_op jit(solution)/shard_map/ppermute | solution.py:364
  35.4 13.8 %collective-permute-start.3 = (bf16[1,96,512]{2,1,0:T(8,128)(2,1)S(1)}, bf16[1,96,512]{2,1,0:T(8,128)(2,1)S(1)}, u32[]{:S(2)}, u32[]{:S(2)}) collective-permute-start(bf16[1,96,512]{2,1,0:T(8,128)(2,1)S(1)} %get-tuple-element.103), channel_id=1, source_target_pairs={{0,8},{4,12},{8,0},{12,4},{16,24},{20,28},{24,16},{28,20},{1,9},{5... | collective-permute-start | bytes 294920 | tf_op jit(solution)/shard_map/ppermute | solution.py:364
  36.0 14.5 %collective-permute-start.5 = (bf16[1,96,512]{2,1,0:T(8,128)(2,1)S(1)}, bf16[1,96,512]{2,1,0:T(8,128)(2,1)S(1)}, u32[]{:S(2)}, u32[]{:S(2)}) collective-permute-start(bf16[1,96,512]{2,1,0:T(8,128)(2,1)S(1)} %get-tuple-element.102), channel_id=1, source_target_pairs={{0,16},{4,20},{8,24},{12,28},{16,0},{20,4},{24,8},{28,12},{1,17},{... | collective-permute-start | bytes 294920 | tf_op jit(solution)/shard_map/ppermute | solution.py:364
  49.2 5.7 %collective-permute-start.4 = (bf16[2,96,512]{2,1,0:T(8,128)(2,1)S(1)}, bf16[2,96,512]{2,1,0:T(8,128)(2,1)S(1)}, u32[]{:S(2)}, u32[]{:S(2)}) collective-permute-start(bf16[2,96,512]{2,1,0:T(8,128)(2,1)S(1)} %pad_maximum_fusion.4.refs_0_), channel_id=1, source_target_pairs={{0,16},{4,20},{8,24},{12,28},{16,0},{20,4},{24,8},{28,12},{1,17},{... | collective-permute-start | bytes 589832 | tf_op jit(solution)/shard_map/ppermute | solution.py:364
  50.5 5.7 %collective-permute-start.6 = (bf16[2,96,512]{2,1,0:T(8,128)(2,1)S(1)}, bf16[2,96,512]{2,1,0:T(8,128)(2,1)S(1)}, u32[]{:S(2)}, u32[]{:S(2)}) collective-permute-start(bf16[2,96,512]{2,1,0:T(8,128)(2,1)S(1)} %pad_maximum_fusion.5.refs_2_), channel_id=1, source_target_pairs={{0,8},{4,12},{8,0},{12,4},{16,24},{20,28},{24,16},{28,20},{1,9},{5... | collective-permute-start | bytes 589832 | tf_op jit(solution)/shard_map/ppermute | solution.py:364
  51.3 4.9 %collective-permute-start.14 = (bf16[2,96,512]{2,1,0:T(8,128)(2,1)S(1)}, bf16[2,96,512]{2,1,0:T(8,128)(2,1)S(1)}, u32[]{:S(2)}, u32[]{:S(2)}) collective-permute-start(bf16[2,96,512]{2,1,0:T(8,128)(2,1)S(1)} %pad_maximum_fusion.4.refs_0_), channel_id=1, source_target_pairs={{0,4},{4,0},{8,12},{12,8},{16,20},{20,16},{24,28},{28,24},{1,5},{5... | collective-permute-start | bytes 589832 | tf_op jit(solution)/shard_map/ppermute | solution.py:364
  54.9 4.6 %collective-permute-start.16 = (bf16[2,96,512]{2,1,0:T(8,128)(2,1)S(1)}, bf16[2,96,512]{2,1,0:T(8,128)(2,1)S(1)}, u32[]{:S(2)}, u32[]{:S(2)}) collective-permute-start(bf16[2,96,512]{2,1,0:T(8,128)(2,1)S(1)} %pad_maximum_fusion.5.refs_2_), channel_id=1, source_target_pairs={{0,4},{4,0},{8,12},{12,8},{16,20},{20,16},{24,28},{28,24},{1,5},{5... | collective-permute-start | bytes 589832 | tf_op jit(solution)/shard_map/ppermute | solution.py:364
  56.2 8.3 %collective-permute-start.18 = (bf16[2,288,512]{2,1,0:T(8,128)(2,1)S(1)}, bf16[2,288,512]{2,1,0:T(8,128)(2,1)}, u32[]{:S(2)}, u32[]{:S(2)}) collective-permute-start(bf16[2,288,512]{2,1,0:T(8,128)(2,1)S(1)} %pad_maximum_fusion.refs_4_), channel_id=1, source_target_pairs={{0,4},{4,0},{8,12},{12,8},{16,20},{20,16},{24,28},{28,24},{1,5},{5... | collective-permute-start | bytes 1769480 | tf_op jit(solution)/shard_map/ppermute | solution.py:364
  56.9 7.6 %collective-permute-start.20 = (bf16[2,288,512]{2,1,0:T(8,128)(2,1)S(1)}, bf16[2,288,512]{2,1,0:T(8,128)(2,1)}, u32[]{:S(2)}, u32[]{:S(2)}) collective-permute-start(bf16[2,288,512]{2,1,0:T(8,128)(2,1)S(1)} %pad_maximum_fusion.1.refs_6_), channel_id=1, source_target_pairs={{0,4},{4,0},{8,12},{12,8},{16,20},{20,16},{24,28},{28,24},{1,5},{5... | collective-permute-start | bytes 1769480 | tf_op jit(solution)/shard_map/ppermute | solution.py:364
  57.4 7.1 %collective-permute-start.19 = (bf16[2,288,512]{2,1,0:T(8,128)(2,1)S(1)}, bf16[2,288,512]{2,1,0:T(8,128)(2,1)}, u32[]{:S(2)}, u32[]{:S(2)}) collective-permute-start(bf16[2,288,512]{2,1,0:T(8,128)(2,1)S(1)} %collective-permute-done.11.refs_5_), channel_id=1, source_target_pairs={{0,4},{4,0},{8,12},{12,8},{16,20},{20,16},{24,28},{28,24},{1,5},{5... | collective-permute-start | bytes 1769480 | tf_op jit(solution)/shard_map/ppermute | solution.py:364
  58.2 6.3 %collective-permute-start.21 = (bf16[2,288,512]{2,1,0:T(8,128)(2,1)S(1)}, bf16[2,288,512]{2,1,0:T(8,128)(2,1)}, u32[]{:S(2)}, u32[]{:S(2)}) collective-permute-start(bf16[2,288,512]{2,1,0:T(8,128)(2,1)S(1)} %collective-permute-done.13.refs_7_), channel_id=1, source_target_pairs={{0,4},{4,0},{8,12},{12,8},{16,20},{20,16},{24,28},{28,24},{1,5},{5... | collective-permute-start | bytes 1769480 | tf_op jit(solution)/shard_map/ppermute | solution.py:364
  60.2 1.4 collective-permute-start.15
  62.4 1.4 collective-permute-start.17
  64.5 1.1 copy-start.9
  88.3 18.5 %copy-start.12 = (bf16[2,128,512]{2,1,0:T(8,128)(2,1)S(1)}, bf16[2,128,512]{2,1,0:T(8,128)(2,1)}, u32[]{:S(2)}) copy-start(bf16[2,128,512]{2,1,0:T(8,128)(2,1)} %cots.1) | copy-start | bytes 786436
  88.3 18.5 %copy-start.22 = (s32[2,128,2]{1,2,0:T(2,128)S(1)}, s32[2,128,2]{1,2,0:T(2,128)}, u32[]{:S(2)}) copy-start(s32[2,128,2]{1,2,0:T(2,128)} %param.8) | copy-start | bytes 6148
  93.8 65.8 %collective-permute-start.22 = (bf16[4,768,512]{2,1,0:T(8,128)(2,1)S(1)}, bf16[4,768,512]{2,1,0:T(8,128)(2,1)S(1)}, u32[]{:S(2)}, u32[]{:S(2)}) collective-permute-start(bf16[4,768,512]{2,1,0:T(8,128)(2,1)S(1)} %shard_map.121), channel_id=1, source_target_pairs={{0,4},{4,0},{8,12},{12,8},{16,20},{20,16},{24,28},{28,24},{1,5},{5... | collective-permute-start | bytes 9437192 | tf_op jit(solution)/shard_map/ppermute | solution.py:364
  94.0 5.5 %collective-permute-start = (f32[8,128]{1,0:T(8,128)S(1)}, f32[8,128]{1,0:T(8,128)S(1)}, u32[]{:S(2)}, u32[]{:S(2)}) collective-permute-start(f32[8,128]{1,0:T(8,128)S(1)} %get-tuple-element.52), channel_id=1, source_target_pairs={{0,4},{4,0},{8,12},{12,8},{16,20},{20,16},{24,28},{28,24},{1,5},{5... | collective-permute-start | bytes 12296 | tf_op jit(solution)/shard_map/ppermute | solution.py:364
  99.6 3.6 %collective-permute-start.1 = (f32[8,128]{1,0:T(8,128)S(1)}, f32[8,128]{1,0:T(8,128)S(1)}, u32[]{:S(2)}, u32[]{:S(2)}) collective-permute-start(f32[8,128]{1,0:T(8,128)S(1)} %add.26), channel_id=1, source_target_pairs={{0,8},{4,12},{8,0},{12,4},{16,24},{20,28},{24,16},{28,20},{1,9},{5... | collective-permute-start | bytes 12296 | tf_op jit(solution)/shard_map/ppermute | solution.py:364
  103.2 3.6 %collective-permute-start.2 = (f32[8,128]{1,0:T(8,128)S(1)}, f32[8,128]{1,0:T(8,128)S(1)}, u32[]{:S(2)}, u32[]{:S(2)}) collective-permute-start(f32[8,128]{1,0:T(8,128)S(1)} %add.27), channel_id=1, source_target_pairs={{0,16},{4,20},{8,24},{12,28},{16,0},{20,4},{24,8},{28,12},{1,17},{... | collective-permute-start | bytes 12296 | tf_op jit(solution)/shard_map/ppermute | solution.py:364
  107.2 9.7 %collective-permute-start.29 = (bf16[2,96,512]{2,1,0:T(8,128)(2,1)S(1)}, bf16[2,96,512]{2,1,0:T(8,128)(2,1)S(1)}, u32[]{:S(2)}, u32[]{:S(2)}) collective-permute-start(bf16[2,96,512]{2,1,0:T(8,128)(2,1)S(1)} %get-tuple-element.68), channel_id=1, source_target_pairs={{0,1},{1,2},{2,3},{3,0},{4,5},{5,6},{6,7},{7,4},{8,9},{9,10},{10,1... | collective-permute-start | bytes 589832 | tf_op jit(solution)/shard_map/ppermute | solution.py:367
  108.4 13.8 %collective-permute-start.30 = (bf16[2,96,512]{2,1,0:T(8,128)(2,1)S(1)}, bf16[2,96,512]{2,1,0:T(8,128)(2,1)S(1)}, u32[]{:S(2)}, u32[]{:S(2)}) collective-permute-start(bf16[2,96,512]{2,1,0:T(8,128)(2,1)S(1)} %get-tuple-element.69), channel_id=1, source_target_pairs={{0,2},{1,3},{2,0},{3,1},{4,6},{5,7},{6,4},{7,5},{8,10},{9,11},{10,... | collective-permute-start | bytes 589832 | tf_op jit(solution)/shard_map/ppermute | solution.py:367
  110.4 11.9 %collective-permute-start.31 = (bf16[2,96,512]{2,1,0:T(8,128)(2,1)S(1)}, bf16[2,96,512]{2,1,0:T(8,128)(2,1)S(1)}, u32[]{:S(2)}, u32[]{:S(2)}) collective-permute-start(bf16[2,96,512]{2,1,0:T(8,128)(2,1)S(1)} %get-tuple-element.70), channel_id=1, source_target_pairs={{0,3},{1,0},{2,1},{3,2},{4,7},{5,4},{6,5},{7,6},{8,11},{9,8},{10,9... | collective-permute-start | bytes 589832 | tf_op jit(solution)/shard_map/ppermute | solution.py:367
  122.3 20.5 %collective-permute-start.32 = (bf16[2,384,512]{2,1,0:T(8,128)(2,1)S(1)}, bf16[2,384,512]{2,1,0:T(8,128)(2,1)S(1)}, u32[]{:S(2)}, u32[]{:S(2)}) collective-permute-start(bf16[2,384,512]{2,1,0:T(8,128)(2,1)S(1)} %constant_dynamic-update-slice_fusion.refs_0_), channel_id=1, source_target_pairs={{0,8},{4,12},{8,0},{12,4},{16,24},{20,28},{24,16},{28,20},{1,9},{5... | collective-permute-start | bytes 2359304 | tf_op jit(solution)/shard_map/ppermute | solution.py:364
  123.1 35.9 %collective-permute-start.33 = (bf16[2,384,512]{2,1,0:T(8,128)(2,1)S(1)}, bf16[2,384,512]{2,1,0:T(8,128)(2,1)S(1)}, u32[]{:S(2)}, u32[]{:S(2)}) collective-permute-start(bf16[2,384,512]{2,1,0:T(8,128)(2,1)S(1)} %constant_dynamic-update-slice_fusion.refs_0_), channel_id=1, source_target_pairs={{0,16},{4,20},{8,24},{12,28},{16,0},{20,4},{24,8},{28,12},{1,17},{... | collective-permute-start | bytes 2359304 | tf_op jit(solution)/shard_map/ppermute | solution.py:364
  124.7 34.4 %collective-permute-start.34 = (bf16[2,384,512]{2,1,0:T(8,128)(2,1)S(1)}, bf16[2,384,512]{2,1,0:T(8,128)(2,1)S(1)}, u32[]{:S(2)}, u32[]{:S(2)}) collective-permute-start(bf16[2,384,512]{2,1,0:T(8,128)(2,1)S(1)} %constant_dynamic-update-slice_fusion.refs_0_), channel_id=1, source_target_pairs={{0,24},{4,28},{8,16},{12,20},{16,8},{20,12},{24,0},{28,4},{1,25},{... | collective-permute-start | bytes 2359304 | tf_op jit(solution)/shard_map/ppermute | solution.py:364
  125.8 42.2 %collective-permute-start.35 = (bf16[2,384,512]{2,1,0:T(8,128)(2,1)S(1)}, bf16[2,384,512]{2,1,0:T(8,128)(2,1)S(1)}, u32[]{:S(2)}, u32[]{:S(2)}) collective-permute-start(bf16[2,384,512]{2,1,0:T(8,128)(2,1)S(1)} %constant_dynamic-update-slice_fusion.refs_0_), channel_id=1, source_target_pairs={{0,4},{4,0},{8,12},{12,8},{16,20},{20,16},{24,28},{28,24},{1,5},{5... | collective-permute-start | bytes 2359304 | tf_op jit(solution)/shard_map/ppermute | solution.py:364
  142.8 25.3 %collective-permute-start.36 = (bf16[2,384,512]{2,1,0:T(8,128)(2,1)S(1)}, bf16[2,384,512]{2,1,0:T(8,128)(2,1)S(1)}, u32[]{:S(2)}, u32[]{:S(2)}) collective-permute-start(bf16[2,384,512]{2,1,0:T(8,128)(2,1)S(1)} %collective-permute-done.32.refs_1_), channel_id=1, source_target_pairs={{0,4},{4,0},{8,12},{12,8},{16,20},{20,16},{24,28},{28,24},{1,5},{5... | collective-permute-start | bytes 2359304 | tf_op jit(solution)/shard_map/ppermute | solution.py:364
  159.1 9.0 %collective-permute-start.37 = (bf16[2,384,512]{2,1,0:T(8,128)(2,1)S(1)}, bf16[2,384,512]{2,1,0:T(8,128)(2,1)S(1)}, u32[]{:S(2)}, u32[]{:S(2)}) collective-permute-start(bf16[2,384,512]{2,1,0:T(8,128)(2,1)S(1)} %collective-permute-done.33.refs_2_), channel_id=1, source_target_pairs={{0,4},{4,0},{8,12},{12,8},{16,20},{20,16},{24,28},{28,24},{1,5},{5... | collective-permute-start | bytes 2359304 | tf_op jit(solution)/shard_map/ppermute | solution.py:364
  159.1 9.0 %collective-permute-start.38 = (bf16[2,384,512]{2,1,0:T(8,128)(2,1)S(1)}, bf16[2,384,512]{2,1,0:T(8,128)(2,1)S(1)}, u32[]{:S(2)}, u32[]{:S(2)}) collective-permute-start(bf16[2,384,512]{2,1,0:T(8,128)(2,1)S(1)} %collective-permute-done.34.refs_3_), channel_id=1, source_target_pairs={{0,4},{4,0},{8,12},{12,8},{16,20},{20,16},{24,28},{28,24},{1,5},{5... | collective-permute-start | bytes 2359304 | tf_op jit(solution)/shard_map/ppermute | solution.py:364
  168.0 11.6 %copy-start.2 = (bf16[768,512]{1,0:T(8,128)(2,1)}, bf16[768,512]{1,0:T(8,128)(2,1)S(1)}, u32[]{:S(2)}) copy-start(bf16[768,512]{1,0:T(8,128)(2,1)S(1)} %get-tuple-element.59.refs_0_.refs_12_) | copy-start | bytes 2359300
  179.6 10.5 %copy-start = (bf16[768,1024]{1,0:T(8,128)(2,1)}, bf16[768,1024]{1,0:T(8,128)(2,1)S(1)}, u32[]{:S(2)}) copy-start(bf16[768,1024]{1,0:T(8,128)(2,1)S(1)} %get-tuple-element.76.up_g) | copy-start | bytes 4718596
  179.6 28.7 %copy-start.13 = (bf16[2,128,512]{2,1,0:T(8,128)(2,1)S(1)}, bf16[2,128,512]{2,1,0:T(8,128)(2,1)}, u32[]{:S(2)}) copy-start(bf16[2,128,512]{2,1,0:T(8,128)(2,1)} %tokens.3) | copy-start | bytes 786436
  190.2 26.0 %collective-permute-start.45 = (bf16[4,768,512]{2,1,0:T(8,128)(2,1)}, bf16[4,768,512]{2,1,0:T(8,128)(2,1)}, u32[]{:S(2)}, u32[]{:S(2)}) collective-permute-start(bf16[4,768,512]{2,1,0:T(8,128)(2,1)} %shard_map.127._), channel_id=1, source_target_pairs={{0,4},{4,0},{8,12},{12,8},{16,20},{20,16},{24,28},{28,24},{1,5},{5... | collective-permute-start | bytes 9437192 | tf_op jit(solution)/shard_map/ppermute | solution.py:364
  190.3 7.2 %collective-permute-start.41 = (f32[8,96]{1,0:T(8,128)S(1)}, f32[8,96]{1,0:T(8,128)S(1)}, u32[]{:S(2)}, u32[]{:S(2)}) collective-permute-start(f32[8,96]{1,0:T(8,128)S(1)} %get-tuple-element.107), channel_id=1, source_target_pairs={{0,1},{1,2},{2,3},{3,0},{4,5},{5,6},{6,7},{7,4},{8,9},{9,10},{10,1... | collective-permute-start | bytes 9224 | tf_op jit(solution)/shard_map/ppermute | solution.py:367
  195.1 4.5 %collective-permute-start.40 = (f32[8,96]{1,0:T(8,128)S(1)}, f32[8,96]{1,0:T(8,128)S(1)}, u32[]{:S(2)}, u32[]{:S(2)}) collective-permute-start(f32[8,96]{1,0:T(8,128)S(1)} %get-tuple-element.106), channel_id=1, source_target_pairs={{0,2},{1,3},{2,0},{3,1},{4,6},{5,7},{6,4},{7,5},{8,10},{9,11},{10,... | collective-permute-start | bytes 9224 | tf_op jit(solution)/shard_map/ppermute | solution.py:367
  195.7 3.8 %collective-permute-start.39 = (f32[8,96]{1,0:T(8,128)S(1)}, f32[8,96]{1,0:T(8,128)S(1)}, u32[]{:S(2)}, u32[]{:S(2)}) collective-permute-start(f32[8,96]{1,0:T(8,128)S(1)} %get-tuple-element.105), channel_id=1, source_target_pairs={{0,3},{1,0},{2,1},{3,2},{4,7},{5,4},{6,5},{7,6},{8,11},{9,8},{10,9... | collective-permute-start | bytes 9224 | tf_op jit(solution)/shard_map/ppermute | solution.py:367
  199.6 1.2 collective-permute-start.42
  200.8 3.7 %collective-permute-start.43 = (f32[4,8,96]{2,1,0:T(8,128)S(1)}, f32[4,8,96]{2,1,0:T(8,128)S(1)}, u32[]{:S(2)}, u32[]{:S(2)}) collective-permute-start(f32[4,8,96]{2,1,0:T(8,128)S(1)} %fusion.5), channel_id=1, source_target_pairs={{0,8},{4,12},{8,0},{12,4},{16,24},{20,28},{24,16},{28,20},{1,9},{5... | collective-permute-start | bytes 36872 | tf_op jit(solution)/shard_map/ppermute | solution.py:364
  202.1 25.9 %collective-permute-start.23 = (bf16[768,512]{1,0:T(8,128)(2,1)}, bf16[768,512]{1,0:T(8,128)(2,1)S(1)}, u32[]{:S(2)}, u32[]{:S(2)}) collective-permute-start(bf16[768,512]{1,0:T(8,128)(2,1)} %copy-done.7), channel_id=1, source_target_pairs={{0,8},{4,12},{8,0},{12,4},{16,24},{20,28},{24,16},{28,20},{1,9},{5... | collective-permute-start | bytes 2359304 | tf_op jit(solution)/shard_map/ppermute | solution.py:364
  204.6 3.7 %collective-permute-start.44 = (f32[4,8,96]{2,1,0:T(8,128)S(1)}, f32[4,8,96]{2,1,0:T(8,128)S(1)}, u32[]{:S(2)}, u32[]{:S(2)}) collective-permute-start(f32[4,8,96]{2,1,0:T(8,128)S(1)} %fusion.10), channel_id=1, source_target_pairs={{0,16},{4,20},{8,24},{12,28},{16,0},{20,4},{24,8},{28,12},{1,17},{... | collective-permute-start | bytes 36872 | tf_op jit(solution)/shard_map/ppermute | solution.py:364
  209.4 3.8 %collective-permute-start.53 = (f32[8,512]{1,0:T(8,128)S(1)}, f32[8,512]{1,0:T(8,128)S(1)}, u32[]{:S(2)}, u32[]{:S(2)}) collective-permute-start(f32[8,512]{1,0:T(8,128)S(1)} %get-tuple-element.95), channel_id=1, source_target_pairs={{0,1},{1,0},{2,3},{3,2},{4,5},{5,4},{6,7},{7,6},{8,9},{9,8},{10,11... | collective-permute-start | bytes 49160 | tf_op jit(solution)/shard_map/ppermute | solution.py:588
  209.9 37.5 %collective-permute-start.24 = (bf16[768,512]{1,0:T(8,128)(2,1)}, bf16[768,512]{1,0:T(8,128)(2,1)S(1)}, u32[]{:S(2)}, u32[]{:S(2)}) collective-permute-start(bf16[768,512]{1,0:T(8,128)(2,1)} %copy-done.6), channel_id=1, source_target_pairs={{0,16},{4,20},{8,24},{12,28},{16,0},{20,4},{24,8},{28,12},{1,17},{... | collective-permute-start | bytes 2359304 | tf_op jit(solution)/shard_map/ppermute | solution.py:364
  211.6 35.8 %collective-permute-start.25 = (bf16[768,512]{1,0:T(8,128)(2,1)}, bf16[768,512]{1,0:T(8,128)(2,1)S(1)}, u32[]{:S(2)}, u32[]{:S(2)}) collective-permute-start(bf16[768,512]{1,0:T(8,128)(2,1)} %copy-done.5), channel_id=1, source_target_pairs={{0,24},{4,28},{8,16},{12,20},{16,8},{20,12},{24,0},{28,4},{1,25},{... | collective-permute-start | bytes 2359304 | tf_op jit(solution)/shard_map/ppermute | solution.py:364
  213.1 38.1 %collective-permute-start.54 = (f32[8,512]{1,0:T(8,128)S(1)}, f32[8,512]{1,0:T(8,128)S(1)}, u32[]{:S(2)}, u32[]{:S(2)}) collective-permute-start(f32[8,512]{1,0:T(8,128)S(1)} %add.32), channel_id=1, source_target_pairs={{0,2},{1,3},{2,0},{3,1},{4,6},{5,7},{6,4},{7,5},{8,10},{9,11},{10,... | collective-permute-start | bytes 49160 | tf_op jit(solution)/shard_map/ppermute | solution.py:588
  216.1 1.4 copy-start.1
  227.2 37.3 %collective-permute-start.46 = (bf16[2,384,512]{2,1,0:T(8,128)(2,1)S(1)}, bf16[2,384,512]{2,1,0:T(8,128)(2,1)S(1)}, u32[]{:S(2)}, u32[]{:S(2)}) collective-permute-start(bf16[2,384,512]{2,1,0:T(8,128)(2,1)S(1)} %get-tuple-element.78), channel_id=1, source_target_pairs={{0,16},{4,20},{8,24},{12,28},{16,0},{20,4},{24,8},{28,12},{1,17},{... | collective-permute-start | bytes 2359304 | tf_op jit(solution)/shard_map/ppermute | solution.py:364
  228.0 37.8 %collective-permute-start.48 = (bf16[2,384,512]{2,1,0:T(8,128)(2,1)S(1)}, bf16[2,384,512]{2,1,0:T(8,128)(2,1)S(1)}, u32[]{:S(2)}, u32[]{:S(2)}) collective-permute-start(bf16[2,384,512]{2,1,0:T(8,128)(2,1)S(1)} %get-tuple-element.82), channel_id=1, source_target_pairs={{0,8},{4,12},{8,0},{12,4},{16,24},{20,28},{24,16},{28,20},{1,9},{5... | collective-permute-start | bytes 2359304 | tf_op jit(solution)/shard_map/ppermute | solution.py:364
  229.6 17.8 %copy-start.3 = (bf16[768,512]{1,0:T(8,128)(2,1)S(1)}, bf16[768,512]{1,0:T(8,128)(2,1)}, u32[]{:S(2)}) copy-start(bf16[768,512]{1,0:T(8,128)(2,1)} %copy-done.2) | copy-start | bytes 2359300
  247.8 8.8 %collective-permute-start.26 = (bf16[2,96,512]{2,1,0:T(8,128)(2,1)S(1)}, bf16[2,96,512]{2,1,0:T(8,128)(2,1)S(1)}, u32[]{:S(2)}, u32[]{:S(2)}) collective-permute-start(bf16[2,96,512]{2,1,0:T(8,128)(2,1)S(1)} %get-tuple-element.64), channel_id=1, source_target_pairs={{0,3},{1,0},{2,1},{3,2},{4,7},{5,4},{6,5},{7,6},{8,11},{9,8},{10,9... | collective-permute-start | bytes 589832 | tf_op jit(solution)/shard_map/ppermute | solution.py:367
  250.7 12.3 %collective-permute-start.27 = (bf16[2,96,512]{2,1,0:T(8,128)(2,1)S(1)}, bf16[2,96,512]{2,1,0:T(8,128)(2,1)S(1)}, u32[]{:S(2)}, u32[]{:S(2)}) collective-permute-start(bf16[2,96,512]{2,1,0:T(8,128)(2,1)S(1)} %get-tuple-element.65), channel_id=1, source_target_pairs={{0,2},{1,3},{2,0},{3,1},{4,6},{5,7},{6,4},{7,5},{8,10},{9,11},{10,... | collective-permute-start | bytes 589832 | tf_op jit(solution)/shard_map/ppermute | solution.py:367
  251.2 11.8 %collective-permute-start.28 = (bf16[2,96,512]{2,1,0:T(8,128)(2,1)S(1)}, bf16[2,96,512]{2,1,0:T(8,128)(2,1)S(1)}, u32[]{:S(2)}, u32[]{:S(2)}) collective-permute-start(bf16[2,96,512]{2,1,0:T(8,128)(2,1)S(1)} %get-tuple-element.66), channel_id=1, source_target_pairs={{0,1},{1,2},{2,3},{3,0},{4,5},{5,6},{6,7},{7,4},{8,9},{9,10},{10,1... | collective-permute-start | bytes 589832 | tf_op jit(solution)/shard_map/ppermute | solution.py:367
  264.7 11.9 %collective-permute-start.47 = (bf16[1,384,512]{2,1,0:T(8,128)(2,1)S(1)}, bf16[1,384,512]{2,1,0:T(8,128)(2,1)S(1)}, u32[]{:S(2)}, u32[]{:S(2)}) collective-permute-start(bf16[1,384,512]{2,1,0:T(8,128)(2,1)S(1)} %get-tuple-element.80), channel_id=1, source_target_pairs={{0,8},{4,12},{8,0},{12,4},{16,24},{20,28},{24,16},{28,20},{1,9},{5... | collective-permute-start | bytes 1179656 | tf_op jit(solution)/shard_map/ppermute | solution.py:364
  265.9 10.6 %collective-permute-start.49 = (bf16[1,384,512]{2,1,0:T(8,128)(2,1)S(1)}, bf16[1,384,512]{2,1,0:T(8,128)(2,1)S(1)}, u32[]{:S(2)}, u32[]{:S(2)}) collective-permute-start(bf16[1,384,512]{2,1,0:T(8,128)(2,1)S(1)} %get-tuple-element.84), channel_id=1, source_target_pairs={{0,16},{4,20},{8,24},{12,28},{16,0},{20,4},{24,8},{28,12},{1,17},{... | collective-permute-start | bytes 1179656 | tf_op jit(solution)/shard_map/ppermute | solution.py:364
  276.7 14.0 %collective-permute-start.50 = (bf16[2,96,512]{2,1,0:T(8,128)(2,1)S(1)}, bf16[2,96,512]{2,1,0:T(8,128)(2,1)S(1)}, u32[]{:S(2)}, u32[]{:S(2)}) collective-permute-start(bf16[2,96,512]{2,1,0:T(8,128)(2,1)S(1)} %get-tuple-element.86), channel_id=1, source_target_pairs={{0,3},{1,0},{2,1},{3,2},{4,7},{5,4},{6,5},{7,6},{8,11},{9,8},{10,9... | collective-permute-start | bytes 589832 | tf_op jit(solution)/shard_map/ppermute | solution.py:367
  278.0 15.9 %collective-permute-start.51 = (bf16[2,96,512]{2,1,0:T(8,128)(2,1)S(1)}, bf16[2,96,512]{2,1,0:T(8,128)(2,1)S(1)}, u32[]{:S(2)}, u32[]{:S(2)}) collective-permute-start(bf16[2,96,512]{2,1,0:T(8,128)(2,1)S(1)} %get-tuple-element.87), channel_id=1, source_target_pairs={{0,2},{1,3},{2,0},{3,1},{4,6},{5,7},{6,4},{7,5},{8,10},{9,11},{10,... | collective-permute-start | bytes 589832 | tf_op jit(solution)/shard_map/ppermute | solution.py:367
  279.3 14.6 %collective-permute-start.52 = (bf16[2,96,512]{2,1,0:T(8,128)(2,1)S(1)}, bf16[2,96,512]{2,1,0:T(8,128)(2,1)S(1)}, u32[]{:S(2)}, u32[]{:S(2)}) collective-permute-start(bf16[2,96,512]{2,1,0:T(8,128)(2,1)S(1)} %get-tuple-element.88), channel_id=1, source_target_pairs={{0,1},{1,2},{2,3},{3,0},{4,5},{5,6},{6,7},{7,4},{8,9},{9,10},{10,1... | collective-permute-start | bytes 589832 | tf_op jit(solution)/shard_map/ppermute | solution.py:367
  281.2 12.7 %copy-start.4 = (bf16[512,4]{0,1:T(4,128)(2,1)S(1)}, bf16[512,4]{0,1:T(4,128)(2,1)}, u32[]{:S(2)}) copy-start(bf16[512,4]{0,1:T(4,128)(2,1)} %param.9) | copy-start | bytes 12292
  (14 other events, 11.8 us)
